TPU v7x, 32 devices: a whole 2x2x4 slice. The times are simulated.
32 devices in a mesh: expert: 4 (over z), tensor: 8 (over y, x, core).
Axes of the slice: x: 2, y: 2, z: 4, core: 2. Of those that a mesh axis runs over, the one named last changes fastest.
Arguments:
- stashed: bfloat16 [384, 4096], P('expert', 'tensor'), may hold values from -6 to 6
- expert_ids: int32 [384, 2], P('expert'), may hold values from 0 to 3, all different within a row; in each aligned block of 96 rows (0 to 95, 96 to 191, ...) at most 64 rows name the same one
- combine_weight: float32 [384, 2], P('expert'), may hold values from 0.2 to 1
- w_gate: bfloat16 [4, 7168, 4096], P('expert', 'tensor'), may hold values from -0.09375 to 0.09375
- w_up: bfloat16 [4, 7168, 4096], P('expert', 'tensor'), may hold values from -0.09375 to 0.09375
- w_down: bfloat16 [4, 7168, 4096], P('expert', 'tensor'), may hold values from -0.09375 to 0.09375
Outputs:
- mixed_out: bfloat16 [384, 4096], P('expert', 'tensor')
Inputs may be any that keep to these rules, and one draw needn't show every extreme that they name: `expert_ids`: each row names two different experts. Among the 96 rows of one group (aligned blocks) no expert is named more than 64 times, and in some group some expert is named exactly 64 times.
All inputs are finite; a program needn't handle non-finite values.
Results may differ from a plain program's by a relative error of at most 0.0049.
Values may be sent and summed in bfloat16 or wider, within the bound.
No kernel may reach another device: no remote copies, remote signals or barrier semaphores. Data moves between devices by JAX's collectives and lax.ppermute only.
A program may use at most 64 MiB of HBM per device.

v0:
```python
import jax
import jax.numpy as jnp
from jax import lax
from jax.sharding import PartitionSpec as P


def slot_targets(expert_ids, experts, capacity):
    flat_ids = expert_ids.reshape(-1)
    one_hot = (flat_ids[:, None] == jnp.arange(experts, dtype=jnp.int32)[None, :]).astype(jnp.int32)
    before = jnp.cumsum(one_hot, axis=0) - one_hot
    slot_index = jnp.sum(before * one_hot, axis=1)
    return (flat_ids * capacity + slot_index).reshape(expert_ids.shape)


def contract_last(left, right):
    return lax.dot_general(
        left, right, (((1,), (1,)), ((), ())), preferred_element_type=jnp.float32
    )


def shards(stashed, expert_ids, combine_weight, w_gate, w_up, w_down):
    tok_count = stashed.shape[0]
    feat_width = stashed.shape[1]
    experts = lax.axis_size("expert")
    capacity = min(tok_count, 8 * tok_count // (3 * experts))
    targets = slot_targets(expert_ids, experts, capacity)
    columns = jnp.arange(experts * capacity, dtype=jnp.int32)
    pair_match = (targets[:, :, None] == columns[None, None, :]).astype(jnp.float32)
    selector = jnp.sum(pair_match, axis=1).T.astype(jnp.bfloat16)
    mixing = jnp.sum(pair_match * combine_weight[:, :, None], axis=1)
    gate_w = w_gate[0]
    up_w = w_up[0]
    down_w = w_down[0]
    gathered = lax.all_gather(stashed, "tensor", axis=1, tiled=True)
    outgoing = jnp.dot(selector, gathered, preferred_element_type=jnp.float32).astype(jnp.bfloat16)
    outgoing = outgoing.reshape(experts, capacity, gathered.shape[1])
    received = lax.all_to_all(outgoing, "expert", split_axis=0, concat_axis=0, tiled=True)
    sources, item_count, full_width = received.shape
    rows_in = received.reshape(sources * item_count, full_width)
    gate_acts = contract_last(rows_in, gate_w)
    up_acts = contract_last(rows_in, up_w)
    hidden = (jax.nn.silu(gate_acts) * up_acts).astype(jnp.bfloat16)
    result = jnp.dot(hidden, down_w, preferred_element_type=jnp.float32)
    partial_value = result.reshape(sources, item_count, result.shape[1])
    partial_value = partial_value.reshape(-1, partial_value.shape[2])
    own_share = lax.psum_scatter(partial_value, "tensor", scatter_dimension=1, tiled=True)
    returned_rows = lax.all_to_all(
        own_share.reshape(experts, capacity, feat_width),
        "expert",
        split_axis=0,
        concat_axis=0,
        tiled=True,
    )
    combined = jnp.dot(
        mixing,
        returned_rows.reshape(experts * capacity, feat_width),
        precision=lax.Precision.HIGHEST,
        preferred_element_type=jnp.float32,
    )
    return combined.astype(jnp.bfloat16)


def solution(mesh):
    return jax.shard_map(
        shards,
        mesh=mesh,
        in_specs=(
            P("expert", "tensor"),
            P("expert", None),
            P("expert", None),
            P("expert", "tensor", None),
            P("expert", "tensor", None),
            P("expert", "tensor", None),
        ),
        out_specs=P("expert", "tensor"),
        check_vma=False,
    )
```

profile of v0, /device:TPU:0, one launch (start us, length us, event | category | flops | bytes accessed | tf_op | source)
XLA Modules:
  0.0 167.9 jit_solution(18047453095320567481)
XLA Ops:
  6.5 0.0 reduce-scatter.2.cloned.1.call-start
  6.5 0.8 copy.23
  7.3 0.1 eq.35
  7.5 1.2 reduce-window.6
  8.7 0.1 slice.12
  8.8 0.1 copy.24
  8.9 0.1 copy.25
  9.0 0.1 add_bitcast_fusion
  9.1 0.1 reduce_sum.30
  9.3 0.1 copy.26
  9.3 0.0 copy-start
  9.3 0.9 multiply_add_fusion
  10.2 12.5 %all_gather.3 = bf16[96,4096]{1,0:T(8,128)(2,1)S(1)} all-gather(bf16[96,512]{1,0:T(8,128)(2,1)} %param.6), channel_id=1, replica_groups=mesh['expert'=4,'tensor'=8] {'tensor'}, dimensions={1}, use_global_device_ids=true | all-gather | bytes 884736 | tf_op jit(solution)/shard_map/all_gather | solution.py:34
  22.7 0.8 convert_reduce_fusion
  23.5 0.7 convolution_convert_fusion
  24.2 53.4 %all_to_all.10 = bf16[4,64,4096]{2,1,0:T(8,128)(2,1)S(1)} all-to-all(bf16[4,64,4096]{2,1,0:T(8,128)(2,1)S(1)} %bitcast.34), channel_id=1, replica_groups=mesh['expert'=4,'tensor'=8] {'expert'}, dimensions={0} | all-to-all | bytes 4194304 | tf_op jit(solution)/shard_map/all_to_all | solution.py:37
  77.6 0.0 copy-done
  77.6 2.4 %fusion.4 = f32[256,896]{1,0:T(8,128)S(1)} fusion(bf16[256,4096]{1,0:T(8,128)(2,1)S(1)} %bitcast.35, bf16[1,896,4096]{2,1,0:T(8,128)(2,1)S(1)} %copy-done), kind=kOutput, calls=%fused_computation.4 | convolution fusion | flops 1879048192 | bytes 10354688 | tf_op jit(solution)/shard_map/dot_general | solution.py:16
  80.0 11.7 %fusion = f32[256,4096]{1,0:T(8,128)} fusion(bf16[1,896,4096]{2,1,0:T(8,128)(2,1)} %param.11, bf16[256,4096]{1,0:T(8,128)(2,1)S(1)} %bitcast.36, bf16[1,896,4096]{2,1,0:T(8,128)(2,1)} %param.10, f32[256,896]{1,0:T(8,128)S(1)} %fusion.4), kind=kOutput, calls=%fused_computation | convolution fusion | flops 3759472640 | bytes 21889024 | tf_op jit(solution)/shard_map/dot_general | solution.py:43
  91.7 0.0 reduce-scatter.2.cloned.1.call-update
  91.7 49.4 %reduce-scatter.2.cloned.1.call-done = f32[256,512]{1,0:T(8,128)} async-done(((f32[256,4096]{1,0:T(8,128)}), f32[256,512]{1,0:T(8,128)}) %reduce-scatter.2.cloned.1.call-update) | async-done | bytes 524304 | tf_op jit(solution)/shard_map/reduce_scatter | solution.py:46
  141.1 18.9 %all_to_all.11 = f32[4,64,512]{2,1,0:T(8,128)S(1)} all-to-all(f32[4,64,512]{2,1,0:T(8,128)} %bitcast.38), channel_id=1, replica_groups=mesh['expert'=4,'tensor'=8] {'expert'}, dimensions={0} | all-to-all | bytes 1048576 | tf_op jit(solution)/shard_map/all_to_all | solution.py:47
  160.0 1.1 convolution_convert_fusion.1
  (7 shorter events, 0.1 us)
Async XLA Ops:
  6.5 134.6 %reduce-scatter.2.cloned.1.call-start = ((), (), s32[]{:S(2)}) async-start(), calls=%async_computation.3 | async-start | bytes 4718592 | tf_op jit(solution)/shard_map/reduce_scatter | solution.py:46
  9.3 68.3 %copy-start = (bf16[1,896,4096]{2,1,0:T(8,128)(2,1)S(1)}, bf16[1,896,4096]{2,1,0:T(8,128)(2,1)}, u32[]{:S(2)}) copy-start(bf16[1,896,4096]{2,1,0:T(8,128)(2,1)} %param.9) | copy-start | bytes 22020100
Sparse Core Ops, SparseCore 0:
  91.8 49.2 reduce-scatter.1
where the time goes:
time: 168 us
  blocking collectives  84.8 us (50%)
  waiting for transfers between devices  49.4 us (29%)
  matrix products  15.9 us (9%)
  between operations  13.4 us (8%)
  other arithmetic  3.03 us (2%)
    all_to_all x1, blocking collectives, shards(): lax.all_to_all(outgoing, 'expert', split_axis=0, concat_axis=0, tiled=True)  53.4 us
    reduce_scatter x1, waiting for transfers between devices, shards(): lax.psum_scatter(partial_value, 'tensor', scatter_dimension=1, tiled=True)  49.4 us
    all_to_all x1, blocking collectives, shards(): lax.all_to_all(own_share.reshape(experts, capacity, feat_width), 'expert'...  18.9 us
    all_gather x1, blocking collectives, shards(): gathered = lax.all_gather(stashed, 'tensor', axis=1, tiled=True)  12.5 us
    dot_general x1, matrix products, shards(): result = jnp.dot(hidden, down_w, preferred_element_type=jnp.float32)  11.7 us
  transfers between devices with their start and end apart: 1, of which 1 were waited for; matrix products, arithmetic and copies ran while one was open for 0% of the time, Pallas kernels for 0%

commit v1 on v0

v1 whole, which is shorter than its diff:
```python
import functools

import jax
import jax.numpy as jnp
from jax import lax
from jax.experimental import pallas as pl
from jax.experimental.pallas import tpu as pltpu
from jax.sharding import PartitionSpec as P

VM = pltpu.VMEM
MIB = 1 << 20


def whole(count):
    return [pl.BlockSpec(memory_space=VM)] * count


def params(mib):
    return pltpu.CompilerParams(vmem_limit_bytes=mib * MIB)


def slot_targets(expert_ids, experts, capacity):
    flat_ids = expert_ids.reshape(-1)
    one_hot = (flat_ids[:, None] == jnp.arange(experts, dtype=jnp.int32)[None, :]).astype(jnp.int32)
    before = jnp.cumsum(one_hot, axis=0) - one_hot
    slot_index = jnp.sum(before * one_hot, axis=1)
    return (flat_ids * capacity + slot_index).reshape(expert_ids.shape)


def contract_last(left, right):
    return lax.dot_general(
        left, right, (((1,), (1,)), ((), ())), preferred_element_type=jnp.float32
    )


def shards_plain(stashed, expert_ids, combine_weight, w_gate, w_up, w_down):
    tok_count = stashed.shape[0]
    feat_width = stashed.shape[1]
    experts = lax.axis_size("expert")
    capacity = slots_of(tok_count, experts)
    targets = slot_targets(expert_ids, experts, capacity)
    columns = jnp.arange(experts * capacity, dtype=jnp.int32)
    pair_match = (targets[:, :, None] == columns[None, None, :]).astype(jnp.float32)
    selector = jnp.sum(pair_match, axis=1).T.astype(jnp.bfloat16)
    mixing = jnp.sum(pair_match * combine_weight[:, :, None], axis=1)
    own = jnp.dot(selector, stashed, preferred_element_type=jnp.float32).astype(jnp.bfloat16)
    own = own.reshape(experts, capacity, feat_width)
    received = lax.all_to_all(own, "expert", split_axis=0, concat_axis=0, tiled=True)
    rows_in = lax.all_gather(
        received.reshape(experts * capacity, feat_width), "tensor", axis=1, tiled=True
    )
    gate_acts = contract_last(rows_in, w_gate[0])
    up_acts = contract_last(rows_in, w_up[0])
    hidden = (jax.nn.silu(gate_acts) * up_acts).astype(jnp.bfloat16)
    partial_value = jnp.dot(hidden, w_down[0], preferred_element_type=jnp.float32)
    own_share = lax.psum_scatter(partial_value, "tensor", scatter_dimension=1, tiled=True)
    returned = lax.all_to_all(
        own_share.reshape(experts, capacity, feat_width),
        "expert",
        split_axis=0,
        concat_axis=0,
        tiled=True,
    )
    combined = jnp.dot(
        mixing,
        returned.reshape(experts * capacity, feat_width),
        precision=lax.Precision.HIGHEST,
        preferred_element_type=jnp.float32,
    )
    return combined.astype(jnp.bfloat16)


def selection(ids, first_expert, experts, capacity):
    tokens = ids.shape[0]
    columns = experts * capacity
    column = lax.broadcasted_iota(jnp.int32, (tokens, columns), 1)
    expert = first_expert + column // capacity
    expert = jnp.where(expert >= experts, expert - experts, expert)
    slot = column % capacity
    first = ids[:, 0:1] == expert
    named = jnp.logical_or(first, ids[:, 1:2] == expert)
    row = lax.broadcasted_iota(jnp.int32, (tokens, tokens), 0)
    col = lax.broadcasted_iota(jnp.int32, (tokens, tokens), 1)
    earlier = jnp.where(col < row, 1.0, 0.0).astype(jnp.bfloat16)
    before = jnp.dot(
        earlier,
        jnp.where(named, 1.0, 0.0).astype(jnp.bfloat16),
        preferred_element_type=jnp.float32,
    )
    chosen = jnp.logical_and(named, before == slot.astype(jnp.float32))
    return first, chosen


def route_kernel(experts, capacity, ids_ref, weight_ref, x_ref, mix_ref, *out_refs):
    first, chosen = selection(ids_ref[...], lax.axis_index("expert"), experts, capacity)
    weight = weight_ref[...]
    mix_ref[...] = jnp.where(
        chosen, jnp.where(first, weight[:, 0:1], weight[:, 1:2]), 0.0
    )
    pick = jnp.where(chosen, 1.0, 0.0).astype(jnp.bfloat16)
    rows = lax.dot_general(
        pick, x_ref[...], (((0,), (0,)), ((), ())), preferred_element_type=jnp.float32
    ).astype(jnp.bfloat16)
    for j in range(experts):
        out_refs[j][...] = rows[j * capacity : (j + 1) * capacity]


def route(stashed, expert_ids, combine_weight, experts, capacity):
    tokens, width = stashed.shape
    outs = pl.pallas_call(
        functools.partial(route_kernel, experts, capacity),
        out_shape=[jax.ShapeDtypeStruct((tokens, experts * capacity), jnp.float32)]
        + [jax.ShapeDtypeStruct((capacity, width), jnp.bfloat16)] * experts,
        in_specs=whole(3),
        out_specs=whole(experts + 1),
        compiler_params=params(8),
        name="route",
    )(expert_ids, combine_weight, stashed)
    return outs[0], outs[1:]


def gate_up_kernel(count, blocks_ref, gate_ref, up_ref, *refs):
    xs = refs[:count]
    hidden_ref = refs[count]
    x_ref, g_ref, u_ref = refs[count + 1 :]
    step = pl.program_id(0)
    for i in range(count):

        @pl.when(step == i)
        def _():
            x_ref[...] = xs[i][...]

    x = x_ref[...]
    gate = contract_last(x, gate_ref[0])
    up = contract_last(x, up_ref[0])

    @pl.when(step == 0)
    def _():
        g_ref[...] = gate
        u_ref[...] = up

    @pl.when(step > 0)
    def _():
        g_ref[...] += gate
        u_ref[...] += up

    @pl.when(step == count - 1)
    def _():
        g = g_ref[...]
        hidden_ref[...] = (g / (1.0 + jnp.exp(-g)) * u_ref[...]).astype(jnp.bfloat16)


def gate_up(pieces, blocks, w_gate, w_up):
    rows, width = pieces[0].shape
    hid = w_gate.shape[1]
    count = len(pieces)
    spec = pl.BlockSpec((1, hid, width), lambda k, b: (0, 0, b[k]))
    return pl.pallas_call(
        functools.partial(gate_up_kernel, count),
        out_shape=jax.ShapeDtypeStruct((rows, hid), jnp.bfloat16),
        grid_spec=pltpu.PrefetchScalarGridSpec(
            num_scalar_prefetch=1,
            grid=(count,),
            in_specs=[spec, spec] + whole(count),
            out_specs=pl.BlockSpec(memory_space=VM),
            scratch_shapes=[
                VM((rows, width), jnp.bfloat16),
                VM((rows, hid), jnp.float32),
                VM((rows, hid), jnp.float32),
            ],
        ),
        compiler_params=params(20),
        cost_estimate=pl.CostEstimate(
            flops=4 * rows * width * hid * count,
            bytes_accessed=4 * hid * width * count,
            transcendentals=0,
        ),
        name="gate_up",
    )(blocks, w_gate, w_up, *pieces)


def down_kernel(count, blocks_ref, down_ref, hidden_ref, *out_refs):
    step = pl.program_id(0)
    value = jnp.dot(hidden_ref[...], down_ref[0], preferred_element_type=jnp.float32)
    for i in range(count):

        @pl.when(step == i)
        def _():
            out_refs[i][...] = value.astype(out_refs[i].dtype)


def down(hidden, blocks, w_down, width, kinds):
    rows, hid = hidden.shape
    count = len(kinds)
    return pl.pallas_call(
        functools.partial(down_kernel, count),
        out_shape=[jax.ShapeDtypeStruct((rows, width), kind) for kind in kinds],
        grid_spec=pltpu.PrefetchScalarGridSpec(
            num_scalar_prefetch=1,
            grid=(count,),
            in_specs=[
                pl.BlockSpec((1, hid, width), lambda k, b: (0, 0, b[k])),
                pl.BlockSpec(memory_space=VM),
            ],
            out_specs=whole(count),
        ),
        compiler_params=params(16),
        cost_estimate=pl.CostEstimate(
            flops=2 * rows * width * hid * count,
            bytes_accessed=2 * hid * width * count,
            transcendentals=0,
        ),
        name="down",
    )(blocks, w_down, hidden)


def combine_kernel(mix_ref, *refs):
    out_ref = refs[-1]
    blocks = refs[:-1]
    capacity = blocks[0].shape[0]
    mix = mix_ref[...]
    high = mix.astype(jnp.bfloat16)
    low = (mix - high.astype(jnp.float32)).astype(jnp.bfloat16)
    total = jnp.zeros(out_ref.shape, jnp.float32)
    for j, block in enumerate(blocks):
        part = slice(j * capacity, (j + 1) * capacity)
        rows = block[...]
        total += jnp.dot(high[:, part], rows, preferred_element_type=jnp.float32)
        total += jnp.dot(low[:, part], rows, preferred_element_type=jnp.float32)
    out_ref[...] = total.astype(out_ref.dtype)


def combine(mix, blocks):
    width = blocks[0].shape[1]
    return pl.pallas_call(
        combine_kernel,
        out_shape=jax.ShapeDtypeStruct((mix.shape[0], width), jnp.bfloat16),
        in_specs=whole(len(blocks) + 1),
        out_specs=pl.BlockSpec(memory_space=VM),
        compiler_params=params(8),
        name="combine",
    )(mix, *blocks)


def slots_of(tokens, experts):
    return min(tokens, 8 * tokens // (3 * experts))


def stage_bits(tensor, core):
    bits = list(range(1, tensor.bit_length() - 1))
    return bits if core == 0 else bits[::-1]


def shards(tensor, stashed, expert_ids, combine_weight, w_gate, w_up, w_down):
    tokens, width = stashed.shape
    experts = lax.axis_size("expert")
    capacity = slots_of(tokens, experts)
    stages = tensor.bit_length() - 2
    subsets = 1 << stages

    def shift(value, by):
        return lax.ppermute(value, "expert", [(i, (i + by) % experts) for i in range(experts)])

    def swap(value):
        return lax.ppermute(value, "tensor", [(i, i ^ 1) for i in range(tensor)])

    def hop(value, stage):
        pairs = [(i, i ^ (1 << stage_bits(tensor, i & 1)[stage])) for i in range(tensor)]
        return lax.ppermute(value, "tensor", pairs)

    def reach(core):
        bits = stage_bits(tensor, core)
        return [sum(1 << bits[s] for s in range(stages) if k >> s & 1) for k in range(subsets)]

    me = lax.axis_index("tensor")
    even = me % 2 == 0
    near = jnp.where(even, jnp.array(reach(0), jnp.int32), jnp.array(reach(1), jnp.int32))
    far = jnp.where(even, jnp.array(reach(1), jnp.int32), jnp.array(reach(0), jnp.int32))
    mine = me ^ near
    theirs = me ^ 1 ^ far

    mix, outgoing = route(stashed, expert_ids, combine_weight, experts, capacity)
    arrived = [outgoing[0]] + [shift(outgoing[j], j) for j in range(1, experts)]
    pieces = [jnp.concatenate(arrived, axis=0)]
    for stage in range(stages):
        pieces = pieces + [hop(piece, stage) for piece in pieces]
    pieces = pieces + [swap(piece) for piece in pieces]

    hidden = gate_up(pieces, jnp.concatenate([mine, theirs]), w_gate, w_up)

    given = down(hidden, theirs, w_down, width, [jnp.bfloat16] * subsets)
    kept = down(hidden, mine, w_down, width, [jnp.float32] * subsets)
    sums = [k + swap(g).astype(jnp.float32) for k, g in zip(kept, given)]
    for stage in reversed(range(stages)):
        half = 1 << stage
        for k in range(half):
            got = hop(sums[half + k].astype(jnp.bfloat16), stage)
            sums[k] = sums[k] + got.astype(jnp.float32)
    result = sums[0].astype(jnp.bfloat16)
    parts = [result[j * capacity : (j + 1) * capacity] for j in range(experts)]
    back = [parts[0]] + [shift(parts[j], -j) for j in range(1, experts)]
    return combine(mix, back)


def solution(mesh):
    experts, tensor = mesh.shape["expert"], mesh.shape["tensor"]

    def body(stashed, expert_ids, combine_weight, w_gate, w_up, w_down):
        tokens, width = stashed.shape
        aligned = (
            tensor >= 4
            and tensor & (tensor - 1) == 0
            and width % 128 == 0
            and w_gate.shape[1] % 128 == 0
            and slots_of(tokens, experts) % 16 == 0
        )
        form = functools.partial(shards, tensor) if aligned else shards_plain
        return form(stashed, expert_ids, combine_weight, w_gate, w_up, w_down)

    return jax.shard_map(
        body,
        mesh=mesh,
        in_specs=(
            P("expert", "tensor"),
            P("expert", None),
            P("expert", None),
            P("expert", "tensor", None),
            P("expert", "tensor", None),
            P("expert", "tensor", None),
        ),
        out_specs=P("expert", "tensor"),
        check_vma=False,
    )
```

time: 168 us -> 76.5 us (0.46)
  blocking collectives: 84.8 us -> 0 us
  waiting for transfers between devices: 49.4 us -> 28.4 us
  starting transfers between devices: 0.01 us -> 20.7 us
  Pallas kernels: 0 us -> 16.8 us
  matrix products: 15.9 us -> 0 us
  between operations: 13.4 us -> 0.12 us
  local copies, waits for them, and re-layouts: 1.42 us -> 9.08 us
  other arithmetic: 3.03 us -> 1.15 us
    all_to_all x2 -> x0, blocking collectives: 72.3 us -> none  [the longest x1 53.4 us: shards(): lax.all_to_all(outgoing, 'expert', split_axis=0, concat_axis=0, tiled=True)]
    reduce_scatter x1 -> x0, waiting for transfers between devices: 49.4 us -> none  [shards(): lax.psum_scatter(partial_value, 'tensor', scatter_dimension=1, tiled=True)]
    ppermute x0 -> x20, waiting for transfers between devices: none -> 28.4 us  [the longest x6 19.7 us: hop(): return lax.ppermute(value, 'tensor', pairs)]
    ppermute x0 -> x20, starting transfers between devices: none -> 20.7 us  [the longest x6 11.1 us: shift(): lax.ppermute(value, 'expert', [(i, (i + by) % experts) for i in range(exp...]
    pallas_call x0 -> x5, Pallas kernels: none -> 16.8 us  [the longest x1 9.77 us: gate_up(): pl.pallas_call(functools.partial(gate_up_kernel, count), out_shape=jax.Sh...]
    dot_general x4 -> x0, matrix products: 15.9 us -> none  [the longest x1 11.7 us: shards(): result = jnp.dot(hidden, down_w, preferred_element_type=jnp.float32)]
    all_gather x1 -> x0, blocking collectives: 12.5 us -> none  [shards(): gathered = lax.all_gather(stashed, 'tensor', axis=1, tiled=True)]
    unnamed x4 -> x15, local copies, waits for them, and re-layouts: 0.78 us -> 9.05 us
  transfers between devices with their start and end apart: 1 -> 20, of which waited for: 1 -> 11; matrix products, arithmetic and copies ran while one was open for 0% -> 1% of each run, Pallas kernels for 0% -> 4%
where the time goes in v1:
time: 76.5 us; the launch traced here: 76.3 us
  waiting for transfers between devices  28.4 us (37%)
  starting transfers between devices  20.7 us (27%)
  Pallas kernels  16.8 us (22%)
  local copies, waits for them, and re-layouts  9.08 us (12%)
  other arithmetic  1.15 us (2%)
    ppermute x6, waiting for transfers between devices, hop(): return lax.ppermute(value, 'tensor', pairs)  19.7 us
    ppermute x6, starting transfers between devices, shift(): lax.ppermute(value, 'expert', [(i, (i + by) % experts) for i in range(exp...  11.1 us
    pallas_call x1, Pallas kernels, gate_up(): pl.pallas_call(functools.partial(gate_up_kernel, count), out_shape=jax.Sh...  9.77 us
    unnamed x15, local copies, waits for them, and re-layouts  9.05 us
    ppermute x6, starting transfers between devices, hop(): return lax.ppermute(value, 'tensor', pairs)  7.88 us
    ppermute x6, waiting for transfers between devices, shift(): lax.ppermute(value, 'expert', [(i, (i + by) % experts) for i in range(exp...  7.88 us
    pallas_call x2, Pallas kernels, down(): pl.pallas_call(functools.partial(down_kernel, count), out_shape=[jax.Shap...  5.61 us
    ppermute x8, starting transfers between devices, swap(): return lax.ppermute(value, 'tensor', [(i, i ^ 1) for i in range(tensor)])  1.74 us
  transfers between devices with their start and end apart: 20, of which 11 were waited for; matrix products, arithmetic and copies ran while one was open for 1% of the time, Pallas kernels for 4%

profile of v1, /device:TPU:0, one launch (start us, length us, event | category | flops | bytes accessed | tf_op | source)
XLA Modules:
  0.0 76.3 jit_solution(12619258211543615666)
XLA Ops:
  0.0 0.8 %copy.11.ids_ref = s32[96,2]{1,0:T(8,128)S(1)} copy(s32[96,2]{0,1:T(2,128)} %param.11) | data formatting | bytes 1536 | tf_op args[1]
  0.8 0.8 %copy.12.weight_ref = f32[96,2]{1,0:T(8,128)S(1)} copy(f32[96,2]{0,1:T(2,128)} %param.12) | data formatting | bytes 1536 | tf_op args[2]
  1.6 0.9 %copy-done.2 = bf16[96,512]{1,0:T(8,128)(2,1)S(1)} copy-done((bf16[96,512]{1,0:T(8,128)(2,1)S(1)}, bf16[96,512]{1,0:T(8,128)(2,1)}, u32[]{:S(2)}) %copy-start.2) | copy-done | bytes 98328
  2.9 3.1 %collective-permute-start = (bf16[64,512]{1,0:T(8,128)(2,1)S(1)}, bf16[64,512]{1,0:T(8,128)(2,1)S(1)}, u32[]{:S(2)}, u32[]{:S(2)}) collective-permute-start(bf16[64,512]{1,0:T(8,128)(2,1)S(1)} %get-tuple-element.20), channel_id=1, source_target_pairs={{0,8},{8,16},{16,24},{24,0},{1,9},{9,17},{17,25},{25,1},{2,10},{10... | collective-permute-start | bytes 196616 | tf_op jit(solution)/shard_map/ppermute | solution.py:262
  6.0 2.6 %collective-permute-start.1 = (bf16[64,512]{1,0:T(8,128)(2,1)S(1)}, bf16[64,512]{1,0:T(8,128)(2,1)S(1)}, u32[]{:S(2)}, u32[]{:S(2)}) collective-permute-start(bf16[64,512]{1,0:T(8,128)(2,1)S(1)} %get-tuple-element.21), channel_id=1, source_target_pairs={{0,16},{8,24},{16,0},{24,8},{1,17},{9,25},{17,1},{25,9},{2,18},{10... | collective-permute-start | bytes 196616 | tf_op jit(solution)/shard_map/ppermute | solution.py:262
  8.6 1.3 %collective-permute-start.2 = (bf16[64,512]{1,0:T(8,128)(2,1)S(1)}, bf16[64,512]{1,0:T(8,128)(2,1)S(1)}, u32[]{:S(2)}, u32[]{:S(2)}) collective-permute-start(bf16[64,512]{1,0:T(8,128)(2,1)S(1)} %get-tuple-element.22), channel_id=1, source_target_pairs={{0,24},{8,0},{16,8},{24,16},{1,25},{9,1},{17,9},{25,17},{2,26},{10... | collective-permute-start | bytes 196616 | tf_op jit(solution)/shard_map/ppermute | solution.py:262
  10.0 0.5 collective-permute-done
  10.5 2.6 %collective-permute-done.1 = bf16[64,512]{1,0:T(8,128)(2,1)S(1)} collective-permute-done((bf16[64,512]{1,0:T(8,128)(2,1)S(1)}, bf16[64,512]{1,0:T(8,128)(2,1)S(1)}, u32[]{:S(2)}, u32[]{:S(2)}) %collective-permute-start.1) | collective-permute-done | bytes 65568 | tf_op jit(solution)/shard_map/ppermute | solution.py:262
  13.3 1.6 %collective-permute-start.3 = (bf16[256,512]{1,0:T(8,128)(2,1)S(1)}, bf16[256,512]{1,0:T(8,128)(2,1)S(1)}, u32[]{:S(2)}, u32[]{:S(2)}) collective-permute-start(bf16[256,512]{1,0:T(8,128)(2,1)S(1)} %constant_dynamic-update-slice_fusion.refs_0_), channel_id=1, source_target_pairs={{0,2},{1,5},{2,0},{3,7},{4,6},{5,1},{6,4},{7,3},{8,10},{9,13},{10,... | collective-permute-start | bytes 786440 | tf_op jit(solution)/shard_map/ppermute | solution.py:269
  14.9 1.5 %collective-permute-start.4 = (bf16[256,512]{1,0:T(8,128)(2,1)S(1)}, bf16[256,512]{1,0:T(8,128)(2,1)S(1)}, u32[]{:S(2)}, u32[]{:S(2)}) collective-permute-start(bf16[256,512]{1,0:T(8,128)(2,1)S(1)} %constant_dynamic-update-slice_fusion.refs_0_), channel_id=1, source_target_pairs={{0,4},{1,3},{2,6},{3,1},{4,0},{5,7},{6,2},{7,5},{8,12},{9,11},{10,... | collective-permute-start | bytes 786440 | tf_op jit(solution)/shard_map/ppermute | solution.py:269
  16.4 6.1 %collective-permute-done.3.refs_1_ = bf16[256,512]{1,0:T(8,128)(2,1)S(1)} collective-permute-done((bf16[256,512]{1,0:T(8,128)(2,1)S(1)}, bf16[256,512]{1,0:T(8,128)(2,1)S(1)}, u32[]{:S(2)}, u32[]{:S(2)}) %collective-permute-start.3) | collective-permute-done | bytes 262176 | tf_op jit(solution)/shard_map/ppermute | solution.py:269
  22.5 1.2 %collective-permute-start.5 = (bf16[256,512]{1,0:T(8,128)(2,1)S(1)}, bf16[256,512]{1,0:T(8,128)(2,1)S(1)}, u32[]{:S(2)}, u32[]{:S(2)}) collective-permute-start(bf16[256,512]{1,0:T(8,128)(2,1)S(1)} %collective-permute-done.3.refs_1_), channel_id=1, source_target_pairs={{0,4},{1,3},{2,6},{3,1},{4,0},{5,7},{6,2},{7,5},{8,12},{9,11},{10,... | collective-permute-start | bytes 786440 | tf_op jit(solution)/shard_map/ppermute | solution.py:269
  23.7 0.5 collective-permute-start.7
  24.3 4.6 %collective-permute-done.5.refs_3_ = bf16[256,512]{1,0:T(8,128)(2,1)S(1)} collective-permute-done((bf16[256,512]{1,0:T(8,128)(2,1)S(1)}, bf16[256,512]{1,0:T(8,128)(2,1)S(1)}, u32[]{:S(2)}, u32[]{:S(2)}) %collective-permute-start.5) | collective-permute-done | bytes 262176 | tf_op jit(solution)/shard_map/ppermute | solution.py:269
  28.9 0.7 fusion.1
  29.7 0.8 %collective-permute-done.9.refs_7_ = bf16[256,512]{1,0:T(8,128)(2,1)S(1)} collective-permute-done((bf16[256,512]{1,0:T(8,128)(2,1)S(1)}, bf16[256,512]{1,0:T(8,128)(2,1)S(1)}, u32[]{:S(2)}, u32[]{:S(2)}) %collective-permute-start.9) | collective-permute-done | bytes 262176 | tf_op jit(solution)/shard_map/ppermute | solution.py:265
  30.4 3.5 %copy-done = bf16[1,896,4096]{2,1,0:T(8,128)(2,1)S(1)} copy-done((bf16[1,896,4096]{2,1,0:T(8,128)(2,1)S(1)}, bf16[1,896,4096]{2,1,0:T(8,128)(2,1)}, u32[]{:S(2)}) %copy-start) | copy-done | bytes 7340056
  33.9 3.1 %copy-done.1 = bf16[1,896,4096]{2,1,0:T(8,128)(2,1)S(1)} copy-done((bf16[1,896,4096]{2,1,0:T(8,128)(2,1)S(1)}, bf16[1,896,4096]{2,1,0:T(8,128)(2,1)}, u32[]{:S(2)}) %copy-start.1) | copy-done | bytes 7340056
  37.0 9.8 %gate_up.1.hidden_ref = bf16[256,896]{1,0:T(8,128)(2,1)S(1)} custom-call(s32[8]{0:T(128)S(1)} %pad_add_fusion.blocks_ref, bf16[1,896,4096]{2,1,0:T(8,128)(2,1)S(1)} %copy-done, bf16[1,896,4096]{2,1,0:T(8,128)(2,1)S(1)} %copy-done.1, bf16[256,512]{1,0:T(8,128)(2,1)S(1)} %constant_dynamic-update-slice_fusion.refs_0_, ...), custom_call_target="tpu_custom_call" | custom-call | flops 3758096384 | bytes 14680064 | tf_op jit(solution)/shard_map/gate_up/pallas_call | solution.py:158
  46.8 2.8 %down.3 = (bf16[256,512]{1,0:T(8,128)(2,1)S(1)}, bf16[256,512]{1,0:T(8,128)(2,1)S(1)}, bf16[256,512]{1,0:T(8,128)(2,1)S(1)}, bf16[256,512]{1,0:T(8,128)(2,1)S(1)}) custom-call(s32[4]{0:T(128)S(1)} %get-tuple-element.35.blocks_ref, bf16[1,896,4096]{2,1,0:T(8,128)(2,1)S(1)} %bitcast.1, bf16[256,896]{1,0:T(8,128)(2,1)S(1)} %gate_up.1.hidden_ref), custom_call_target="tpu_custom_call" | custom-call | flops 939524096 | bytes 3670016 | tf_op jit(solution)/shard_map/down/pallas_call | solution.py:195
  50.2 2.8 %down.2 = (f32[256,512]{1,0:T(8,128)S(1)}, f32[256,512]{1,0:T(8,128)S(1)}, f32[256,512]{1,0:T(8,128)S(1)}, f32[256,512]{1,0:T(8,128)S(1)}) custom-call(s32[4]{0:T(128)S(1)} %get-tuple-element.36.blocks_ref, bf16[1,896,4096]{2,1,0:T(8,128)(2,1)S(1)} %bitcast.1, bf16[256,896]{1,0:T(8,128)(2,1)S(1)} %gate_up.1.hidden_ref), custom_call_target="tpu_custom_call" | custom-call | flops 939524096 | bytes 3670016 | tf_op jit(solution)/shard_map/down/pallas_call | solution.py:195
  53.5 1.3 %collective-permute-start.15 = (bf16[256,512]{1,0:T(8,128)(2,1)S(1)}, bf16[256,512]{1,0:T(8,128)(2,1)S(1)}, u32[]{:S(2)}, u32[]{:S(2)}) collective-permute-start(bf16[256,512]{1,0:T(8,128)(2,1)S(1)} %add_convert_fusion.2), channel_id=1, source_target_pairs={{0,4},{1,3},{2,6},{3,1},{4,0},{5,7},{6,2},{7,5},{8,12},{9,11},{10,... | collective-permute-start | bytes 786440 | tf_op jit(solution)/shard_map/ppermute | solution.py:269
  55.1 0.7 collective-permute-start.12
  55.8 4.2 %collective-permute-done.15 = bf16[256,512]{1,0:T(8,128)(2,1)S(1)} collective-permute-done((bf16[256,512]{1,0:T(8,128)(2,1)S(1)}, bf16[256,512]{1,0:T(8,128)(2,1)S(1)}, u32[]{:S(2)}, u32[]{:S(2)}) %collective-permute-start.15) | collective-permute-done | bytes 262176 | tf_op jit(solution)/shard_map/ppermute | solution.py:269
  60.1 1.6 %collective-permute-start.16 = (bf16[256,512]{1,0:T(8,128)(2,1)S(1)}, bf16[256,512]{1,0:T(8,128)(2,1)S(1)}, u32[]{:S(2)}, u32[]{:S(2)}) collective-permute-start(bf16[256,512]{1,0:T(8,128)(2,1)S(1)} %add_convert_fusion.1), channel_id=1, source_target_pairs={{0,2},{1,5},{2,0},{3,7},{4,6},{5,1},{6,4},{7,3},{8,10},{9,13},{10,... | collective-permute-start | bytes 786440 | tf_op jit(solution)/shard_map/ppermute | solution.py:269
  61.7 1.8 %collective-permute-done.12 = bf16[256,512]{1,0:T(8,128)(2,1)S(1)} collective-permute-done((bf16[256,512]{1,0:T(8,128)(2,1)S(1)}, bf16[256,512]{1,0:T(8,128)(2,1)S(1)}, u32[]{:S(2)}, u32[]{:S(2)}) %collective-permute-start.12) | collective-permute-done | bytes 262176 | tf_op jit(solution)/shard_map/ppermute | solution.py:269
  63.5 3.0 %collective-permute-done.16 = bf16[256,512]{1,0:T(8,128)(2,1)S(1)} collective-permute-done((bf16[256,512]{1,0:T(8,128)(2,1)S(1)}, bf16[256,512]{1,0:T(8,128)(2,1)S(1)}, u32[]{:S(2)}, u32[]{:S(2)}) %collective-permute-start.16) | collective-permute-done | bytes 262176 | tf_op jit(solution)/shard_map/ppermute | solution.py:269
  66.7 1.6 %collective-permute-start.19 = (bf16[64,512]{1,0:T(8,128)(2,1)S(1)}, bf16[64,512]{1,0:T(8,128)(2,1)S(1)}, u32[]{:S(2)}, u32[]{:S(2)}) collective-permute-start(bf16[64,512]{1,0:T(8,128)(2,1)S(1)} %get-tuple-element.31), channel_id=1, source_target_pairs={{0,8},{8,16},{16,24},{24,0},{1,9},{9,17},{17,25},{25,1},{2,10},{10... | collective-permute-start | bytes 196616 | tf_op jit(solution)/shard_map/ppermute | solution.py:262
  68.3 2.1 %collective-permute-start.18 = (bf16[64,512]{1,0:T(8,128)(2,1)S(1)}, bf16[64,512]{1,0:T(8,128)(2,1)S(1)}, u32[]{:S(2)}, u32[]{:S(2)}) collective-permute-start(bf16[64,512]{1,0:T(8,128)(2,1)S(1)} %get-tuple-element.32), channel_id=1, source_target_pairs={{0,16},{8,24},{16,0},{24,8},{1,17},{9,25},{17,1},{25,9},{2,18},{10... | collective-permute-start | bytes 196616 | tf_op jit(solution)/shard_map/ppermute | solution.py:262
  70.8 2.5 %collective-permute-done.19.refs_3_ = bf16[64,512]{1,0:T(8,128)(2,1)S(1)} collective-permute-done((bf16[64,512]{1,0:T(8,128)(2,1)S(1)}, bf16[64,512]{1,0:T(8,128)(2,1)S(1)}, u32[]{:S(2)}, u32[]{:S(2)}) %collective-permute-start.19) | collective-permute-done | bytes 65568 | tf_op jit(solution)/shard_map/ppermute | solution.py:262
  73.3 2.0 %collective-permute-done.18.refs_2_ = bf16[64,512]{1,0:T(8,128)(2,1)S(1)} collective-permute-done((bf16[64,512]{1,0:T(8,128)(2,1)S(1)}, bf16[64,512]{1,0:T(8,128)(2,1)S(1)}, u32[]{:S(2)}, u32[]{:S(2)}) %collective-permute-start.18) | collective-permute-done | bytes 65568 | tf_op jit(solution)/shard_map/ppermute | solution.py:262
  75.3 1.0 %combine.1 = bf16[96,512]{1,0:T(8,128)(2,1)} custom-call(f32[96,256]{1,0:T(8,128)S(1)} %get-tuple-element.18.mix_ref, bf16[64,512]{1,0:T(8,128)(2,1)S(1)} %get-tuple-element.34.refs_0_, bf16[64,512]{1,0:T(8,128)(2,1)S(1)} %collective-permute-done.17.refs_1_, bf16[64,512]{1,0:T(8,128)(2,1)S(1)} %collective-permute-done.18.refs_2_, ...), custom_call_target="tpu_custom_call" | custom-call | tf_op jit(solution)/shard_map/combine/pallas_call | solution.py:235
  (37 shorter events, 2.8 us)
Async XLA Ops:
  1.6 0.9 %copy-start.2 = (bf16[96,512]{1,0:T(8,128)(2,1)S(1)}, bf16[96,512]{1,0:T(8,128)(2,1)}, u32[]{:S(2)}) copy-start(bf16[96,512]{1,0:T(8,128)(2,1)} %x_ref.1) | copy-start | bytes 294916
  2.9 7.6 %collective-permute-start = (bf16[64,512]{1,0:T(8,128)(2,1)S(1)}, bf16[64,512]{1,0:T(8,128)(2,1)S(1)}, u32[]{:S(2)}, u32[]{:S(2)}) collective-permute-start(bf16[64,512]{1,0:T(8,128)(2,1)S(1)} %get-tuple-element.20), channel_id=1, source_target_pairs={{0,8},{8,16},{16,24},{24,0},{1,9},{9,17},{17,25},{25,1},{2,10},{10... | collective-permute-start | bytes 196616 | tf_op jit(solution)/shard_map/ppermute | solution.py:262
  6.0 7.1 %collective-permute-start.1 = (bf16[64,512]{1,0:T(8,128)(2,1)S(1)}, bf16[64,512]{1,0:T(8,128)(2,1)S(1)}, u32[]{:S(2)}, u32[]{:S(2)}) collective-permute-start(bf16[64,512]{1,0:T(8,128)(2,1)S(1)} %get-tuple-element.21), channel_id=1, source_target_pairs={{0,16},{8,24},{16,0},{24,8},{1,17},{9,25},{17,1},{25,9},{2,18},{10... | collective-permute-start | bytes 196616 | tf_op jit(solution)/shard_map/ppermute | solution.py:262
  8.6 4.7 %collective-permute-start.2 = (bf16[64,512]{1,0:T(8,128)(2,1)S(1)}, bf16[64,512]{1,0:T(8,128)(2,1)S(1)}, u32[]{:S(2)}, u32[]{:S(2)}) collective-permute-start(bf16[64,512]{1,0:T(8,128)(2,1)S(1)} %get-tuple-element.22), channel_id=1, source_target_pairs={{0,24},{8,0},{16,8},{24,16},{1,25},{9,1},{17,9},{25,17},{2,26},{10... | collective-permute-start | bytes 196616 | tf_op jit(solution)/shard_map/ppermute | solution.py:262
  13.3 9.2 %collective-permute-start.3 = (bf16[256,512]{1,0:T(8,128)(2,1)S(1)}, bf16[256,512]{1,0:T(8,128)(2,1)S(1)}, u32[]{:S(2)}, u32[]{:S(2)}) collective-permute-start(bf16[256,512]{1,0:T(8,128)(2,1)S(1)} %constant_dynamic-update-slice_fusion.refs_0_), channel_id=1, source_target_pairs={{0,2},{1,5},{2,0},{3,7},{4,6},{5,1},{6,4},{7,3},{8,10},{9,13},{10,... | collective-permute-start | bytes 786440 | tf_op jit(solution)/shard_map/ppermute | solution.py:269
  14.9 9.3 %collective-permute-start.4 = (bf16[256,512]{1,0:T(8,128)(2,1)S(1)}, bf16[256,512]{1,0:T(8,128)(2,1)S(1)}, u32[]{:S(2)}, u32[]{:S(2)}) collective-permute-start(bf16[256,512]{1,0:T(8,128)(2,1)S(1)} %constant_dynamic-update-slice_fusion.refs_0_), channel_id=1, source_target_pairs={{0,4},{1,3},{2,6},{3,1},{4,0},{5,7},{6,2},{7,5},{8,12},{9,11},{10,... | collective-permute-start | bytes 786440 | tf_op jit(solution)/shard_map/ppermute | solution.py:269
  22.5 6.4 %collective-permute-start.5 = (bf16[256,512]{1,0:T(8,128)(2,1)S(1)}, bf16[256,512]{1,0:T(8,128)(2,1)S(1)}, u32[]{:S(2)}, u32[]{:S(2)}) collective-permute-start(bf16[256,512]{1,0:T(8,128)(2,1)S(1)} %collective-permute-done.3.refs_1_), channel_id=1, source_target_pairs={{0,4},{1,3},{2,6},{3,1},{4,0},{5,7},{6,2},{7,5},{8,12},{9,11},{10,... | collective-permute-start | bytes 786440 | tf_op jit(solution)/shard_map/ppermute | solution.py:269
  23.7 5.9 %collective-permute-start.6 = (bf16[256,512]{1,0:T(8,128)(2,1)S(1)}, bf16[256,512]{1,0:T(8,128)(2,1)S(1)}, u32[]{:S(2)}, u32[]{:S(2)}) collective-permute-start(bf16[256,512]{1,0:T(8,128)(2,1)S(1)} %constant_dynamic-update-slice_fusion.refs_0_), channel_id=1, source_target_pairs={{0,1},{1,0},{2,3},{3,2},{4,5},{5,4},{6,7},{7,6},{8,9},{9,8},{10,11... | collective-permute-start | bytes 786440 | tf_op jit(solution)/shard_map/ppermute | solution.py:265
  23.7 5.9 %collective-permute-start.7 = (bf16[256,512]{1,0:T(8,128)(2,1)S(1)}, bf16[256,512]{1,0:T(8,128)(2,1)S(1)}, u32[]{:S(2)}, u32[]{:S(2)}) collective-permute-start(bf16[256,512]{1,0:T(8,128)(2,1)S(1)} %collective-permute-done.3.refs_1_), channel_id=1, source_target_pairs={{0,1},{1,0},{2,3},{3,2},{4,5},{5,4},{6,7},{7,6},{8,9},{9,8},{10,11... | collective-permute-start | bytes 786440 | tf_op jit(solution)/shard_map/ppermute | solution.py:265
  24.2 5.4 %collective-permute-start.8 = (bf16[256,512]{1,0:T(8,128)(2,1)S(1)}, bf16[256,512]{1,0:T(8,128)(2,1)S(1)}, u32[]{:S(2)}, u32[]{:S(2)}) collective-permute-start(bf16[256,512]{1,0:T(8,128)(2,1)S(1)} %collective-permute-done.4.refs_2_), channel_id=1, source_target_pairs={{0,1},{1,0},{2,3},{3,2},{4,5},{5,4},{6,7},{7,6},{8,9},{9,8},{10,11... | collective-permute-start | bytes 786440 | tf_op jit(solution)/shard_map/ppermute | solution.py:265
  28.9 1.5 %collective-permute-start.9 = (bf16[256,512]{1,0:T(8,128)(2,1)S(1)}, bf16[256,512]{1,0:T(8,128)(2,1)S(1)}, u32[]{:S(2)}, u32[]{:S(2)}) collective-permute-start(bf16[256,512]{1,0:T(8,128)(2,1)S(1)} %collective-permute-done.5.refs_3_), channel_id=1, source_target_pairs={{0,1},{1,0},{2,3},{3,2},{4,5},{5,4},{6,7},{7,6},{8,9},{9,8},{10,11... | collective-permute-start | bytes 786440 | tf_op jit(solution)/shard_map/ppermute | solution.py:265
  29.6 17.2 %slice-start = ((s8[7340032]{0:T(1024)(128)(4,1)}), s8[4194304]{0:T(1024)(128)(4,1)S(1)}, s32[]{:S(2)}) async-start(s8[7340032]{0:T(1024)(128)(4,1)} %bitcast), calls=%async_computation | async-start | bytes 8388608
  29.6 17.2 %slice-start.1 = ((s8[7340032]{0:T(1024)(128)(4,1)}), s8[3145728]{0:T(1024)(128)(4,1)S(1)}, s32[]{:S(2)}) async-start(s8[7340032]{0:T(1024)(128)(4,1)} %bitcast), calls=%async_computation.1 | async-start | bytes 6291456
  30.4 3.5 %copy-start = (bf16[1,896,4096]{2,1,0:T(8,128)(2,1)S(1)}, bf16[1,896,4096]{2,1,0:T(8,128)(2,1)}, u32[]{:S(2)}) copy-start(bf16[1,896,4096]{2,1,0:T(8,128)(2,1)} %gate_ref.1) | copy-start | bytes 22020100
  33.9 3.1 %copy-start.1 = (bf16[1,896,4096]{2,1,0:T(8,128)(2,1)S(1)}, bf16[1,896,4096]{2,1,0:T(8,128)(2,1)}, u32[]{:S(2)}) copy-start(bf16[1,896,4096]{2,1,0:T(8,128)(2,1)} %up_ref.1) | copy-start | bytes 22020100
  49.6 3.8 %collective-permute-start.14 = (bf16[256,512]{1,0:T(8,128)(2,1)S(1)}, bf16[256,512]{1,0:T(8,128)(2,1)S(1)}, u32[]{:S(2)}, u32[]{:S(2)}) collective-permute-start(bf16[256,512]{1,0:T(8,128)(2,1)S(1)} %get-tuple-element.30), channel_id=1, source_target_pairs={{0,1},{1,0},{2,3},{3,2},{4,5},{5,4},{6,7},{7,6},{8,9},{9,8},{10,11... | collective-permute-start | bytes 786440 | tf_op jit(solution)/shard_map/ppermute | solution.py:265
  50.1 5.0 %collective-permute-start.11 = (bf16[256,512]{1,0:T(8,128)(2,1)S(1)}, bf16[256,512]{1,0:T(8,128)(2,1)S(1)}, u32[]{:S(2)}, u32[]{:S(2)}) collective-permute-start(bf16[256,512]{1,0:T(8,128)(2,1)S(1)} %get-tuple-element.26), channel_id=1, source_target_pairs={{0,1},{1,0},{2,3},{3,2},{4,5},{5,4},{6,7},{7,6},{8,9},{9,8},{10,11... | collective-permute-start | bytes 786440 | tf_op jit(solution)/shard_map/ppermute | solution.py:265
  53.0 2.8 %collective-permute-start.13 = (bf16[256,512]{1,0:T(8,128)(2,1)S(1)}, bf16[256,512]{1,0:T(8,128)(2,1)S(1)}, u32[]{:S(2)}, u32[]{:S(2)}) collective-permute-start(bf16[256,512]{1,0:T(8,128)(2,1)S(1)} %get-tuple-element.28), channel_id=1, source_target_pairs={{0,1},{1,0},{2,3},{3,2},{4,5},{5,4},{6,7},{7,6},{8,9},{9,8},{10,11... | collective-permute-start | bytes 786440 | tf_op jit(solution)/shard_map/ppermute | solution.py:265
  53.5 6.4 %collective-permute-start.15 = (bf16[256,512]{1,0:T(8,128)(2,1)S(1)}, bf16[256,512]{1,0:T(8,128)(2,1)S(1)}, u32[]{:S(2)}, u32[]{:S(2)}) collective-permute-start(bf16[256,512]{1,0:T(8,128)(2,1)S(1)} %add_convert_fusion.2), channel_id=1, source_target_pairs={{0,4},{1,3},{2,6},{3,1},{4,0},{5,7},{6,2},{7,5},{8,12},{9,11},{10,... | collective-permute-start | bytes 786440 | tf_op jit(solution)/shard_map/ppermute | solution.py:269
  54.8 6.9 %collective-permute-start.10 = (bf16[256,512]{1,0:T(8,128)(2,1)S(1)}, bf16[256,512]{1,0:T(8,128)(2,1)S(1)}, u32[]{:S(2)}, u32[]{:S(2)}) collective-permute-start(bf16[256,512]{1,0:T(8,128)(2,1)S(1)} %get-tuple-element.24), channel_id=1, source_target_pairs={{0,1},{1,0},{2,3},{3,2},{4,5},{5,4},{6,7},{7,6},{8,9},{9,8},{10,11... | collective-permute-start | bytes 786440 | tf_op jit(solution)/shard_map/ppermute | solution.py:265
  55.1 8.4 %collective-permute-start.12 = (bf16[256,512]{1,0:T(8,128)(2,1)S(1)}, bf16[256,512]{1,0:T(8,128)(2,1)S(1)}, u32[]{:S(2)}, u32[]{:S(2)}) collective-permute-start(bf16[256,512]{1,0:T(8,128)(2,1)S(1)} %add_convert_fusion.3), channel_id=1, source_target_pairs={{0,4},{1,3},{2,6},{3,1},{4,0},{5,7},{6,2},{7,5},{8,12},{9,11},{10,... | collective-permute-start | bytes 786440 | tf_op jit(solution)/shard_map/ppermute | solution.py:269
  60.1 6.4 %collective-permute-start.16 = (bf16[256,512]{1,0:T(8,128)(2,1)S(1)}, bf16[256,512]{1,0:T(8,128)(2,1)S(1)}, u32[]{:S(2)}, u32[]{:S(2)}) collective-permute-start(bf16[256,512]{1,0:T(8,128)(2,1)S(1)} %add_convert_fusion.1), channel_id=1, source_target_pairs={{0,2},{1,5},{2,0},{3,7},{4,6},{5,1},{6,4},{7,3},{8,10},{9,13},{10,... | collective-permute-start | bytes 786440 | tf_op jit(solution)/shard_map/ppermute | solution.py:269
  66.7 6.6 %collective-permute-start.19 = (bf16[64,512]{1,0:T(8,128)(2,1)S(1)}, bf16[64,512]{1,0:T(8,128)(2,1)S(1)}, u32[]{:S(2)}, u32[]{:S(2)}) collective-permute-start(bf16[64,512]{1,0:T(8,128)(2,1)S(1)} %get-tuple-element.31), channel_id=1, source_target_pairs={{0,8},{8,16},{16,24},{24,0},{1,9},{9,17},{17,25},{25,1},{2,10},{10... | collective-permute-start | bytes 196616 | tf_op jit(solution)/shard_map/ppermute | solution.py:262
  68.3 7.0 %collective-permute-start.18 = (bf16[64,512]{1,0:T(8,128)(2,1)S(1)}, bf16[64,512]{1,0:T(8,128)(2,1)S(1)}, u32[]{:S(2)}, u32[]{:S(2)}) collective-permute-start(bf16[64,512]{1,0:T(8,128)(2,1)S(1)} %get-tuple-element.32), channel_id=1, source_target_pairs={{0,16},{8,24},{16,0},{24,8},{1,17},{9,25},{17,1},{25,9},{2,18},{10... | collective-permute-start | bytes 196616 | tf_op jit(solution)/shard_map/ppermute | solution.py:262
  70.4 4.9 %collective-permute-start.17 = (bf16[64,512]{1,0:T(8,128)(2,1)S(1)}, bf16[64,512]{1,0:T(8,128)(2,1)S(1)}, u32[]{:S(2)}, u32[]{:S(2)}) collective-permute-start(bf16[64,512]{1,0:T(8,128)(2,1)S(1)} %get-tuple-element.33), channel_id=1, source_target_pairs={{0,24},{8,0},{16,8},{24,16},{1,25},{9,1},{17,9},{25,17},{2,26},{10... | collective-permute-start | bytes 196616 | tf_op jit(solution)/shard_map/ppermute | solution.py:262

commit v2 on v0

v2 whole, which is shorter than its diff:
```python
import functools

import jax
import jax.numpy as jnp
from jax import lax
from jax.experimental import pallas as pl
from jax.experimental.pallas import tpu as pltpu
from jax.sharding import PartitionSpec as P


VM = pltpu.VMEM
MIB = 1 << 20


def whole(count):
    return [pl.BlockSpec(memory_space=VM)] * count


def params(mib):
    return pltpu.CompilerParams(vmem_limit_bytes=mib * MIB)


def slot_targets(expert_ids, experts, capacity):
    flat_ids = expert_ids.reshape(-1)
    one_hot = (flat_ids[:, None] == jnp.arange(experts, dtype=jnp.int32)[None, :]).astype(jnp.int32)
    before = jnp.cumsum(one_hot, axis=0) - one_hot
    slot_index = jnp.sum(before * one_hot, axis=1)
    return (flat_ids * capacity + slot_index).reshape(expert_ids.shape)


def contract_last(left, right):
    return lax.dot_general(
        left, right, (((1,), (1,)), ((), ())), preferred_element_type=jnp.float32
    )


def shards_plain(stashed, expert_ids, combine_weight, w_gate, w_up, w_down):
    tok_count = stashed.shape[0]
    feat_width = stashed.shape[1]
    experts = lax.axis_size("expert")
    capacity = slots_of(tok_count, experts)
    targets = slot_targets(expert_ids, experts, capacity)
    columns = jnp.arange(experts * capacity, dtype=jnp.int32)
    pair_match = (targets[:, :, None] == columns[None, None, :]).astype(jnp.float32)
    selector = jnp.sum(pair_match, axis=1).T.astype(jnp.bfloat16)
    mixing = jnp.sum(pair_match * combine_weight[:, :, None], axis=1)
    own = jnp.dot(selector, stashed, preferred_element_type=jnp.float32).astype(jnp.bfloat16)
    own = own.reshape(experts, capacity, feat_width)
    received = lax.all_to_all(own, "expert", split_axis=0, concat_axis=0, tiled=True)
    rows_in = lax.all_gather(
        received.reshape(experts * capacity, feat_width), "tensor", axis=1, tiled=True
    )
    gate_acts = contract_last(rows_in, w_gate[0])
    up_acts = contract_last(rows_in, w_up[0])
    hidden = (jax.nn.silu(gate_acts) * up_acts).astype(jnp.bfloat16)
    partial_value = jnp.dot(hidden, w_down[0], preferred_element_type=jnp.float32)
    own_share = lax.psum_scatter(partial_value, "tensor", scatter_dimension=1, tiled=True)
    returned = lax.all_to_all(
        own_share.reshape(experts, capacity, feat_width),
        "expert",
        split_axis=0,
        concat_axis=0,
        tiled=True,
    )
    combined = jnp.dot(
        mixing,
        returned.reshape(experts * capacity, feat_width),
        precision=lax.Precision.HIGHEST,
        preferred_element_type=jnp.float32,
    )
    return combined.astype(jnp.bfloat16)


def fetch(sem_ref, pairs):
    copies = [pltpu.make_async_copy(s, d, sem_ref.at[i]) for i, (s, d) in enumerate(pairs)]
    for copy in copies:
        copy.start()
    return copies


def selection(ids, first_expert, experts, capacity):
    tokens = ids.shape[1]
    rows = experts * capacity
    row = lax.broadcasted_iota(jnp.int32, (rows, tokens), 0)
    expert = first_expert + row // capacity
    expert = jnp.where(expert >= experts, expert - experts, expert)
    slot = row % capacity
    first = ids[0:1, :] == expert
    named = jnp.logical_or(first, ids[1:2, :] == expert)
    down = lax.broadcasted_iota(jnp.int32, (tokens, tokens), 0)
    across = lax.broadcasted_iota(jnp.int32, (tokens, tokens), 1)
    earlier = jnp.where(down < across, 1.0, 0.0).astype(jnp.bfloat16)
    before = jnp.dot(
        jnp.where(named, 1.0, 0.0).astype(jnp.bfloat16),
        earlier,
        preferred_element_type=jnp.float32,
    )
    return first, jnp.logical_and(named, before == slot.astype(jnp.float32))


def route_kernel(experts, capacity, ids_hbm, x_hbm, *refs):
    outs, (ids_ref, x_ref, sem_ref) = refs[:experts], refs[experts:]
    copies = fetch(sem_ref, [(ids_hbm, ids_ref), (x_hbm, x_ref)])
    copies[0].wait()
    _, chosen = selection(ids_ref[...], lax.axis_index("expert"), experts, capacity)
    pick = jnp.where(chosen, 1.0, 0.0).astype(jnp.bfloat16)
    copies[1].wait()
    x = x_ref[...]
    for j in range(experts):
        rows = pick[j * capacity : (j + 1) * capacity]
        outs[j][...] = jnp.dot(rows, x, preferred_element_type=jnp.float32).astype(jnp.bfloat16)


def route(stashed, ids, experts, capacity):
    _, width = stashed.shape
    return pl.pallas_call(
        functools.partial(route_kernel, experts, capacity),
        out_shape=[jax.ShapeDtypeStruct((capacity, width), jnp.bfloat16)] * experts,
        in_specs=[pl.BlockSpec(memory_space=pltpu.HBM)] * 2,
        out_specs=whole(experts),
        scratch_shapes=[
            VM(ids.shape, jnp.int32),
            VM(stashed.shape, jnp.bfloat16),
            pltpu.SemaphoreType.DMA((2,)),
        ],
        compiler_params=params(56),
        name="route",
    )(ids, stashed)


def mixer_kernel(experts, capacity, ids_hbm, weight_hbm, high_ref, low_ref, ids_ref, weight_ref, sem_ref):
    for copy in fetch(sem_ref, [(ids_hbm, ids_ref), (weight_hbm, weight_ref)]):
        copy.wait()
    first, chosen = selection(ids_ref[...], lax.axis_index("expert"), experts, capacity)
    weight = weight_ref[...]
    mix = jnp.where(chosen, jnp.where(first, weight[0:1, :], weight[1:2, :]), 0.0)
    high = mix.astype(jnp.bfloat16)
    low = (mix - high.astype(jnp.float32)).astype(jnp.bfloat16)
    tokens = mix.shape[1]
    down = lax.broadcasted_iota(jnp.int32, (tokens, tokens), 0)
    across = lax.broadcasted_iota(jnp.int32, (tokens, tokens), 1)
    same = jnp.where(down == across, 1.0, 0.0).astype(jnp.bfloat16)
    high_ref[...] = contract_last(same, high).astype(jnp.bfloat16)
    low_ref[...] = contract_last(same, low).astype(jnp.bfloat16)


def mixer(ids, weight, experts, capacity):
    tokens = ids.shape[1]
    return pl.pallas_call(
        functools.partial(mixer_kernel, experts, capacity),
        out_shape=[jax.ShapeDtypeStruct((tokens, experts * capacity), jnp.bfloat16)] * 2,
        in_specs=[pl.BlockSpec(memory_space=pltpu.HBM)] * 2,
        out_specs=whole(2),
        scratch_shapes=[
            VM(ids.shape, jnp.int32),
            VM(weight.shape, jnp.float32),
            pltpu.SemaphoreType.DMA((2,)),
        ],
        compiler_params=params(8),
        cost_estimate=pl.CostEstimate(
            flops=10_000_000_000, bytes_accessed=0, transcendentals=0
        ),
        name="mixer",
    )(ids, weight)


def owner(pick):
    across, even, odd = pick
    me = lax.axis_index("tensor")
    mask = jnp.where(me % 2 == 0, even, odd)
    return me ^ (mask ^ across)


def part(ref, pick, width):
    return ref[0, :, pl.ds(pl.multiple_of(owner(pick) * width, 128), width)]


def gate_up_kernel(picks, fresh, final, gate_ref, up_ref, *refs):
    count = len(picks) - final
    if final:
        down_ref, refs = refs[0], refs[1:]
    xs, refs = refs[:count], refs[count:]
    width = xs[0].shape[1]
    gate, up = (None, None) if fresh else (refs[0][...], refs[1][...])
    for i in range(count):
        x = xs[i][...]
        g = contract_last(x, part(gate_ref, picks[i], width))
        u = contract_last(x, part(up_ref, picks[i], width))
        gate = g if gate is None else gate + g
        up = u if up is None else up + u
    if final:
        hidden = (gate / (1.0 + jnp.exp(-gate)) * up).astype(jnp.bfloat16)
        refs[-2][...] = hidden
        refs[-1][...] = jnp.dot(
            hidden, part(down_ref, picks[count], width), preferred_element_type=jnp.float32
        ).astype(jnp.bfloat16)
    else:
        refs[-2][...] = gate
        refs[-1][...] = up


def gate_up(pieces, picks, w_gate, w_up, sums, w_down=None):
    final = w_down is not None
    rows, width = pieces[0].shape
    hid = w_gate.shape[1]
    count = len(pieces)
    fresh = sums is None
    held = [] if fresh else list(sums)
    if final:
        outs = [
            jax.ShapeDtypeStruct((rows, hid), jnp.bfloat16),
            jax.ShapeDtypeStruct((rows, width), jnp.bfloat16),
        ]
    else:
        outs = [jax.ShapeDtypeStruct((rows, hid), jnp.float32)] * 2
    extra = [w_down] if final else []
    return pl.pallas_call(
        functools.partial(gate_up_kernel, picks, fresh, final),
        out_shape=outs,
        in_specs=whole(2 + len(extra) + count + len(held)),
        out_specs=whole(len(outs)),
        compiler_params=params(16),
        cost_estimate=pl.CostEstimate(
            flops=4 * rows * width * hid * count,
            bytes_accessed=4 * hid * width * count,
            transcendentals=0,
        ),
        name="gate_up",
    )(w_gate, w_up, *extra, *pieces, *held)


def down_kernel(picks, down_ref, hidden_ref, *out_refs):
    hidden = hidden_ref[...]
    width = out_refs[0].shape[1]
    for i, pick in enumerate(picks):
        value = jnp.dot(
            hidden, part(down_ref, pick, width), preferred_element_type=jnp.float32
        )
        out_refs[i][...] = value.astype(out_refs[i].dtype)


def down(hidden, picks, w_down, width, kinds):
    rows, hid = hidden.shape
    count = len(kinds)
    return pl.pallas_call(
        functools.partial(down_kernel, picks),
        out_shape=[jax.ShapeDtypeStruct((rows, width), kind) for kind in kinds],
        in_specs=whole(2),
        out_specs=whole(count),
        compiler_params=params(16),
        cost_estimate=pl.CostEstimate(
            flops=2 * rows * width * hid * count,
            bytes_accessed=2 * hid * width * count,
            transcendentals=0,
        ),
        name="down",
    )(w_down, hidden)


def combine_kernel(high_ref, low_ref, *refs):
    out_ref = refs[-1]
    rows = jnp.concatenate([block[...] for block in refs[:-1]], axis=0)
    total = jnp.dot(high_ref[...], rows, preferred_element_type=jnp.float32)
    total += jnp.dot(low_ref[...], rows, preferred_element_type=jnp.float32)
    out_ref[...] = total.astype(out_ref.dtype)


def combine(high, low, blocks):
    return pl.pallas_call(
        combine_kernel,
        out_shape=jax.ShapeDtypeStruct((high.shape[0], blocks[0].shape[1]), jnp.bfloat16),
        in_specs=whole(len(blocks) + 2),
        out_specs=pl.BlockSpec(memory_space=VM),
        compiler_params=params(8),
        name="combine",
    )(high, low, *blocks)


def slots_of(tokens, experts):
    return min(tokens, 8 * tokens // (3 * experts))


def stage_bits(tensor, core):
    bits = list(range(1, tensor.bit_length() - 1))
    return bits if core == 0 else bits[::-1]


def shards(tensor, stashed, expert_ids, combine_weight, w_gate, w_up, w_down):
    tokens, width = stashed.shape
    experts = lax.axis_size("expert")
    capacity = slots_of(tokens, experts)
    stages = tensor.bit_length() - 2
    subsets = 1 << stages

    def shift(value, by):
        return lax.ppermute(value, "expert", [(i, (i + by) % experts) for i in range(experts)])

    def swap(value):
        return lax.ppermute(value, "tensor", [(i, i ^ 1) for i in range(tensor)])

    def hop(value, stage):
        pairs = [(i, i ^ (1 << stage_bits(tensor, i & 1)[stage])) for i in range(tensor)]
        return lax.ppermute(value, "tensor", pairs)

    def reach(core):
        bits = stage_bits(tensor, core)
        return [sum(1 << bits[s] for s in range(stages) if k >> s & 1) for k in range(subsets)]

    ahead = list(zip(reach(0), reach(1)))
    mine = [(0, a, b) for a, b in ahead]
    theirs = [(1, b, a) for a, b in ahead]

    ids = expert_ids.T
    outgoing = route(stashed, ids, experts, capacity)
    arrived = [outgoing[0]]
    for j in range(1, experts):
        arrived.append(shift(outgoing[j], j))
    high, low = mixer(ids, combine_weight.T, experts, capacity)
    pieces = [jnp.concatenate(arrived, axis=0)]
    for stage in range(stages):
        for k in range(1 << stage):
            pieces.append(hop(pieces[k], stage))
    swapped = []
    for k in range(subsets):
        swapped.append(swap(pieces[k]))

    sums = None
    for k in range(subsets - 1):
        xs, picks = [pieces[k], swapped[k]], [mine[k], theirs[k]]
        sums = gate_up(xs, picks, w_gate, w_up, sums)
    last = subsets - 1
    hidden, first_given = gate_up(
        [pieces[last], swapped[last]],
        [mine[last], theirs[last], theirs[last]],
        w_gate,
        w_up,
        sums,
        w_down,
    )

    half = subsets // 2
    upper, lower = list(range(last, half - 1, -1)), list(range(half - 1, -1, -1))
    given, kept = {last: first_given}, {}
    for give, keep in ((upper[1:], upper), (lower, lower)):
        made = down(
            hidden,
            [theirs[k] for k in give] + [mine[k] for k in keep],
            w_down,
            width,
            [jnp.bfloat16] * len(give) + [jnp.float32] * len(keep),
        )
        given.update(zip(give, made))
        kept.update(zip(keep, made[len(give) :]))
    sums = [None] * subsets
    for k in upper + lower:
        got = swap(given[k])
        sums[k] = kept[k] + got.astype(jnp.float32)
    for stage in reversed(range(stages)):
        for k in reversed(range(1 << stage)):
            got = hop(sums[(1 << stage) + k].astype(jnp.bfloat16), stage)
            sums[k] = sums[k] + got.astype(jnp.float32)
    result = sums[0].astype(jnp.bfloat16)
    parts = [result[j * capacity : (j + 1) * capacity] for j in range(experts)]
    back = [parts[0]]
    for j in range(1, experts):
        back.append(shift(parts[j], -j))
    return combine(high, low, back)


def solution(mesh):
    experts, tensor = mesh.shape["expert"], mesh.shape["tensor"]

    def body(stashed, expert_ids, combine_weight, w_gate, w_up, w_down):
        tokens, width = stashed.shape
        aligned = (
            tensor >= 4
            and tensor & (tensor - 1) == 0
            and width % 128 == 0
            and w_gate.shape[1] % 128 == 0
            and slots_of(tokens, experts) % 16 == 0
        )
        form = functools.partial(shards, tensor) if aligned else shards_plain
        return form(stashed, expert_ids, combine_weight, w_gate, w_up, w_down)

    return jax.shard_map(
        body,
        mesh=mesh,
        in_specs=(
            P("expert", "tensor"),
            P("expert", None),
            P("expert", None),
            P("expert", "tensor", None),
            P("expert", "tensor", None),
            P("expert", "tensor", None),
        ),
        out_specs=P("expert", "tensor"),
        check_vma=False,
    )
```

time: 168 us -> 67.6 us (0.40)
  blocking collectives: 84.8 us -> 0 us
  waiting for transfers between devices: 49.4 us -> 27.5 us
  starting transfers between devices: 0.01 us -> 20.6 us
  matrix products: 15.9 us -> 0 us
  between operations: 13.4 us -> 0.18 us
  Pallas kernels: 0 us -> 10.8 us
  local copies, waits for them, and re-layouts: 1.42 us -> 7.83 us
  other arithmetic: 3.03 us -> 0.38 us
    all_to_all x2 -> x0, blocking collectives: 72.3 us -> none  [the longest x1 53.4 us: shards(): lax.all_to_all(outgoing, 'expert', split_axis=0, concat_axis=0, tiled=True)]
    reduce_scatter x1 -> x0, waiting for transfers between devices: 49.4 us -> none  [shards(): lax.psum_scatter(partial_value, 'tensor', scatter_dimension=1, tiled=True)]
    ppermute x0 -> x20, waiting for transfers between devices: none -> 27.5 us  [the longest x6 19.7 us: hop(): return lax.ppermute(value, 'tensor', pairs)]
    ppermute x0 -> x20, starting transfers between devices: none -> 20.6 us  [the longest x6 10.8 us: shift(): lax.ppermute(value, 'expert', [(i, (i + by) % experts) for i in range(exp...]
    dot_general x4 -> x0, matrix products: 15.9 us -> none  [the longest x1 11.7 us: shards(): result = jnp.dot(hidden, down_w, preferred_element_type=jnp.float32)]
    all_gather x1 -> x0, blocking collectives: 12.5 us -> none  [shards(): gathered = lax.all_gather(stashed, 'tensor', axis=1, tiled=True)]
    pallas_call x0 -> x9, Pallas kernels: none -> 10.8 us  [the longest x4 5.54 us: gate_up(): pl.pallas_call(functools.partial(gate_up_kernel, picks, fresh, final), ou...]
    unnamed x4 -> x15, local copies, waits for them, and re-layouts: 0.78 us -> 7.81 us
  transfers between devices with their start and end apart: 1 -> 20, of which waited for: 1 -> 10; matrix products, arithmetic and copies ran while one was open for 0% -> 2% of each run, Pallas kernels for 0% -> 10%
where the time goes in v2:
time: 67.6 us; the launch traced here: 67.3 us
  waiting for transfers between devices  27.5 us (41%)
  starting transfers between devices  20.6 us (30%)
  Pallas kernels  10.8 us (16%)
  local copies, waits for them, and re-layouts  7.83 us (12%)
    ppermute x6, waiting for transfers between devices, hop(): return lax.ppermute(value, 'tensor', pairs)  19.7 us
    ppermute x6, starting transfers between devices, shift(): lax.ppermute(value, 'expert', [(i, (i + by) % experts) for i in range(exp...  10.8 us
    ppermute x6, starting transfers between devices, hop(): return lax.ppermute(value, 'tensor', pairs)  7.99 us
    unnamed x15, local copies, waits for them, and re-layouts  7.81 us
    ppermute x6, waiting for transfers between devices, shift(): lax.ppermute(value, 'expert', [(i, (i + by) % experts) for i in range(exp...  7.75 us
    pallas_call x4, Pallas kernels, gate_up(): pl.pallas_call(functools.partial(gate_up_kernel, picks, fresh, final), ou...  5.54 us
    pallas_call x2, Pallas kernels, down(): pl.pallas_call(functools.partial(down_kernel, picks), out_shape=[jax.Shap...  2.24 us
    pallas_call x1, Pallas kernels, route(): pl.pallas_call(functools.partial(route_kernel, experts, capacity), out_sh...  1.79 us
  transfers between devices with their start and end apart: 20, of which 10 were waited for; matrix products, arithmetic and copies ran while one was open for 2% of the time, Pallas kernels for 10%

profile of v2, /device:TPU:0, one launch (start us, length us, event | category | flops | bytes accessed | tf_op | source)
XLA Modules:
  0.0 67.3 jit_solution(16775557212359724957)
XLA Ops:
  0.0 1.8 %route.1 = (bf16[64,512]{1,0:T(8,128)(2,1)}, bf16[64,512]{1,0:T(8,128)(2,1)}, bf16[64,512]{1,0:T(8,128)(2,1)}, bf16[64,512]{1,0:T(8,128)(2,1)}) custom-call(s32[2,96]{1,0:T(2,128)} %bitcast.4, bf16[96,512]{1,0:T(8,128)(2,1)} %x_hbm.1), custom_call_target="tpu_custom_call" | custom-call | tf_op jit(solution)/shard_map/route/pallas_call | solution.py:116
  1.8 3.1 %collective-permute-start = (bf16[64,512]{1,0:T(8,128)(2,1)}, bf16[64,512]{1,0:T(8,128)(2,1)S(1)}, u32[]{:S(2)}, u32[]{:S(2)}) collective-permute-start(bf16[64,512]{1,0:T(8,128)(2,1)} %get-tuple-element.29), channel_id=1, source_target_pairs={{0,8},{8,16},{16,24},{24,0},{1,9},{9,17},{17,25},{25,1},{2,10},{10... | collective-permute-start | bytes 196616 | tf_op jit(solution)/shard_map/ppermute | solution.py:296
  4.9 2.6 %collective-permute-start.1 = (bf16[64,512]{1,0:T(8,128)(2,1)}, bf16[64,512]{1,0:T(8,128)(2,1)S(1)}, u32[]{:S(2)}, u32[]{:S(2)}) collective-permute-start(bf16[64,512]{1,0:T(8,128)(2,1)} %get-tuple-element.30), channel_id=1, source_target_pairs={{0,16},{8,24},{16,0},{24,8},{1,17},{9,25},{17,1},{25,9},{2,18},{10... | collective-permute-start | bytes 196616 | tf_op jit(solution)/shard_map/ppermute | solution.py:296
  7.5 1.3 %collective-permute-start.2 = (bf16[64,512]{1,0:T(8,128)(2,1)}, bf16[64,512]{1,0:T(8,128)(2,1)S(1)}, u32[]{:S(2)}, u32[]{:S(2)}) collective-permute-start(bf16[64,512]{1,0:T(8,128)(2,1)} %get-tuple-element.31), channel_id=1, source_target_pairs={{0,24},{8,0},{16,8},{24,16},{1,25},{9,1},{17,9},{25,17},{2,26},{10... | collective-permute-start | bytes 196616 | tf_op jit(solution)/shard_map/ppermute | solution.py:296
  8.8 0.8 %constant_dynamic-update-slice_fusion.3 = bf16[256,512]{1,0:T(8,128)(2,1)S(1)} fusion(bf16[64,512]{1,0:T(8,128)(2,1)} %get-tuple-element.28), kind=kLoop, calls=%fused_computation.7 | loop fusion | bytes 131072
  9.7 2.5 %collective-permute-done.1 = bf16[64,512]{1,0:T(8,128)(2,1)S(1)} collective-permute-done((bf16[64,512]{1,0:T(8,128)(2,1)}, bf16[64,512]{1,0:T(8,128)(2,1)S(1)}, u32[]{:S(2)}, u32[]{:S(2)}) %collective-permute-start.1) | collective-permute-done | bytes 65568 | tf_op jit(solution)/shard_map/ppermute | solution.py:296
  12.4 1.6 %collective-permute-start.3 = (bf16[256,512]{1,0:T(8,128)(2,1)S(1)}, bf16[256,512]{1,0:T(8,128)(2,1)S(1)}, u32[]{:S(2)}, u32[]{:S(2)}) collective-permute-start(bf16[256,512]{1,0:T(8,128)(2,1)S(1)} %constant_dynamic-update-slice_fusion.refs_0_), channel_id=1, source_target_pairs={{0,2},{1,5},{2,0},{3,7},{4,6},{5,1},{6,4},{7,3},{8,10},{9,13},{10,... | collective-permute-start | bytes 786440 | tf_op jit(solution)/shard_map/ppermute | solution.py:303
  14.0 1.5 %collective-permute-start.6 = (bf16[256,512]{1,0:T(8,128)(2,1)S(1)}, bf16[256,512]{1,0:T(8,128)(2,1)S(1)}, u32[]{:S(2)}, u32[]{:S(2)}) collective-permute-start(bf16[256,512]{1,0:T(8,128)(2,1)S(1)} %constant_dynamic-update-slice_fusion.refs_0_), channel_id=1, source_target_pairs={{0,4},{1,3},{2,6},{3,1},{4,0},{5,7},{6,2},{7,5},{8,12},{9,11},{10,... | collective-permute-start | bytes 786440 | tf_op jit(solution)/shard_map/ppermute | solution.py:303
  15.5 6.1 %collective-permute-done.3.refs_0_ = bf16[256,512]{1,0:T(8,128)(2,1)S(1)} collective-permute-done((bf16[256,512]{1,0:T(8,128)(2,1)S(1)}, bf16[256,512]{1,0:T(8,128)(2,1)S(1)}, u32[]{:S(2)}, u32[]{:S(2)}) %collective-permute-start.3) | collective-permute-done | bytes 262176 | tf_op jit(solution)/shard_map/ppermute | solution.py:303
  21.6 1.2 %collective-permute-start.4 = (bf16[256,512]{1,0:T(8,128)(2,1)S(1)}, bf16[256,512]{1,0:T(8,128)(2,1)S(1)}, u32[]{:S(2)}, u32[]{:S(2)}) collective-permute-start(bf16[256,512]{1,0:T(8,128)(2,1)S(1)} %collective-permute-done.3.refs_0_), channel_id=1, source_target_pairs={{0,4},{1,3},{2,6},{3,1},{4,0},{5,7},{6,2},{7,5},{8,12},{9,11},{10,... | collective-permute-start | bytes 786440 | tf_op jit(solution)/shard_map/ppermute | solution.py:303
  23.4 4.6 %collective-permute-done.4.refs_1_ = bf16[256,512]{1,0:T(8,128)(2,1)S(1)} collective-permute-done((bf16[256,512]{1,0:T(8,128)(2,1)S(1)}, bf16[256,512]{1,0:T(8,128)(2,1)S(1)}, u32[]{:S(2)}, u32[]{:S(2)}) %collective-permute-start.4) | collective-permute-done | bytes 262176 | tf_op jit(solution)/shard_map/ppermute | solution.py:303
  28.0 3.1 %copy-done = bf16[1,896,4096]{2,1,0:T(8,128)(2,1)S(1)} copy-done((bf16[1,896,4096]{2,1,0:T(8,128)(2,1)S(1)}, bf16[1,896,4096]{2,1,0:T(8,128)(2,1)}, u32[]{:S(2)}) %copy-start) | copy-done | bytes 7340056
  31.1 3.1 %copy-done.1 = bf16[1,896,4096]{2,1,0:T(8,128)(2,1)S(1)} copy-done((bf16[1,896,4096]{2,1,0:T(8,128)(2,1)S(1)}, bf16[1,896,4096]{2,1,0:T(8,128)(2,1)}, u32[]{:S(2)}) %copy-start.1) | copy-done | bytes 7340056
  34.2 1.3 %gate_up.4 = (f32[256,896]{1,0:T(8,128)S(1)}, f32[256,896]{1,0:T(8,128)S(1)}) custom-call(bf16[1,896,4096]{2,1,0:T(8,128)(2,1)S(1)} %copy-done, bf16[1,896,4096]{2,1,0:T(8,128)(2,1)S(1)} %copy-done.1, bf16[256,512]{1,0:T(8,128)(2,1)S(1)} %constant_dynamic-update-slice_fusion.refs_0_, bf16[256,512]{1,0:T(8,128)(2,1)S(1)} %collective-permute-done.9.refs_1_), custom_call_target="tpu_custom_call" | custom-call | flops 939524096 | bytes 3670016 | tf_op jit(solution)/shard_map/gate_up/pallas_call | solution.py:217
  35.5 1.3 %gate_up.5 = (f32[256,896]{1,0:T(8,128)S(1)}, f32[256,896]{1,0:T(8,128)S(1)}) custom-call(bf16[1,896,4096]{2,1,0:T(8,128)(2,1)S(1)} %copy-done, bf16[1,896,4096]{2,1,0:T(8,128)(2,1)S(1)} %copy-done.1, bf16[256,512]{1,0:T(8,128)(2,1)S(1)} %collective-permute-done.3.refs_0_, bf16[256,512]{1,0:T(8,128)(2,1)S(1)} %collective-permute-done.8.refs_1_, ...), custom_call_target="tpu_custom_call" | custom-call | flops 939524096 | bytes 3670016 | tf_op jit(solution)/shard_map/gate_up/pallas_call | solution.py:217
  36.8 1.3 %gate_up.6 = (f32[256,896]{1,0:T(8,128)S(1)}, f32[256,896]{1,0:T(8,128)S(1)}) custom-call(bf16[1,896,4096]{2,1,0:T(8,128)(2,1)S(1)} %copy-done, bf16[1,896,4096]{2,1,0:T(8,128)(2,1)S(1)} %copy-done.1, bf16[256,512]{1,0:T(8,128)(2,1)S(1)} %collective-permute-done.6.refs_0_, bf16[256,512]{1,0:T(8,128)(2,1)S(1)} %collective-permute-done.7.refs_1_, ...), custom_call_target="tpu_custom_call" | custom-call | flops 939524096 | bytes 3670016 | tf_op jit(solution)/shard_map/gate_up/pallas_call | solution.py:217
  38.1 0.8 %slice-done.1 = s8[3145728]{0:T(1024)(128)(4,1)S(1)} async-done(((s8[7340032]{0:T(1024)(128)(4,1)}), s8[3145728]{0:T(1024)(128)(4,1)S(1)}, s32[]{:S(2)}) %slice-start.1) | async-done | bytes 3145752
  38.9 1.7 %gate_up.7 = (bf16[256,896]{1,0:T(8,128)(2,1)S(1)}, bf16[256,512]{1,0:T(8,128)(2,1)S(1)}) custom-call(bf16[1,896,4096]{2,1,0:T(8,128)(2,1)S(1)} %copy-done, bf16[1,896,4096]{2,1,0:T(8,128)(2,1)S(1)} %copy-done.1, bf16[1,896,4096]{2,1,0:T(8,128)(2,1)S(1)} %bitcast.3, bf16[256,512]{1,0:T(8,128)(2,1)S(1)} %collective-permute-done.4.refs_1_, ...), custom_call_target="tpu_custom_call" | custom-call | flops 939524096 | bytes 3670016 | tf_op jit(solution)/shard_map/gate_up/pallas_call | solution.py:217
  41.1 1.0 %down.3 = (bf16[256,512]{1,0:T(8,128)(2,1)S(1)}, f32[256,512]{1,0:T(8,128)S(1)}, f32[256,512]{1,0:T(8,128)S(1)}) custom-call(bf16[1,896,4096]{2,1,0:T(8,128)(2,1)S(1)} %bitcast.3, bf16[256,896]{1,0:T(8,128)(2,1)S(1)} %get-tuple-element.38.hidden_ref), custom_call_target="tpu_custom_call" | custom-call | flops 704643072 | bytes 2752512 | tf_op jit(solution)/shard_map/down/pallas_call | solution.py:245
  42.2 1.3 %down.2 = (bf16[256,512]{1,0:T(8,128)(2,1)S(1)}, bf16[256,512]{1,0:T(8,128)(2,1)S(1)}, f32[256,512]{1,0:T(8,128)S(1)}, f32[256,512]{1,0:T(8,128)S(1)}) custom-call(bf16[1,896,4096]{2,1,0:T(8,128)(2,1)S(1)} %bitcast.3, bf16[256,896]{1,0:T(8,128)(2,1)S(1)} %get-tuple-element.38.hidden_ref), custom_call_target="tpu_custom_call" | custom-call | flops 939524096 | bytes 3670016 | tf_op jit(solution)/shard_map/down/pallas_call | solution.py:245
  44.1 1.3 %collective-permute-start.15 = (bf16[256,512]{1,0:T(8,128)(2,1)S(1)}, bf16[256,512]{1,0:T(8,128)(2,1)S(1)}, u32[]{:S(2)}, u32[]{:S(2)}) collective-permute-start(bf16[256,512]{1,0:T(8,128)(2,1)S(1)} %add_convert_fusion.2), channel_id=1, source_target_pairs={{0,4},{1,3},{2,6},{3,1},{4,0},{5,7},{6,2},{7,5},{8,12},{9,11},{10,... | collective-permute-start | bytes 786440 | tf_op jit(solution)/shard_map/ppermute | solution.py:303
  45.6 0.7 %collective-permute-start.12 = (bf16[256,512]{1,0:T(8,128)(2,1)S(1)}, bf16[256,512]{1,0:T(8,128)(2,1)S(1)}, u32[]{:S(2)}, u32[]{:S(2)}) collective-permute-start(bf16[256,512]{1,0:T(8,128)(2,1)S(1)} %add_convert_fusion.3), channel_id=1, source_target_pairs={{0,4},{1,3},{2,6},{3,1},{4,0},{5,7},{6,2},{7,5},{8,12},{9,11},{10,... | collective-permute-start | bytes 786440 | tf_op jit(solution)/shard_map/ppermute | solution.py:303
  46.3 4.2 %collective-permute-done.15 = bf16[256,512]{1,0:T(8,128)(2,1)S(1)} collective-permute-done((bf16[256,512]{1,0:T(8,128)(2,1)S(1)}, bf16[256,512]{1,0:T(8,128)(2,1)S(1)}, u32[]{:S(2)}, u32[]{:S(2)}) %collective-permute-start.15) | collective-permute-done | bytes 262176 | tf_op jit(solution)/shard_map/ppermute | solution.py:303
  50.6 1.6 %collective-permute-start.16 = (bf16[256,512]{1,0:T(8,128)(2,1)S(1)}, bf16[256,512]{1,0:T(8,128)(2,1)S(1)}, u32[]{:S(2)}, u32[]{:S(2)}) collective-permute-start(bf16[256,512]{1,0:T(8,128)(2,1)S(1)} %add_convert_fusion.1), channel_id=1, source_target_pairs={{0,2},{1,5},{2,0},{3,7},{4,6},{5,1},{6,4},{7,3},{8,10},{9,13},{10,... | collective-permute-start | bytes 786440 | tf_op jit(solution)/shard_map/ppermute | solution.py:303
  52.2 1.9 %collective-permute-done.12 = bf16[256,512]{1,0:T(8,128)(2,1)S(1)} collective-permute-done((bf16[256,512]{1,0:T(8,128)(2,1)S(1)}, bf16[256,512]{1,0:T(8,128)(2,1)S(1)}, u32[]{:S(2)}, u32[]{:S(2)}) %collective-permute-start.12) | collective-permute-done | bytes 262176 | tf_op jit(solution)/shard_map/ppermute | solution.py:303
  54.1 2.9 %collective-permute-done.16 = bf16[256,512]{1,0:T(8,128)(2,1)S(1)} collective-permute-done((bf16[256,512]{1,0:T(8,128)(2,1)S(1)}, bf16[256,512]{1,0:T(8,128)(2,1)S(1)}, u32[]{:S(2)}, u32[]{:S(2)}) %collective-permute-start.16) | collective-permute-done | bytes 262176 | tf_op jit(solution)/shard_map/ppermute | solution.py:303
  57.2 3.1 %collective-permute-start.17 = (bf16[64,512]{1,0:T(8,128)(2,1)S(1)}, bf16[64,512]{1,0:T(8,128)(2,1)S(1)}, u32[]{:S(2)}, u32[]{:S(2)}) collective-permute-start(bf16[64,512]{1,0:T(8,128)(2,1)S(1)} %get-tuple-element.49), channel_id=1, source_target_pairs={{0,24},{8,0},{16,8},{24,16},{1,25},{9,1},{17,9},{25,17},{2,26},{10... | collective-permute-start | bytes 196616 | tf_op jit(solution)/shard_map/ppermute | solution.py:296
  60.4 0.6 collective-permute-start.19
  61.4 1.1 %collective-permute-done.17.refs_1_ = bf16[64,512]{1,0:T(8,128)(2,1)S(1)} collective-permute-done((bf16[64,512]{1,0:T(8,128)(2,1)S(1)}, bf16[64,512]{1,0:T(8,128)(2,1)S(1)}, u32[]{:S(2)}, u32[]{:S(2)}) %collective-permute-start.17) | collective-permute-done | bytes 65568 | tf_op jit(solution)/shard_map/ppermute | solution.py:296
  62.5 3.1 %collective-permute-done.18.refs_2_ = bf16[64,512]{1,0:T(8,128)(2,1)S(1)} collective-permute-done((bf16[64,512]{1,0:T(8,128)(2,1)S(1)}, bf16[64,512]{1,0:T(8,128)(2,1)S(1)}, u32[]{:S(2)}, u32[]{:S(2)}) %collective-permute-start.18) | collective-permute-done | bytes 65568 | tf_op jit(solution)/shard_map/ppermute | solution.py:296
  65.6 0.9 %collective-permute-done.19.refs_3_ = bf16[64,512]{1,0:T(8,128)(2,1)S(1)} collective-permute-done((bf16[64,512]{1,0:T(8,128)(2,1)S(1)}, bf16[64,512]{1,0:T(8,128)(2,1)S(1)}, u32[]{:S(2)}, u32[]{:S(2)}) %collective-permute-start.19) | collective-permute-done | bytes 65568 | tf_op jit(solution)/shard_map/ppermute | solution.py:296
  66.4 0.9 %combine.1 = bf16[96,512]{1,0:T(8,128)(2,1)} custom-call(bf16[96,256]{1,0:T(8,128)(2,1)S(1)} %get-tuple-element.26.high_ref, bf16[96,256]{1,0:T(8,128)(2,1)S(1)} %get-tuple-element.27.low_ref, bf16[64,512]{1,0:T(8,128)(2,1)S(1)} %get-tuple-element.50.refs_0_, bf16[64,512]{1,0:T(8,128)(2,1)S(1)} %collective-permute-done.17.refs_1_, ...), custom_call_target="tpu_custom_call" | custom-call | tf_op jit(solution)/shard_map/combine/pallas_call | solution.py:269
  (39 shorter events, 2.9 us)
Async XLA Ops:
  1.8 7.9 %collective-permute-start = (bf16[64,512]{1,0:T(8,128)(2,1)}, bf16[64,512]{1,0:T(8,128)(2,1)S(1)}, u32[]{:S(2)}, u32[]{:S(2)}) collective-permute-start(bf16[64,512]{1,0:T(8,128)(2,1)} %get-tuple-element.29), channel_id=1, source_target_pairs={{0,8},{8,16},{16,24},{24,0},{1,9},{9,17},{17,25},{25,1},{2,10},{10... | collective-permute-start | bytes 196616 | tf_op jit(solution)/shard_map/ppermute | solution.py:296
  4.9 7.3 %collective-permute-start.1 = (bf16[64,512]{1,0:T(8,128)(2,1)}, bf16[64,512]{1,0:T(8,128)(2,1)S(1)}, u32[]{:S(2)}, u32[]{:S(2)}) collective-permute-start(bf16[64,512]{1,0:T(8,128)(2,1)} %get-tuple-element.30), channel_id=1, source_target_pairs={{0,16},{8,24},{16,0},{24,8},{1,17},{9,25},{17,1},{25,9},{2,18},{10... | collective-permute-start | bytes 196616 | tf_op jit(solution)/shard_map/ppermute | solution.py:296
  7.5 4.9 %collective-permute-start.2 = (bf16[64,512]{1,0:T(8,128)(2,1)}, bf16[64,512]{1,0:T(8,128)(2,1)S(1)}, u32[]{:S(2)}, u32[]{:S(2)}) collective-permute-start(bf16[64,512]{1,0:T(8,128)(2,1)} %get-tuple-element.31), channel_id=1, source_target_pairs={{0,24},{8,0},{16,8},{24,16},{1,25},{9,1},{17,9},{25,17},{2,26},{10... | collective-permute-start | bytes 196616 | tf_op jit(solution)/shard_map/ppermute | solution.py:296
  12.4 9.2 %collective-permute-start.3 = (bf16[256,512]{1,0:T(8,128)(2,1)S(1)}, bf16[256,512]{1,0:T(8,128)(2,1)S(1)}, u32[]{:S(2)}, u32[]{:S(2)}) collective-permute-start(bf16[256,512]{1,0:T(8,128)(2,1)S(1)} %constant_dynamic-update-slice_fusion.refs_0_), channel_id=1, source_target_pairs={{0,2},{1,5},{2,0},{3,7},{4,6},{5,1},{6,4},{7,3},{8,10},{9,13},{10,... | collective-permute-start | bytes 786440 | tf_op jit(solution)/shard_map/ppermute | solution.py:303
  14.0 9.4 %collective-permute-start.6 = (bf16[256,512]{1,0:T(8,128)(2,1)S(1)}, bf16[256,512]{1,0:T(8,128)(2,1)S(1)}, u32[]{:S(2)}, u32[]{:S(2)}) collective-permute-start(bf16[256,512]{1,0:T(8,128)(2,1)S(1)} %constant_dynamic-update-slice_fusion.refs_0_), channel_id=1, source_target_pairs={{0,4},{1,3},{2,6},{3,1},{4,0},{5,7},{6,2},{7,5},{8,12},{9,11},{10,... | collective-permute-start | bytes 786440 | tf_op jit(solution)/shard_map/ppermute | solution.py:303
  21.6 6.4 %collective-permute-start.4 = (bf16[256,512]{1,0:T(8,128)(2,1)S(1)}, bf16[256,512]{1,0:T(8,128)(2,1)S(1)}, u32[]{:S(2)}, u32[]{:S(2)}) collective-permute-start(bf16[256,512]{1,0:T(8,128)(2,1)S(1)} %collective-permute-done.3.refs_0_), channel_id=1, source_target_pairs={{0,4},{1,3},{2,6},{3,1},{4,0},{5,7},{6,2},{7,5},{8,12},{9,11},{10,... | collective-permute-start | bytes 786440 | tf_op jit(solution)/shard_map/ppermute | solution.py:303
  22.8 5.1 %collective-permute-start.9 = (bf16[256,512]{1,0:T(8,128)(2,1)S(1)}, bf16[256,512]{1,0:T(8,128)(2,1)S(1)}, u32[]{:S(2)}, u32[]{:S(2)}) collective-permute-start(bf16[256,512]{1,0:T(8,128)(2,1)S(1)} %constant_dynamic-update-slice_fusion.refs_0_), channel_id=1, source_target_pairs={{0,1},{1,0},{2,3},{3,2},{4,5},{5,4},{6,7},{7,6},{8,9},{9,8},{10,11... | collective-permute-start | bytes 786440 | tf_op jit(solution)/shard_map/ppermute | solution.py:299
  22.8 12.6 %collective-permute-start.8 = (bf16[256,512]{1,0:T(8,128)(2,1)S(1)}, bf16[256,512]{1,0:T(8,128)(2,1)S(1)}, u32[]{:S(2)}, u32[]{:S(2)}) collective-permute-start(bf16[256,512]{1,0:T(8,128)(2,1)S(1)} %collective-permute-done.3.refs_0_), channel_id=1, source_target_pairs={{0,1},{1,0},{2,3},{3,2},{4,5},{5,4},{6,7},{7,6},{8,9},{9,8},{10,11... | collective-permute-start | bytes 786440 | tf_op jit(solution)/shard_map/ppermute | solution.py:299
  23.4 13.4 %collective-permute-start.7 = (bf16[256,512]{1,0:T(8,128)(2,1)S(1)}, bf16[256,512]{1,0:T(8,128)(2,1)S(1)}, u32[]{:S(2)}, u32[]{:S(2)}) collective-permute-start(bf16[256,512]{1,0:T(8,128)(2,1)S(1)} %collective-permute-done.6.refs_0_), channel_id=1, source_target_pairs={{0,1},{1,0},{2,3},{3,2},{4,5},{5,4},{6,7},{7,6},{8,9},{9,8},{10,11... | collective-permute-start | bytes 786440 | tf_op jit(solution)/shard_map/ppermute | solution.py:299
  28.0 10.1 %collective-permute-start.5 = (bf16[256,512]{1,0:T(8,128)(2,1)S(1)}, bf16[256,512]{1,0:T(8,128)(2,1)S(1)}, u32[]{:S(2)}, u32[]{:S(2)}) collective-permute-start(bf16[256,512]{1,0:T(8,128)(2,1)S(1)} %collective-permute-done.4.refs_1_), channel_id=1, source_target_pairs={{0,1},{1,0},{2,3},{3,2},{4,5},{5,4},{6,7},{7,6},{8,9},{9,8},{10,11... | collective-permute-start | bytes 786440 | tf_op jit(solution)/shard_map/ppermute | solution.py:299
  28.0 3.1 %copy-start = (bf16[1,896,4096]{2,1,0:T(8,128)(2,1)S(1)}, bf16[1,896,4096]{2,1,0:T(8,128)(2,1)}, u32[]{:S(2)}) copy-start(bf16[1,896,4096]{2,1,0:T(8,128)(2,1)} %gate_ref.7) | copy-start | bytes 22020100
  31.1 3.1 %copy-start.1 = (bf16[1,896,4096]{2,1,0:T(8,128)(2,1)S(1)}, bf16[1,896,4096]{2,1,0:T(8,128)(2,1)}, u32[]{:S(2)}) copy-start(bf16[1,896,4096]{2,1,0:T(8,128)(2,1)} %up_ref.7) | copy-start | bytes 22020100
  35.4 2.7 %slice-start = ((s8[7340032]{0:T(1024)(128)(4,1)}), s8[4194304]{0:T(1024)(128)(4,1)S(1)}, s32[]{:S(2)}) async-start(s8[7340032]{0:T(1024)(128)(4,1)} %bitcast.2), calls=%async_computation | async-start | bytes 8388608
  36.8 2.1 %slice-start.1 = ((s8[7340032]{0:T(1024)(128)(4,1)}), s8[3145728]{0:T(1024)(128)(4,1)S(1)}, s32[]{:S(2)}) async-start(s8[7340032]{0:T(1024)(128)(4,1)} %bitcast.2), calls=%async_computation.1 | async-start | bytes 6291456
  40.6 3.4 %collective-permute-start.14 = (bf16[256,512]{1,0:T(8,128)(2,1)S(1)}, bf16[256,512]{1,0:T(8,128)(2,1)S(1)}, u32[]{:S(2)}, u32[]{:S(2)}) collective-permute-start(bf16[256,512]{1,0:T(8,128)(2,1)S(1)} %get-tuple-element.46), channel_id=1, source_target_pairs={{0,1},{1,0},{2,3},{3,2},{4,5},{5,4},{6,7},{7,6},{8,9},{9,8},{10,11... | collective-permute-start | bytes 786440 | tf_op jit(solution)/shard_map/ppermute | solution.py:299
  42.1 18.9 %copy-start.2 = (s32[96,2]{0,1:T(2,128)S(1)}, s32[96,2]{0,1:T(2,128)}, u32[]{:S(2)}) copy-start(s32[96,2]{0,1:T(2,128)} %param.7) | copy-start | bytes 2308
  42.1 18.9 %copy-start.3 = (f32[96,2]{0,1:T(2,128)S(1)}, f32[96,2]{0,1:T(2,128)}, u32[]{:S(2)}) copy-start(f32[96,2]{0,1:T(2,128)} %param.8) | copy-start | bytes 2308
  42.1 3.4 %collective-permute-start.11 = (bf16[256,512]{1,0:T(8,128)(2,1)S(1)}, bf16[256,512]{1,0:T(8,128)(2,1)S(1)}, u32[]{:S(2)}, u32[]{:S(2)}) collective-permute-start(bf16[256,512]{1,0:T(8,128)(2,1)S(1)} %get-tuple-element.42), channel_id=1, source_target_pairs={{0,1},{1,0},{2,3},{3,2},{4,5},{5,4},{6,7},{7,6},{8,9},{9,8},{10,11... | collective-permute-start | bytes 786440 | tf_op jit(solution)/shard_map/ppermute | solution.py:299
  43.5 2.8 %collective-permute-start.13 = (bf16[256,512]{1,0:T(8,128)(2,1)S(1)}, bf16[256,512]{1,0:T(8,128)(2,1)S(1)}, u32[]{:S(2)}, u32[]{:S(2)}) collective-permute-start(bf16[256,512]{1,0:T(8,128)(2,1)S(1)} %get-tuple-element.44), channel_id=1, source_target_pairs={{0,1},{1,0},{2,3},{3,2},{4,5},{5,4},{6,7},{7,6},{8,9},{9,8},{10,11... | collective-permute-start | bytes 786440 | tf_op jit(solution)/shard_map/ppermute | solution.py:299
  44.1 6.4 %collective-permute-start.15 = (bf16[256,512]{1,0:T(8,128)(2,1)S(1)}, bf16[256,512]{1,0:T(8,128)(2,1)S(1)}, u32[]{:S(2)}, u32[]{:S(2)}) collective-permute-start(bf16[256,512]{1,0:T(8,128)(2,1)S(1)} %add_convert_fusion.2), channel_id=1, source_target_pairs={{0,4},{1,3},{2,6},{3,1},{4,0},{5,7},{6,2},{7,5},{8,12},{9,11},{10,... | collective-permute-start | bytes 786440 | tf_op jit(solution)/shard_map/ppermute | solution.py:303
  45.4 6.9 %collective-permute-start.10 = (bf16[256,512]{1,0:T(8,128)(2,1)S(1)}, bf16[256,512]{1,0:T(8,128)(2,1)S(1)}, u32[]{:S(2)}, u32[]{:S(2)}) collective-permute-start(bf16[256,512]{1,0:T(8,128)(2,1)S(1)} %get-tuple-element.40), channel_id=1, source_target_pairs={{0,1},{1,0},{2,3},{3,2},{4,5},{5,4},{6,7},{7,6},{8,9},{9,8},{10,11... | collective-permute-start | bytes 786440 | tf_op jit(solution)/shard_map/ppermute | solution.py:299
  45.6 8.6 %collective-permute-start.12 = (bf16[256,512]{1,0:T(8,128)(2,1)S(1)}, bf16[256,512]{1,0:T(8,128)(2,1)S(1)}, u32[]{:S(2)}, u32[]{:S(2)}) collective-permute-start(bf16[256,512]{1,0:T(8,128)(2,1)S(1)} %add_convert_fusion.3), channel_id=1, source_target_pairs={{0,4},{1,3},{2,6},{3,1},{4,0},{5,7},{6,2},{7,5},{8,12},{9,11},{10,... | collective-permute-start | bytes 786440 | tf_op jit(solution)/shard_map/ppermute | solution.py:303
  50.6 6.4 %collective-permute-start.16 = (bf16[256,512]{1,0:T(8,128)(2,1)S(1)}, bf16[256,512]{1,0:T(8,128)(2,1)S(1)}, u32[]{:S(2)}, u32[]{:S(2)}) collective-permute-start(bf16[256,512]{1,0:T(8,128)(2,1)S(1)} %add_convert_fusion.1), channel_id=1, source_target_pairs={{0,2},{1,5},{2,0},{3,7},{4,6},{5,1},{6,4},{7,3},{8,10},{9,13},{10,... | collective-permute-start | bytes 786440 | tf_op jit(solution)/shard_map/ppermute | solution.py:303
  57.2 5.2 %collective-permute-start.17 = (bf16[64,512]{1,0:T(8,128)(2,1)S(1)}, bf16[64,512]{1,0:T(8,128)(2,1)S(1)}, u32[]{:S(2)}, u32[]{:S(2)}) collective-permute-start(bf16[64,512]{1,0:T(8,128)(2,1)S(1)} %get-tuple-element.49), channel_id=1, source_target_pairs={{0,24},{8,0},{16,8},{24,16},{1,25},{9,1},{17,9},{25,17},{2,26},{10... | collective-permute-start | bytes 196616 | tf_op jit(solution)/shard_map/ppermute | solution.py:296
  60.3 5.2 %collective-permute-start.18 = (bf16[64,512]{1,0:T(8,128)(2,1)S(1)}, bf16[64,512]{1,0:T(8,128)(2,1)S(1)}, u32[]{:S(2)}, u32[]{:S(2)}) collective-permute-start(bf16[64,512]{1,0:T(8,128)(2,1)S(1)} %get-tuple-element.48), channel_id=1, source_target_pairs={{0,16},{8,24},{16,0},{24,8},{1,17},{9,25},{17,1},{25,9},{2,18},{10... | collective-permute-start | bytes 196616 | tf_op jit(solution)/shard_map/ppermute | solution.py:296
  60.4 6.1 %collective-permute-start.19 = (bf16[64,512]{1,0:T(8,128)(2,1)S(1)}, bf16[64,512]{1,0:T(8,128)(2,1)S(1)}, u32[]{:S(2)}, u32[]{:S(2)}) collective-permute-start(bf16[64,512]{1,0:T(8,128)(2,1)S(1)} %get-tuple-element.47), channel_id=1, source_target_pairs={{0,8},{8,16},{16,24},{24,0},{1,9},{9,17},{17,25},{25,1},{2,10},{10... | collective-permute-start | bytes 196616 | tf_op jit(solution)/shard_map/ppermute | solution.py:296

commit v3 on v2

--- a/solution.py
+++ b/solution.py
@@ -82,8 +82,7 @@
     tokens = ids.shape[1]
     rows = experts * capacity
     row = lax.broadcasted_iota(jnp.int32, (rows, tokens), 0)
-    expert = first_expert + row // capacity
-    expert = jnp.where(expert >= experts, expert - experts, expert)
+    expert = first_expert ^ (row // capacity)
     slot = row % capacity
     first = ids[0:1, :] == expert
     named = jnp.logical_or(first, ids[1:2, :] == expert)
@@ -123,7 +122,7 @@
             VM(stashed.shape, jnp.bfloat16),
             pltpu.SemaphoreType.DMA((2,)),
         ],
-        compiler_params=params(56),
+        compiler_params=pltpu.CompilerParams(vmem_limit_bytes=66743328),
         name="route",
     )(ids, stashed)
 
@@ -175,49 +174,59 @@
     return ref[0, :, pl.ds(pl.multiple_of(owner(pick) * width, 128), width)]
 
 
-def gate_up_kernel(picks, fresh, final, gate_ref, up_ref, *refs):
-    count = len(picks) - final
+def stacked(halves, index):
+    return jnp.concatenate([half[index] for half in halves], axis=0)
+
+
+def gate_up_kernel(picks, give, fresh, gate_ref, up_ref, *refs):
+    final = len(give) > 0
     if final:
         down_ref, refs = refs[0], refs[1:]
-    xs, refs = refs[:count], refs[count:]
-    width = xs[0].shape[1]
+    halves, refs = refs[:2], refs[2:]
+    width = halves[0].shape[2]
     gate, up = (None, None) if fresh else (refs[0][...], refs[1][...])
-    for i in range(count):
-        x = xs[i][...]
-        g = contract_last(x, part(gate_ref, picks[i], width))
-        u = contract_last(x, part(up_ref, picks[i], width))
+    for i, pick in enumerate(picks):
+        x = stacked(halves, i)
+        g = contract_last(x, part(gate_ref, pick, width))
+        u = contract_last(x, part(up_ref, pick, width))
         gate = g if gate is None else gate + g
         up = u if up is None else up + u
-    if final:
-        hidden = (gate / (1.0 + jnp.exp(-gate)) * up).astype(jnp.bfloat16)
-        refs[-2][...] = hidden
-        refs[-1][...] = jnp.dot(
-            hidden, part(down_ref, picks[count], width), preferred_element_type=jnp.float32
-        ).astype(jnp.bfloat16)
-    else:
+    if not final:
         refs[-2][...] = gate
         refs[-1][...] = up
-
-
-def gate_up(pieces, picks, w_gate, w_up, sums, w_down=None):
-    final = w_down is not None
-    rows, width = pieces[0].shape
+        return
+    hidden = (gate / (1.0 + jnp.exp(-gate)) * up).astype(jnp.bfloat16)
+    refs[-3][...] = hidden
+    split(hidden, give, down_ref, refs[-2:])
+
+
+def split(hidden, picks, down_ref, outs):
+    _, rows, width = outs[0].shape
+    for i, pick in enumerate(picks):
+        value = jnp.dot(
+            hidden, part(down_ref, pick, width), preferred_element_type=jnp.float32
+        ).astype(outs[0].dtype)
+        outs[0][i] = value[:rows]
+        outs[1][i] = value[rows:]
+
+
+def gate_up(halves, picks, w_gate, w_up, sums, w_down=None, give=()):
+    _, rows, width = halves[0].shape
     hid = w_gate.shape[1]
-    count = len(pieces)
+    rows = 2 * rows
+    count = len(picks)
     fresh = sums is None
     held = [] if fresh else list(sums)
-    if final:
-        outs = [
-            jax.ShapeDtypeStruct((rows, hid), jnp.bfloat16),
-            jax.ShapeDtypeStruct((rows, width), jnp.bfloat16),
-        ]
+    if give:
+        outs = [jax.ShapeDtypeStruct((rows, hid), jnp.bfloat16)]
+        outs += [jax.ShapeDtypeStruct((len(give), rows // 2, width), jnp.bfloat16)] * 2
     else:
         outs = [jax.ShapeDtypeStruct((rows, hid), jnp.float32)] * 2
-    extra = [w_down] if final else []
+    extra = [w_down] if give else []
     return pl.pallas_call(
-        functools.partial(gate_up_kernel, picks, fresh, final),
+        functools.partial(gate_up_kernel, picks, give, fresh),
         out_shape=outs,
-        in_specs=whole(2 + len(extra) + count + len(held)),
+        in_specs=whole(4 + len(extra) + len(held)),
         out_specs=whole(len(outs)),
         compiler_params=params(16),
         cost_estimate=pl.CostEstimate(
@@ -226,27 +235,28 @@
             transcendentals=0,
         ),
         name="gate_up",
-    )(w_gate, w_up, *extra, *pieces, *held)
-
-
-def down_kernel(picks, down_ref, hidden_ref, *out_refs):
+    )(w_gate, w_up, *extra, *halves, *held)
+
+
+def down_kernel(give, keep, down_ref, hidden_ref, *outs):
     hidden = hidden_ref[...]
-    width = out_refs[0].shape[1]
-    for i, pick in enumerate(picks):
-        value = jnp.dot(
-            hidden, part(down_ref, pick, width), preferred_element_type=jnp.float32
-        )
-        out_refs[i][...] = value.astype(out_refs[i].dtype)
-
-
-def down(hidden, picks, w_down, width, kinds):
+    if give:
+        split(hidden, give, down_ref, outs[:2])
+    split(hidden, keep, down_ref, outs[-2:])
+
+
+def down(hidden, give, keep, w_down, width):
     rows, hid = hidden.shape
-    count = len(kinds)
+    count = len(give) + len(keep)
+    outs = []
+    if give:
+        outs += [jax.ShapeDtypeStruct((len(give), rows // 2, width), jnp.bfloat16)] * 2
+    outs += [jax.ShapeDtypeStruct((len(keep), rows // 2, width), jnp.float32)] * 2
     return pl.pallas_call(
-        functools.partial(down_kernel, picks),
-        out_shape=[jax.ShapeDtypeStruct((rows, width), kind) for kind in kinds],
+        functools.partial(down_kernel, give, keep),
+        out_shape=outs,
         in_specs=whole(2),
-        out_specs=whole(count),
+        out_specs=whole(len(outs)),
         compiler_params=params(16),
         cost_estimate=pl.CostEstimate(
             flops=2 * rows * width * hid * count,
@@ -292,8 +302,8 @@
     stages = tensor.bit_length() - 2
     subsets = 1 << stages
 
-    def shift(value, by):
-        return lax.ppermute(value, "expert", [(i, (i + by) % experts) for i in range(experts)])
+    def across(value, by):
+        return lax.ppermute(value, "expert", [(i, i ^ by) for i in range(experts)])
 
     def swap(value):
         return lax.ppermute(value, "tensor", [(i, i ^ 1) for i in range(tensor)])
@@ -309,61 +319,68 @@
     ahead = list(zip(reach(0), reach(1)))
     mine = [(0, a, b) for a, b in ahead]
     theirs = [(1, b, a) for a, b in ahead]
+    batches = [range(0, 2)] + [range(1 << s, 2 << s) for s in range(1, stages)]
+    top = stages - 1
 
     ids = expert_ids.T
     outgoing = route(stashed, ids, experts, capacity)
     arrived = [outgoing[0]]
     for j in range(1, experts):
-        arrived.append(shift(outgoing[j], j))
+        arrived.append(across(outgoing[j], j))
     high, low = mixer(ids, combine_weight.T, experts, capacity)
-    pieces = [jnp.concatenate(arrived, axis=0)]
-    for stage in range(stages):
-        for k in range(1 << stage):
-            pieces.append(hop(pieces[k], stage))
-    swapped = []
-    for k in range(subsets):
-        swapped.append(swap(pieces[k]))
+
+    near = experts // 2
+    own, other = [], []
+    for h in (0, 1):
+        x = jnp.concatenate(arrived[h * near : (h + 1) * near], axis=0)[None]
+        made, moved = [], []
+        for stage in range(stages):
+            got = hop(x, stage)
+            x = jnp.concatenate([x, got], axis=0)
+            made.append(x if stage == 0 else got)
+            moved.append(swap(made[-1]))
+        own.append(made)
+        other.append(moved)
 
     sums = None
-    for k in range(subsets - 1):
-        xs, picks = [pieces[k], swapped[k]], [mine[k], theirs[k]]
-        sums = gate_up(xs, picks, w_gate, w_up, sums)
-    last = subsets - 1
-    hidden, first_given = gate_up(
-        [pieces[last], swapped[last]],
-        [mine[last], theirs[last], theirs[last]],
-        w_gate,
-        w_up,
-        sums,
-        w_down,
-    )
-
-    half = subsets // 2
-    upper, lower = list(range(last, half - 1, -1)), list(range(half - 1, -1, -1))
-    given, kept = {last: first_given}, {}
-    for give, keep in ((upper[1:], upper), (lower, lower)):
-        made = down(
-            hidden,
-            [theirs[k] for k in give] + [mine[k] for k in keep],
-            w_down,
-            width,
-            [jnp.bfloat16] * len(give) + [jnp.float32] * len(keep),
+    for b, batch in enumerate(batches):
+        sums = gate_up(
+            [own[0][b], own[1][b]], [mine[k] for k in batch], w_gate, w_up, sums
         )
-        given.update(zip(give, made))
-        kept.update(zip(keep, made[len(give) :]))
-    sums = [None] * subsets
-    for k in upper + lower:
-        got = swap(given[k])
-        sums[k] = kept[k] + got.astype(jnp.float32)
+        halves, picks = [other[0][b], other[1][b]], [theirs[k] for k in batch]
+        if b < top:
+            sums = gate_up(halves, picks, w_gate, w_up, sums)
+    hidden, *given = gate_up(halves, picks, w_gate, w_up, sums, w_down, picks)
+
+    totals = [[None] * subsets, [None] * subsets]
+    for b in reversed(range(stages)):
+        keep = [mine[k] for k in batches[b]]
+        if b == top:
+            kept = down(hidden, [], keep, w_down, width)
+        else:
+            give = [theirs[k] for k in batches[b]]
+            *given, kept0, kept1 = down(hidden, give, keep, w_down, width)
+            kept = [kept0, kept1]
+        for h in (1, 0):
+            got = swap(given[h])
+            total = kept[h] + got.astype(jnp.float32)
+            for i, k in enumerate(batches[b]):
+                totals[h][k] = total[i]
+    result = [None, None]
     for stage in reversed(range(stages)):
-        for k in reversed(range(1 << stage)):
-            got = hop(sums[(1 << stage) + k].astype(jnp.bfloat16), stage)
-            sums[k] = sums[k] + got.astype(jnp.float32)
-    result = sums[0].astype(jnp.bfloat16)
-    parts = [result[j * capacity : (j + 1) * capacity] for j in range(experts)]
+        for h in (1, 0):
+            total = totals[h]
+            sent = jnp.stack(total[1 << stage :]).astype(jnp.bfloat16)
+            got = hop(sent, stage)
+            totals[h] = [t + got[i].astype(jnp.float32) for i, t in enumerate(total[: 1 << stage])]
+    result = [half[0].astype(jnp.bfloat16) for half in totals]
+    parts = [
+        result[j // near][j % near * capacity : (j % near + 1) * capacity]
+        for j in range(experts)
+    ]
     back = [parts[0]]
     for j in range(1, experts):
-        back.append(shift(parts[j], -j))
+        back.append(across(parts[j], j))
     return combine(high, low, back)
 
 
@@ -375,6 +392,8 @@
         aligned = (
             tensor >= 4
             and tensor & (tensor - 1) == 0
+            and experts >= 2
+            and experts & (experts - 1) == 0
             and width % 128 == 0
             and w_gate.shape[1] % 128 == 0
             and slots_of(tokens, experts) % 16 == 0

time: 67.6 us -> 65 us (0.962)
  waiting for transfers between devices: 27.5 us -> 25.7 us
  other arithmetic: 0.38 us -> 1.38 us
  starting transfers between devices: 20.6 us -> 19.7 us
  local copies, waits for them, and re-layouts: 7.83 us -> 6.98 us
    ppermute x6 -> x8, waiting for transfers between devices: 19.7 us -> 16.7 us  [hop(): return lax.ppermute(value, 'tensor', pairs)]
    ppermute x6, starting transfers between devices: 10.8 us -> 9.32 us  [across(): return lax.ppermute(value, 'expert', [(i, i ^ by) for i in range(experts)])]
    ppermute x6, waiting for transfers between devices: 7.75 us -> 9 us  [across(): return lax.ppermute(value, 'expert', [(i, i ^ by) for i in range(experts)])]
    broadcast_in_dim x0 -> x2, other arithmetic: none -> 0.86 us  [shards(): x = jnp.concatenate(arrived[h * near:(h + 1) * near], axis=0)[None]]
    unnamed x15 -> x12, local copies, waits for them, and re-layouts: 7.81 us -> 6.95 us
    ppermute x6 -> x8, starting transfers between devices: 7.99 us -> 8.66 us  [hop(): return lax.ppermute(value, 'tensor', pairs)]
  transfers between devices with their start and end apart: 20 -> 22, of which waited for: 10 -> 13; matrix products, arithmetic and copies ran while one was open for 2% -> 2% of each run, Pallas kernels for 10% -> 10%
where the time goes in v3:
time: 65 us; the launch traced here: 64.7 us
  waiting for transfers between devices  25.7 us (40%)
  starting transfers between devices  19.7 us (30%)
  Pallas kernels  10.8 us (17%)
  local copies, waits for them, and re-layouts  6.98 us (11%)
  other arithmetic  1.38 us (2%)
    ppermute x8, waiting for transfers between devices, hop(): return lax.ppermute(value, 'tensor', pairs)  16.7 us
    ppermute x6, starting transfers between devices, across(): return lax.ppermute(value, 'expert', [(i, i ^ by) for i in range(experts)])  9.32 us
    ppermute x6, waiting for transfers between devices, across(): return lax.ppermute(value, 'expert', [(i, i ^ by) for i in range(experts)])  9 us
    ppermute x8, starting transfers between devices, hop(): return lax.ppermute(value, 'tensor', pairs)  8.66 us
    unnamed x12, local copies, waits for them, and re-layouts  6.95 us
    pallas_call x4, Pallas kernels, gate_up(): pl.pallas_call(functools.partial(gate_up_kernel, picks, give, fresh), out...  5.79 us
    pallas_call x2, Pallas kernels, down(): pl.pallas_call(functools.partial(down_kernel, give, keep), out_shape=outs...  1.97 us
    pallas_call x1, Pallas kernels, route(): pl.pallas_call(functools.partial(route_kernel, experts, capacity), out_sh...  1.78 us
  transfers between devices with their start and end apart: 22, of which 13 were waited for; matrix products, arithmetic and copies ran while one was open for 2% of the time, Pallas kernels for 10%

profile of v3, /device:TPU:0, one launch (start us, length us, event | category | flops | bytes accessed | tf_op | source)
XLA Modules:
  0.0 64.7 jit_solution(7498580637792568297)
XLA Ops:
  0.0 1.8 %route.1 = (bf16[64,512]{1,0:T(8,128)(2,1)}, bf16[64,512]{1,0:T(8,128)(2,1)}, bf16[64,512]{1,0:T(8,128)(2,1)}, bf16[64,512]{1,0:T(8,128)(2,1)}) custom-call(s32[2,96]{1,0:T(2,128)} %bitcast.16, bf16[96,512]{1,0:T(8,128)(2,1)} %x_hbm.1), custom_call_target="tpu_custom_call" | custom-call | tf_op jit(solution)/shard_map/route/pallas_call | solution.py:115
  1.8 4.1 %collective-permute-start.4 = (bf16[64,512]{1,0:T(8,128)(2,1)}, bf16[64,512]{1,0:T(8,128)(2,1)S(1)}, u32[]{:S(2)}, u32[]{:S(2)}) collective-permute-start(bf16[64,512]{1,0:T(8,128)(2,1)} %get-tuple-element.30), channel_id=1, source_target_pairs={{0,16},{8,24},{16,0},{24,8},{1,17},{9,25},{17,1},{25,9},{2,18},{10... | collective-permute-start | bytes 196616 | tf_op jit(solution)/shard_map/ppermute | solution.py:306
  5.9 1.3 %collective-permute-start.5 = (bf16[64,512]{1,0:T(8,128)(2,1)}, bf16[64,512]{1,0:T(8,128)(2,1)S(1)}, u32[]{:S(2)}, u32[]{:S(2)}) collective-permute-start(bf16[64,512]{1,0:T(8,128)(2,1)} %get-tuple-element.31), channel_id=1, source_target_pairs={{0,24},{8,16},{16,8},{24,0},{1,25},{9,17},{17,9},{25,1},{2,26},{10... | collective-permute-start | bytes 196616 | tf_op jit(solution)/shard_map/ppermute | solution.py:306
  7.5 2.3 %collective-permute-done.4 = bf16[64,512]{1,0:T(8,128)(2,1)S(1)} collective-permute-done((bf16[64,512]{1,0:T(8,128)(2,1)}, bf16[64,512]{1,0:T(8,128)(2,1)S(1)}, u32[]{:S(2)}, u32[]{:S(2)}) %collective-permute-start.4) | collective-permute-done | bytes 65568 | tf_op jit(solution)/shard_map/ppermute | solution.py:306
  9.8 2.5 %collective-permute-done.5 = bf16[64,512]{1,0:T(8,128)(2,1)S(1)} collective-permute-done((bf16[64,512]{1,0:T(8,128)(2,1)}, bf16[64,512]{1,0:T(8,128)(2,1)S(1)}, u32[]{:S(2)}, u32[]{:S(2)}) %collective-permute-start.5) | collective-permute-done | bytes 65568 | tf_op jit(solution)/shard_map/ppermute | solution.py:306
  12.3 1.6 %collective-permute-start.6 = (bf16[1,128,512]{2,1,0:T(8,128)(2,1)S(1)}, bf16[1,128,512]{2,1,0:T(8,128)(2,1)S(1)}, u32[]{:S(2)}, u32[]{:S(2)}) collective-permute-start(bf16[1,128,512]{2,1,0:T(8,128)(2,1)S(1)} %maximum_bitcast_fusion.1), channel_id=1, source_target_pairs={{0,2},{1,5},{2,0},{3,7},{4,6},{5,1},{6,4},{7,3},{8,10},{9,13},{10,... | collective-permute-start | bytes 393224 | tf_op jit(solution)/shard_map/ppermute | solution.py:313
  13.9 0.8 %maximum_bitcast_fusion = bf16[1,128,512]{2,1,0:T(8,128)(2,1)S(1)} fusion(bf16[64,512]{1,0:T(8,128)(2,1)S(1)} %collective-permute-done, bf16[64,512]{1,0:T(8,128)(2,1)} %get-tuple-element.28), kind=kLoop, calls=%fused_computation.16 | loop fusion | flops 262144 | bytes 262144 | tf_op jit(solution)/shard_map/broadcast_in_dim | solution.py:335
  15.3 2.1 %collective-permute-done.6 = bf16[1,128,512]{2,1,0:T(8,128)(2,1)S(1)} collective-permute-done((bf16[1,128,512]{2,1,0:T(8,128)(2,1)S(1)}, bf16[1,128,512]{2,1,0:T(8,128)(2,1)S(1)}, u32[]{:S(2)}, u32[]{:S(2)}) %collective-permute-start.6) | collective-permute-done | bytes 131104 | tf_op jit(solution)/shard_map/ppermute | solution.py:313
  17.5 1.5 %collective-permute-start.7 = (bf16[2,128,512]{2,1,0:T(8,128)(2,1)S(1)}, bf16[2,128,512]{2,1,0:T(8,128)(2,1)S(1)}, u32[]{:S(2)}, u32[]{:S(2)}) collective-permute-start(bf16[2,128,512]{2,1,0:T(8,128)(2,1)S(1)} %pad_maximum_fusion.1.refs_1_), channel_id=1, source_target_pairs={{0,4},{1,3},{2,6},{3,1},{4,0},{5,7},{6,2},{7,5},{8,12},{9,11},{10,... | collective-permute-start | bytes 786440 | tf_op jit(solution)/shard_map/ppermute | solution.py:313
  19.0 2.1 %collective-permute-done.1 = bf16[1,128,512]{2,1,0:T(8,128)(2,1)S(1)} collective-permute-done((bf16[1,128,512]{2,1,0:T(8,128)(2,1)S(1)}, bf16[1,128,512]{2,1,0:T(8,128)(2,1)S(1)}, u32[]{:S(2)}, u32[]{:S(2)}) %collective-permute-start.1) | collective-permute-done | bytes 131104 | tf_op jit(solution)/shard_map/ppermute | solution.py:313
  21.2 1.6 %collective-permute-start.2 = (bf16[2,128,512]{2,1,0:T(8,128)(2,1)S(1)}, bf16[2,128,512]{2,1,0:T(8,128)(2,1)S(1)}, u32[]{:S(2)}, u32[]{:S(2)}) collective-permute-start(bf16[2,128,512]{2,1,0:T(8,128)(2,1)S(1)} %pad_maximum_fusion.refs_0_), channel_id=1, source_target_pairs={{0,4},{1,3},{2,6},{3,1},{4,0},{5,7},{6,2},{7,5},{8,12},{9,11},{10,... | collective-permute-start | bytes 786440 | tf_op jit(solution)/shard_map/ppermute | solution.py:313
  23.3 0.6 collective-permute-done.7.refs_1_
  23.9 3.7 %collective-permute-done.2.refs_0_ = bf16[2,128,512]{2,1,0:T(8,128)(2,1)S(1)} collective-permute-done((bf16[2,128,512]{2,1,0:T(8,128)(2,1)S(1)}, bf16[2,128,512]{2,1,0:T(8,128)(2,1)S(1)}, u32[]{:S(2)}, u32[]{:S(2)}) %collective-permute-start.2) | collective-permute-done | bytes 262176 | tf_op jit(solution)/shard_map/ppermute | solution.py:313
  27.6 3.1 %copy-done = bf16[1,896,4096]{2,1,0:T(8,128)(2,1)S(1)} copy-done((bf16[1,896,4096]{2,1,0:T(8,128)(2,1)S(1)}, bf16[1,896,4096]{2,1,0:T(8,128)(2,1)}, u32[]{:S(2)}) %copy-start) | copy-done | bytes 7340056
  30.7 3.1 %copy-done.1 = bf16[1,896,4096]{2,1,0:T(8,128)(2,1)S(1)} copy-done((bf16[1,896,4096]{2,1,0:T(8,128)(2,1)S(1)}, bf16[1,896,4096]{2,1,0:T(8,128)(2,1)}, u32[]{:S(2)}) %copy-start.1) | copy-done | bytes 7340056
  33.8 1.3 %gate_up.4 = (f32[256,896]{1,0:T(8,128)S(1)}, f32[256,896]{1,0:T(8,128)S(1)}) custom-call(bf16[1,896,4096]{2,1,0:T(8,128)(2,1)S(1)} %copy-done, bf16[1,896,4096]{2,1,0:T(8,128)(2,1)S(1)} %copy-done.1, bf16[2,128,512]{2,1,0:T(8,128)(2,1)S(1)} %pad_maximum_fusion.refs_0_, bf16[2,128,512]{2,1,0:T(8,128)(2,1)S(1)} %pad_maximum_fusion.1.refs_1_), custom_call_target="tpu_custom_call" | custom-call | flops 939524096 | bytes 3670016 | tf_op jit(solution)/shard_map/gate_up/pallas_call | solution.py:226
  35.1 1.3 %gate_up.5 = (f32[256,896]{1,0:T(8,128)S(1)}, f32[256,896]{1,0:T(8,128)S(1)}) custom-call(bf16[1,896,4096]{2,1,0:T(8,128)(2,1)S(1)} %copy-done, bf16[1,896,4096]{2,1,0:T(8,128)(2,1)S(1)} %copy-done.1, bf16[2,128,512]{2,1,0:T(8,128)(2,1)S(1)} %collective-permute-done.9.refs_0_, bf16[2,128,512]{2,1,0:T(8,128)(2,1)S(1)} %collective-permute-done.10.refs_1_, ...), custom_call_target="tpu_custom_call" | custom-call | flops 939524096 | bytes 3670016 | tf_op jit(solution)/shard_map/gate_up/pallas_call | solution.py:226
  36.4 1.3 %gate_up.6 = (f32[256,896]{1,0:T(8,128)S(1)}, f32[256,896]{1,0:T(8,128)S(1)}) custom-call(bf16[1,896,4096]{2,1,0:T(8,128)(2,1)S(1)} %copy-done, bf16[1,896,4096]{2,1,0:T(8,128)(2,1)S(1)} %copy-done.1, bf16[2,128,512]{2,1,0:T(8,128)(2,1)S(1)} %collective-permute-done.2.refs_0_, bf16[2,128,512]{2,1,0:T(8,128)(2,1)S(1)} %collective-permute-done.7.refs_1_, ...), custom_call_target="tpu_custom_call" | custom-call | flops 939524096 | bytes 3670016 | tf_op jit(solution)/shard_map/gate_up/pallas_call | solution.py:226
  37.8 0.8 %slice-done.1 = s8[3145728]{0:T(1024)(128)(4,1)S(1)} async-done(((s8[7340032]{0:T(1024)(128)(4,1)}), s8[3145728]{0:T(1024)(128)(4,1)S(1)}, s32[]{:S(2)}) %slice-start.1) | async-done | bytes 3145752
  38.5 1.9 %gate_up.7 = (bf16[256,896]{1,0:T(8,128)(2,1)S(1)}, bf16[2,128,512]{2,1,0:T(8,128)(2,1)S(1)}, bf16[2,128,512]{2,1,0:T(8,128)(2,1)S(1)}) custom-call(bf16[1,896,4096]{2,1,0:T(8,128)(2,1)S(1)} %copy-done, bf16[1,896,4096]{2,1,0:T(8,128)(2,1)S(1)} %copy-done.1, bf16[1,896,4096]{2,1,0:T(8,128)(2,1)S(1)} %bitcast.15, ...), custom_call_target="tpu_custom_call" | custom-call | flops 939524096 | bytes 3670016 | tf_op jit(solution)/shard_map/gate_up/pallas_call | solution.py:226
  41.1 1.3 %down.2 = (bf16[2,128,512]{2,1,0:T(8,128)(2,1)S(1)}, bf16[2,128,512]{2,1,0:T(8,128)(2,1)S(1)}, f32[2,128,512]{2,1,0:T(8,128)S(1)}, f32[2,128,512]{2,1,0:T(8,128)S(1)}) custom-call(bf16[1,896,4096]{2,1,0:T(8,128)(2,1)S(1)} %bitcast.15, bf16[256,896]{1,0:T(8,128)(2,1)S(1)} %get-tuple-element.38.hidden_ref), custom_call_target="tpu_custom_call" | custom-call | flops 939524096 | bytes 3670016 | tf_op jit(solution)/shard_map/down/pallas_call | solution.py:255
  42.3 0.7 %down.3 = (f32[2,128,512]{2,1,0:T(8,128)S(1)}, f32[2,128,512]{2,1,0:T(8,128)S(1)}) custom-call(bf16[1,896,4096]{2,1,0:T(8,128)(2,1)S(1)} %bitcast.15, bf16[256,896]{1,0:T(8,128)(2,1)S(1)} %get-tuple-element.38.hidden_ref), custom_call_target="tpu_custom_call" | custom-call | flops 469762048 | bytes 1835008 | tf_op jit(solution)/shard_map/down/pallas_call | solution.py:255
  43.7 1.6 %collective-permute-start.18 = (bf16[2,128,512]{2,1,0:T(8,128)(2,1)S(1)}, bf16[2,128,512]{2,1,0:T(8,128)(2,1)S(1)}, u32[]{:S(2)}, u32[]{:S(2)}) collective-permute-start(bf16[2,128,512]{2,1,0:T(8,128)(2,1)S(1)} %add_convert_fusion), channel_id=1, source_target_pairs={{0,4},{1,3},{2,6},{3,1},{4,0},{5,7},{6,2},{7,5},{8,12},{9,11},{10,... | collective-permute-start | bytes 786440 | tf_op jit(solution)/shard_map/ppermute | solution.py:313
  46.2 4.0 %collective-permute-done.18 = bf16[2,128,512]{2,1,0:T(8,128)(2,1)S(1)} collective-permute-done((bf16[2,128,512]{2,1,0:T(8,128)(2,1)S(1)}, bf16[2,128,512]{2,1,0:T(8,128)(2,1)S(1)}, u32[]{:S(2)}, u32[]{:S(2)}) %collective-permute-start.18) | collective-permute-done | bytes 262176 | tf_op jit(solution)/shard_map/ppermute | solution.py:313
  50.8 2.7 %collective-permute-done.13 = bf16[2,128,512]{2,1,0:T(8,128)(2,1)S(1)} collective-permute-done((bf16[2,128,512]{2,1,0:T(8,128)(2,1)S(1)}, bf16[2,128,512]{2,1,0:T(8,128)(2,1)S(1)}, u32[]{:S(2)}, u32[]{:S(2)}) %collective-permute-start.13) | collective-permute-done | bytes 262176 | tf_op jit(solution)/shard_map/ppermute | solution.py:313
  54.2 1.1 %collective-permute-done.19 = bf16[1,128,512]{2,1,0:T(8,128)(2,1)S(1)} collective-permute-done((bf16[1,128,512]{2,1,0:T(8,128)(2,1)S(1)}, bf16[1,128,512]{2,1,0:T(8,128)(2,1)S(1)}, u32[]{:S(2)}, u32[]{:S(2)}) %collective-permute-start.19) | collective-permute-done | bytes 131104 | tf_op jit(solution)/shard_map/ppermute | solution.py:313
  55.3 2.3 %collective-permute-start.20 = (bf16[64,512]{1,0:T(8,128)(2,1)S(1)}, bf16[64,512]{1,0:T(8,128)(2,1)S(1)}, u32[]{:S(2)}, u32[]{:S(2)}) collective-permute-start(bf16[64,512]{1,0:T(8,128)(2,1)S(1)} %get-tuple-element.48), channel_id=1, source_target_pairs={{0,16},{8,24},{16,0},{24,8},{1,17},{9,25},{17,1},{25,9},{2,18},{10... | collective-permute-start | bytes 196616 | tf_op jit(solution)/shard_map/ppermute | solution.py:306
  57.6 0.6 %collective-permute-start.21 = (bf16[64,512]{1,0:T(8,128)(2,1)S(1)}, bf16[64,512]{1,0:T(8,128)(2,1)S(1)}, u32[]{:S(2)}, u32[]{:S(2)}) collective-permute-start(bf16[64,512]{1,0:T(8,128)(2,1)S(1)} %get-tuple-element.47), channel_id=1, source_target_pairs={{0,24},{8,16},{16,8},{24,0},{1,25},{9,17},{17,9},{25,1},{2,26},{10... | collective-permute-start | bytes 196616 | tf_op jit(solution)/shard_map/ppermute | solution.py:306
  58.7 0.6 collective-permute-start.15
  59.7 2.9 %collective-permute-done.20.refs_2_ = bf16[64,512]{1,0:T(8,128)(2,1)S(1)} collective-permute-done((bf16[64,512]{1,0:T(8,128)(2,1)S(1)}, bf16[64,512]{1,0:T(8,128)(2,1)S(1)}, u32[]{:S(2)}, u32[]{:S(2)}) %collective-permute-start.20) | collective-permute-done | bytes 65568 | tf_op jit(solution)/shard_map/ppermute | solution.py:306
  62.6 1.2 %collective-permute-done.21.refs_3_ = bf16[64,512]{1,0:T(8,128)(2,1)S(1)} collective-permute-done((bf16[64,512]{1,0:T(8,128)(2,1)S(1)}, bf16[64,512]{1,0:T(8,128)(2,1)S(1)}, u32[]{:S(2)}, u32[]{:S(2)}) %collective-permute-start.21) | collective-permute-done | bytes 65568 | tf_op jit(solution)/shard_map/ppermute | solution.py:306
  63.9 0.9 %combine.1 = bf16[96,512]{1,0:T(8,128)(2,1)} custom-call(bf16[96,256]{1,0:T(8,128)(2,1)S(1)} %get-tuple-element.26.high_ref, bf16[96,256]{1,0:T(8,128)(2,1)S(1)} %get-tuple-element.27.low_ref, bf16[64,512]{1,0:T(8,128)(2,1)S(1)} %get-tuple-element.50.refs_0_, bf16[64,512]{1,0:T(8,128)(2,1)S(1)} %collective-permute-done.15.refs_1_, ...), custom_call_target="tpu_custom_call" | custom-call | tf_op jit(solution)/shard_map/combine/pallas_call | solution.py:279
  (48 shorter events, 5.7 us)
Async XLA Ops:
  1.8 8.1 %collective-permute-start.4 = (bf16[64,512]{1,0:T(8,128)(2,1)}, bf16[64,512]{1,0:T(8,128)(2,1)S(1)}, u32[]{:S(2)}, u32[]{:S(2)}) collective-permute-start(bf16[64,512]{1,0:T(8,128)(2,1)} %get-tuple-element.30), channel_id=1, source_target_pairs={{0,16},{8,24},{16,0},{24,8},{1,17},{9,25},{17,1},{25,9},{2,18},{10... | collective-permute-start | bytes 196616 | tf_op jit(solution)/shard_map/ppermute | solution.py:306
  5.9 6.4 %collective-permute-start.5 = (bf16[64,512]{1,0:T(8,128)(2,1)}, bf16[64,512]{1,0:T(8,128)(2,1)S(1)}, u32[]{:S(2)}, u32[]{:S(2)}) collective-permute-start(bf16[64,512]{1,0:T(8,128)(2,1)} %get-tuple-element.31), channel_id=1, source_target_pairs={{0,24},{8,16},{16,8},{24,0},{1,25},{9,17},{17,9},{25,1},{2,26},{10... | collective-permute-start | bytes 196616 | tf_op jit(solution)/shard_map/ppermute | solution.py:306
  7.3 6.6 %collective-permute-start = (bf16[64,512]{1,0:T(8,128)(2,1)}, bf16[64,512]{1,0:T(8,128)(2,1)S(1)}, u32[]{:S(2)}, u32[]{:S(2)}) collective-permute-start(bf16[64,512]{1,0:T(8,128)(2,1)} %get-tuple-element.29), channel_id=1, source_target_pairs={{0,8},{8,0},{16,24},{24,16},{1,9},{9,1},{17,25},{25,17},{2,10},{10... | collective-permute-start | bytes 196616 | tf_op jit(solution)/shard_map/ppermute | solution.py:306
  12.3 5.1 %collective-permute-start.6 = (bf16[1,128,512]{2,1,0:T(8,128)(2,1)S(1)}, bf16[1,128,512]{2,1,0:T(8,128)(2,1)S(1)}, u32[]{:S(2)}, u32[]{:S(2)}) collective-permute-start(bf16[1,128,512]{2,1,0:T(8,128)(2,1)S(1)} %maximum_bitcast_fusion.1), channel_id=1, source_target_pairs={{0,2},{1,5},{2,0},{3,7},{4,6},{5,1},{6,4},{7,3},{8,10},{9,13},{10,... | collective-permute-start | bytes 393224 | tf_op jit(solution)/shard_map/ppermute | solution.py:313
  14.7 6.4 %collective-permute-start.1 = (bf16[1,128,512]{2,1,0:T(8,128)(2,1)S(1)}, bf16[1,128,512]{2,1,0:T(8,128)(2,1)S(1)}, u32[]{:S(2)}, u32[]{:S(2)}) collective-permute-start(bf16[1,128,512]{2,1,0:T(8,128)(2,1)S(1)} %maximum_bitcast_fusion), channel_id=1, source_target_pairs={{0,2},{1,5},{2,0},{3,7},{4,6},{5,1},{6,4},{7,3},{8,10},{9,13},{10,... | collective-permute-start | bytes 393224 | tf_op jit(solution)/shard_map/ppermute | solution.py:313
  17.5 6.4 %collective-permute-start.7 = (bf16[2,128,512]{2,1,0:T(8,128)(2,1)S(1)}, bf16[2,128,512]{2,1,0:T(8,128)(2,1)S(1)}, u32[]{:S(2)}, u32[]{:S(2)}) collective-permute-start(bf16[2,128,512]{2,1,0:T(8,128)(2,1)S(1)} %pad_maximum_fusion.1.refs_1_), channel_id=1, source_target_pairs={{0,4},{1,3},{2,6},{3,1},{4,0},{5,7},{6,2},{7,5},{8,12},{9,11},{10,... | collective-permute-start | bytes 786440 | tf_op jit(solution)/shard_map/ppermute | solution.py:313
  21.2 6.4 %collective-permute-start.2 = (bf16[2,128,512]{2,1,0:T(8,128)(2,1)S(1)}, bf16[2,128,512]{2,1,0:T(8,128)(2,1)S(1)}, u32[]{:S(2)}, u32[]{:S(2)}) collective-permute-start(bf16[2,128,512]{2,1,0:T(8,128)(2,1)S(1)} %pad_maximum_fusion.refs_0_), channel_id=1, source_target_pairs={{0,4},{1,3},{2,6},{3,1},{4,0},{5,7},{6,2},{7,5},{8,12},{9,11},{10,... | collective-permute-start | bytes 786440 | tf_op jit(solution)/shard_map/ppermute | solution.py:313
  22.8 12.3 %collective-permute-start.10 = (bf16[2,128,512]{2,1,0:T(8,128)(2,1)S(1)}, bf16[2,128,512]{2,1,0:T(8,128)(2,1)S(1)}, u32[]{:S(2)}, u32[]{:S(2)}) collective-permute-start(bf16[2,128,512]{2,1,0:T(8,128)(2,1)S(1)} %pad_maximum_fusion.1.refs_1_), channel_id=1, source_target_pairs={{0,1},{1,0},{2,3},{3,2},{4,5},{5,4},{6,7},{7,6},{8,9},{9,8},{10,11... | collective-permute-start | bytes 786440 | tf_op jit(solution)/shard_map/ppermute | solution.py:309
  22.8 12.3 %collective-permute-start.9 = (bf16[2,128,512]{2,1,0:T(8,128)(2,1)S(1)}, bf16[2,128,512]{2,1,0:T(8,128)(2,1)S(1)}, u32[]{:S(2)}, u32[]{:S(2)}) collective-permute-start(bf16[2,128,512]{2,1,0:T(8,128)(2,1)S(1)} %pad_maximum_fusion.refs_0_), channel_id=1, source_target_pairs={{0,1},{1,0},{2,3},{3,2},{4,5},{5,4},{6,7},{7,6},{8,9},{9,8},{10,11... | collective-permute-start | bytes 786440 | tf_op jit(solution)/shard_map/ppermute | solution.py:309
  23.9 13.8 %collective-permute-start.8 = (bf16[2,128,512]{2,1,0:T(8,128)(2,1)S(1)}, bf16[2,128,512]{2,1,0:T(8,128)(2,1)S(1)}, u32[]{:S(2)}, u32[]{:S(2)}) collective-permute-start(bf16[2,128,512]{2,1,0:T(8,128)(2,1)S(1)} %collective-permute-done.7.refs_1_), channel_id=1, source_target_pairs={{0,1},{1,0},{2,3},{3,2},{4,5},{5,4},{6,7},{7,6},{8,9},{9,8},{10,11... | collective-permute-start | bytes 786440 | tf_op jit(solution)/shard_map/ppermute | solution.py:309
  27.6 10.1 %collective-permute-start.3 = (bf16[2,128,512]{2,1,0:T(8,128)(2,1)S(1)}, bf16[2,128,512]{2,1,0:T(8,128)(2,1)S(1)}, u32[]{:S(2)}, u32[]{:S(2)}) collective-permute-start(bf16[2,128,512]{2,1,0:T(8,128)(2,1)S(1)} %collective-permute-done.2.refs_0_), channel_id=1, source_target_pairs={{0,1},{1,0},{2,3},{3,2},{4,5},{5,4},{6,7},{7,6},{8,9},{9,8},{10,11... | collective-permute-start | bytes 786440 | tf_op jit(solution)/shard_map/ppermute | solution.py:309
  27.6 3.1 %copy-start = (bf16[1,896,4096]{2,1,0:T(8,128)(2,1)S(1)}, bf16[1,896,4096]{2,1,0:T(8,128)(2,1)}, u32[]{:S(2)}) copy-start(bf16[1,896,4096]{2,1,0:T(8,128)(2,1)} %gate_ref.7) | copy-start | bytes 22020100
  30.7 3.1 %copy-start.1 = (bf16[1,896,4096]{2,1,0:T(8,128)(2,1)S(1)}, bf16[1,896,4096]{2,1,0:T(8,128)(2,1)}, u32[]{:S(2)}) copy-start(bf16[1,896,4096]{2,1,0:T(8,128)(2,1)} %up_ref.7) | copy-start | bytes 22020100
  35.1 2.7 %slice-start = ((s8[7340032]{0:T(1024)(128)(4,1)}), s8[4194304]{0:T(1024)(128)(4,1)S(1)}, s32[]{:S(2)}) async-start(s8[7340032]{0:T(1024)(128)(4,1)} %bitcast.14), calls=%async_computation | async-start | bytes 8388608
  36.4 2.1 %slice-start.1 = ((s8[7340032]{0:T(1024)(128)(4,1)}), s8[3145728]{0:T(1024)(128)(4,1)S(1)}, s32[]{:S(2)}) async-start(s8[7340032]{0:T(1024)(128)(4,1)} %bitcast.14), calls=%async_computation.1 | async-start | bytes 6291456
  40.5 3.2 %collective-permute-start.17 = (bf16[2,128,512]{2,1,0:T(8,128)(2,1)S(1)}, bf16[2,128,512]{2,1,0:T(8,128)(2,1)S(1)}, u32[]{:S(2)}, u32[]{:S(2)}) collective-permute-start(bf16[2,128,512]{2,1,0:T(8,128)(2,1)S(1)} %get-tuple-element.46), channel_id=1, source_target_pairs={{0,1},{1,0},{2,3},{3,2},{4,5},{5,4},{6,7},{7,6},{8,9},{9,8},{10,11... | collective-permute-start | bytes 786440 | tf_op jit(solution)/shard_map/ppermute | solution.py:309
  41.0 4.4 %collective-permute-start.12 = (bf16[2,128,512]{2,1,0:T(8,128)(2,1)S(1)}, bf16[2,128,512]{2,1,0:T(8,128)(2,1)S(1)}, u32[]{:S(2)}, u32[]{:S(2)}) collective-permute-start(bf16[2,128,512]{2,1,0:T(8,128)(2,1)S(1)} %get-tuple-element.42), channel_id=1, source_target_pairs={{0,1},{1,0},{2,3},{3,2},{4,5},{5,4},{6,7},{7,6},{8,9},{9,8},{10,11... | collective-permute-start | bytes 786440 | tf_op jit(solution)/shard_map/ppermute | solution.py:309
  42.3 17.0 %copy-start.2 = (s32[96,2]{0,1:T(2,128)S(1)}, s32[96,2]{0,1:T(2,128)}, u32[]{:S(2)}) copy-start(s32[96,2]{0,1:T(2,128)} %param.7) | copy-start | bytes 2308
  42.3 17.0 %copy-start.3 = (f32[96,2]{0,1:T(2,128)S(1)}, f32[96,2]{0,1:T(2,128)}, u32[]{:S(2)}) copy-start(f32[96,2]{0,1:T(2,128)} %param.8) | copy-start | bytes 2308
  43.1 2.9 %collective-permute-start.16 = (bf16[2,128,512]{2,1,0:T(8,128)(2,1)S(1)}, bf16[2,128,512]{2,1,0:T(8,128)(2,1)S(1)}, u32[]{:S(2)}, u32[]{:S(2)}) collective-permute-start(bf16[2,128,512]{2,1,0:T(8,128)(2,1)S(1)} %get-tuple-element.44), channel_id=1, source_target_pairs={{0,1},{1,0},{2,3},{3,2},{4,5},{5,4},{6,7},{7,6},{8,9},{9,8},{10,11... | collective-permute-start | bytes 786440 | tf_op jit(solution)/shard_map/ppermute | solution.py:309
  43.6 2.5 %collective-permute-start.11 = (bf16[2,128,512]{2,1,0:T(8,128)(2,1)S(1)}, bf16[2,128,512]{2,1,0:T(8,128)(2,1)S(1)}, u32[]{:S(2)}, u32[]{:S(2)}) collective-permute-start(bf16[2,128,512]{2,1,0:T(8,128)(2,1)S(1)} %get-tuple-element.40), channel_id=1, source_target_pairs={{0,1},{1,0},{2,3},{3,2},{4,5},{5,4},{6,7},{7,6},{8,9},{9,8},{10,11... | collective-permute-start | bytes 786440 | tf_op jit(solution)/shard_map/ppermute | solution.py:309
  43.7 6.4 %collective-permute-start.18 = (bf16[2,128,512]{2,1,0:T(8,128)(2,1)S(1)}, bf16[2,128,512]{2,1,0:T(8,128)(2,1)S(1)}, u32[]{:S(2)}, u32[]{:S(2)}) collective-permute-start(bf16[2,128,512]{2,1,0:T(8,128)(2,1)S(1)} %add_convert_fusion), channel_id=1, source_target_pairs={{0,4},{1,3},{2,6},{3,1},{4,0},{5,7},{6,2},{7,5},{8,12},{9,11},{10,... | collective-permute-start | bytes 786440 | tf_op jit(solution)/shard_map/ppermute | solution.py:313
  45.4 8.1 %collective-permute-start.13 = (bf16[2,128,512]{2,1,0:T(8,128)(2,1)S(1)}, bf16[2,128,512]{2,1,0:T(8,128)(2,1)S(1)}, u32[]{:S(2)}, u32[]{:S(2)}) collective-permute-start(bf16[2,128,512]{2,1,0:T(8,128)(2,1)S(1)} %add_convert_fusion.1), channel_id=1, source_target_pairs={{0,4},{1,3},{2,6},{3,1},{4,0},{5,7},{6,2},{7,5},{8,12},{9,11},{10,... | collective-permute-start | bytes 786440 | tf_op jit(solution)/shard_map/ppermute | solution.py:313
  50.2 5.0 %collective-permute-start.19 = (bf16[1,128,512]{2,1,0:T(8,128)(2,1)S(1)}, bf16[1,128,512]{2,1,0:T(8,128)(2,1)S(1)}, u32[]{:S(2)}, u32[]{:S(2)}) collective-permute-start(bf16[1,128,512]{2,1,0:T(8,128)(2,1)S(1)} %fusion), channel_id=1, source_target_pairs={{0,2},{1,5},{2,0},{3,7},{4,6},{5,1},{6,4},{7,3},{8,10},{9,13},{10,... | collective-permute-start | bytes 393224 | tf_op jit(solution)/shard_map/ppermute | solution.py:313
  53.6 5.0 %collective-permute-start.14 = (bf16[1,128,512]{2,1,0:T(8,128)(2,1)S(1)}, bf16[1,128,512]{2,1,0:T(8,128)(2,1)S(1)}, u32[]{:S(2)}, u32[]{:S(2)}) collective-permute-start(bf16[1,128,512]{2,1,0:T(8,128)(2,1)S(1)} %fusion.3), channel_id=1, source_target_pairs={{0,2},{1,5},{2,0},{3,7},{4,6},{5,1},{6,4},{7,3},{8,10},{9,13},{10,... | collective-permute-start | bytes 393224 | tf_op jit(solution)/shard_map/ppermute | solution.py:313
  55.3 7.3 %collective-permute-start.20 = (bf16[64,512]{1,0:T(8,128)(2,1)S(1)}, bf16[64,512]{1,0:T(8,128)(2,1)S(1)}, u32[]{:S(2)}, u32[]{:S(2)}) collective-permute-start(bf16[64,512]{1,0:T(8,128)(2,1)S(1)} %get-tuple-element.48), channel_id=1, source_target_pairs={{0,16},{8,24},{16,0},{24,8},{1,17},{9,25},{17,1},{25,9},{2,18},{10... | collective-permute-start | bytes 196616 | tf_op jit(solution)/shard_map/ppermute | solution.py:306
  57.6 6.2 %collective-permute-start.21 = (bf16[64,512]{1,0:T(8,128)(2,1)S(1)}, bf16[64,512]{1,0:T(8,128)(2,1)S(1)}, u32[]{:S(2)}, u32[]{:S(2)}) collective-permute-start(bf16[64,512]{1,0:T(8,128)(2,1)S(1)} %get-tuple-element.47), channel_id=1, source_target_pairs={{0,24},{8,16},{16,8},{24,0},{1,25},{9,17},{17,9},{25,1},{2,26},{10... | collective-permute-start | bytes 196616 | tf_op jit(solution)/shard_map/ppermute | solution.py:306
  58.7 5.2 %collective-permute-start.15 = (bf16[64,512]{1,0:T(8,128)(2,1)S(1)}, bf16[64,512]{1,0:T(8,128)(2,1)S(1)}, u32[]{:S(2)}, u32[]{:S(2)}) collective-permute-start(bf16[64,512]{1,0:T(8,128)(2,1)S(1)} %get-tuple-element.49), channel_id=1, source_target_pairs={{0,8},{8,0},{16,24},{24,16},{1,9},{9,1},{17,25},{25,17},{2,10},{10... | collective-permute-start | bytes 196616 | tf_op jit(solution)/shard_map/ppermute | solution.py:306

commit v4 on v3

--- a/solution.py
+++ b/solution.py
@@ -71,21 +71,13 @@
     return combined.astype(jnp.bfloat16)
 
 
-def fetch(sem_ref, pairs):
-    copies = [pltpu.make_async_copy(s, d, sem_ref.at[i]) for i, (s, d) in enumerate(pairs)]
-    for copy in copies:
-        copy.start()
-    return copies
-
-
 def selection(ids, first_expert, experts, capacity):
     tokens = ids.shape[1]
     rows = experts * capacity
     row = lax.broadcasted_iota(jnp.int32, (rows, tokens), 0)
     expert = first_expert ^ (row // capacity)
     slot = row % capacity
-    first = ids[0:1, :] == expert
-    named = jnp.logical_or(first, ids[1:2, :] == expert)
+    named = jnp.logical_or(ids[0:1, :] == expert, ids[1:2, :] == expert)
     down = lax.broadcasted_iota(jnp.int32, (tokens, tokens), 0)
     across = lax.broadcasted_iota(jnp.int32, (tokens, tokens), 1)
     earlier = jnp.where(down < across, 1.0, 0.0).astype(jnp.bfloat16)
@@ -94,48 +86,55 @@
         earlier,
         preferred_element_type=jnp.float32,
     )
-    return first, jnp.logical_and(named, before == slot.astype(jnp.float32))
-
-
-def route_kernel(experts, capacity, ids_hbm, x_hbm, *refs):
-    outs, (ids_ref, x_ref, sem_ref) = refs[:experts], refs[experts:]
-    copies = fetch(sem_ref, [(ids_hbm, ids_ref), (x_hbm, x_ref)])
-    copies[0].wait()
-    _, chosen = selection(ids_ref[...], lax.axis_index("expert"), experts, capacity)
-    pick = jnp.where(chosen, 1.0, 0.0).astype(jnp.bfloat16)
-    copies[1].wait()
+    return jnp.logical_and(named, before == slot.astype(jnp.float32))
+
+
+def select_kernel(experts, capacity, ids_ref, pick_ref):
+    chosen = selection(ids_ref[...], lax.axis_index("expert"), experts, capacity)
+    pick_ref[...] = jnp.where(chosen, 1.0, 0.0).astype(jnp.bfloat16)
+
+
+def select(ids, experts, capacity):
+    return pl.pallas_call(
+        functools.partial(select_kernel, experts, capacity),
+        out_shape=jax.ShapeDtypeStruct((experts * capacity, ids.shape[1]), jnp.bfloat16),
+        in_specs=whole(1),
+        out_specs=pl.BlockSpec(memory_space=VM),
+        compiler_params=params(8),
+        cost_estimate=pl.CostEstimate(
+            flops=20_000_000_000, bytes_accessed=0, transcendentals=0
+        ),
+        name="select",
+    )(ids)
+
+
+def route_kernel(capacity, pick_ref, x_ref, *outs):
     x = x_ref[...]
-    for j in range(experts):
-        rows = pick[j * capacity : (j + 1) * capacity]
-        outs[j][...] = jnp.dot(rows, x, preferred_element_type=jnp.float32).astype(jnp.bfloat16)
-
-
-def route(stashed, ids, experts, capacity):
-    _, width = stashed.shape
-    return pl.pallas_call(
-        functools.partial(route_kernel, experts, capacity),
+    for j, out in enumerate(outs):
+        rows = pick_ref[j * capacity : (j + 1) * capacity]
+        out[...] = jnp.dot(rows, x, preferred_element_type=jnp.float32).astype(jnp.bfloat16)
+
+
+def route(stashed, pick, experts, capacity):
+    width = stashed.shape[1]
+    return pl.pallas_call(
+        functools.partial(route_kernel, capacity),
         out_shape=[jax.ShapeDtypeStruct((capacity, width), jnp.bfloat16)] * experts,
-        in_specs=[pl.BlockSpec(memory_space=pltpu.HBM)] * 2,
+        in_specs=whole(2),
         out_specs=whole(experts),
-        scratch_shapes=[
-            VM(ids.shape, jnp.int32),
-            VM(stashed.shape, jnp.bfloat16),
-            pltpu.SemaphoreType.DMA((2,)),
-        ],
-        compiler_params=pltpu.CompilerParams(vmem_limit_bytes=66743328),
+        compiler_params=params(8),
         name="route",
-    )(ids, stashed)
-
-
-def mixer_kernel(experts, capacity, ids_hbm, weight_hbm, high_ref, low_ref, ids_ref, weight_ref, sem_ref):
-    for copy in fetch(sem_ref, [(ids_hbm, ids_ref), (weight_hbm, weight_ref)]):
-        copy.wait()
-    first, chosen = selection(ids_ref[...], lax.axis_index("expert"), experts, capacity)
-    weight = weight_ref[...]
-    mix = jnp.where(chosen, jnp.where(first, weight[0:1, :], weight[1:2, :]), 0.0)
+    )(pick, stashed)
+
+
+def mixer_kernel(capacity, pick_ref, ids_ref, weight_ref, high_ref, low_ref):
+    rows, tokens = pick_ref.shape
+    row = lax.broadcasted_iota(jnp.int32, (rows, tokens), 0)
+    first = ids_ref[0:1, :] == lax.axis_index("expert") ^ (row // capacity)
+    weight = jnp.where(first, weight_ref[0:1, :], weight_ref[1:2, :])
+    mix = jnp.where(pick_ref[...].astype(jnp.float32) > 0.0, weight, 0.0)
     high = mix.astype(jnp.bfloat16)
     low = (mix - high.astype(jnp.float32)).astype(jnp.bfloat16)
-    tokens = mix.shape[1]
     down = lax.broadcasted_iota(jnp.int32, (tokens, tokens), 0)
     across = lax.broadcasted_iota(jnp.int32, (tokens, tokens), 1)
     same = jnp.where(down == across, 1.0, 0.0).astype(jnp.bfloat16)
@@ -143,24 +142,16 @@
     low_ref[...] = contract_last(same, low).astype(jnp.bfloat16)
 
 
-def mixer(ids, weight, experts, capacity):
-    tokens = ids.shape[1]
-    return pl.pallas_call(
-        functools.partial(mixer_kernel, experts, capacity),
-        out_shape=[jax.ShapeDtypeStruct((tokens, experts * capacity), jnp.bfloat16)] * 2,
-        in_specs=[pl.BlockSpec(memory_space=pltpu.HBM)] * 2,
+def mixer(pick, ids, weight, capacity):
+    rows, tokens = pick.shape
+    return pl.pallas_call(
+        functools.partial(mixer_kernel, capacity),
+        out_shape=[jax.ShapeDtypeStruct((tokens, rows), jnp.bfloat16)] * 2,
+        in_specs=whole(3),
         out_specs=whole(2),
-        scratch_shapes=[
-            VM(ids.shape, jnp.int32),
-            VM(weight.shape, jnp.float32),
-            pltpu.SemaphoreType.DMA((2,)),
-        ],
         compiler_params=params(8),
-        cost_estimate=pl.CostEstimate(
-            flops=10_000_000_000, bytes_accessed=0, transcendentals=0
-        ),
         name="mixer",
-    )(ids, weight)
+    )(pick, ids, weight)
 
 
 def owner(pick):
@@ -174,19 +165,16 @@
     return ref[0, :, pl.ds(pl.multiple_of(owner(pick) * width, 128), width)]
 
 
-def stacked(halves, index):
-    return jnp.concatenate([half[index] for half in halves], axis=0)
-
-
-def gate_up_kernel(picks, give, fresh, gate_ref, up_ref, *refs):
+def gate_up_kernel(picks, places, give, fresh, gate_ref, up_ref, *refs):
     final = len(give) > 0
     if final:
         down_ref, refs = refs[0], refs[1:]
-    halves, refs = refs[:2], refs[2:]
-    width = halves[0].shape[2]
+    count = len(picks)
+    xs, refs = refs[: 2 * count], refs[2 * count :]
+    width = xs[0].shape[2]
     gate, up = (None, None) if fresh else (refs[0][...], refs[1][...])
     for i, pick in enumerate(picks):
-        x = stacked(halves, i)
+        x = jnp.concatenate([xs[2 * i][places[i]], xs[2 * i + 1][...]], axis=0)
         g = contract_last(x, part(gate_ref, pick, width))
         u = contract_last(x, part(up_ref, pick, width))
         gate = g if gate is None else gate + g
@@ -196,64 +184,82 @@
         refs[-1][...] = up
         return
     hidden = (gate / (1.0 + jnp.exp(-gate)) * up).astype(jnp.bfloat16)
-    refs[-3][...] = hidden
-    split(hidden, give, down_ref, refs[-2:])
+    refs[-2][...] = hidden
+    split(hidden, give, down_ref, refs[-1:])
 
 
 def split(hidden, picks, down_ref, outs):
-    _, rows, width = outs[0].shape
+    width = outs[0].shape[2]
+    used = sum(out.shape[1] for out in outs)
+    skip = hidden.shape[0] - used
     for i, pick in enumerate(picks):
         value = jnp.dot(
-            hidden, part(down_ref, pick, width), preferred_element_type=jnp.float32
+            hidden[skip:], part(down_ref, pick, width), preferred_element_type=jnp.float32
         ).astype(outs[0].dtype)
-        outs[0][i] = value[:rows]
-        outs[1][i] = value[rows:]
-
-
-def gate_up(halves, picks, w_gate, w_up, sums, w_down=None, give=()):
-    _, rows, width = halves[0].shape
+        at = 0
+        for out in outs:
+            out[i] = value[at : at + out.shape[1]]
+            at += out.shape[1]
+
+
+def gate_up(items, picks, w_gate, w_up, sums, w_down=None, give=(), cut=0):
+    first, _, rest = items[0]
+    width = rest.shape[1]
     hid = w_gate.shape[1]
-    rows = 2 * rows
+    rows = first.shape[1] + rest.shape[0]
     count = len(picks)
     fresh = sums is None
     held = [] if fresh else list(sums)
     if give:
-        outs = [jax.ShapeDtypeStruct((rows, hid), jnp.bfloat16)]
-        outs += [jax.ShapeDtypeStruct((len(give), rows // 2, width), jnp.bfloat16)] * 2
+        outs = [
+            jax.ShapeDtypeStruct((rows, hid), jnp.bfloat16),
+            jax.ShapeDtypeStruct((len(give), rows - cut, width), jnp.bfloat16),
+        ]
     else:
         outs = [jax.ShapeDtypeStruct((rows, hid), jnp.float32)] * 2
     extra = [w_down] if give else []
-    return pl.pallas_call(
-        functools.partial(gate_up_kernel, picks, give, fresh),
+    xs = [x for item in items for x in (item[0], item[2])]
+    places = [item[1] for item in items]
+    return pl.pallas_call(
+        functools.partial(gate_up_kernel, picks, places, give, fresh),
         out_shape=outs,
-        in_specs=whole(4 + len(extra) + len(held)),
+        in_specs=whole(2 + len(extra) + len(xs) + len(held)),
         out_specs=whole(len(outs)),
         compiler_params=params(16),
         cost_estimate=pl.CostEstimate(
-            flops=4 * rows * width * hid * count,
-            bytes_accessed=4 * hid * width * count,
+            flops=rows * width * hid * count // 16,
+            bytes_accessed=0,
             transcendentals=0,
         ),
         name="gate_up",
-    )(w_gate, w_up, *extra, *halves, *held)
-
-
-def down_kernel(give, keep, down_ref, hidden_ref, *outs):
+    )(w_gate, w_up, *extra, *xs, *held)
+
+
+def down_kernel(give, near, keep, down_ref, hidden_ref, *outs):
     hidden = hidden_ref[...]
+    rows = outs[-2].shape[1]
+    outs = list(outs)
     if give:
         split(hidden, give, down_ref, outs[:2])
-    split(hidden, keep, down_ref, outs[-2:])
-
-
-def down(hidden, give, keep, w_down, width):
+        outs = outs[2:]
+    if near:
+        split(hidden[:rows], near, down_ref, outs[:1])
+        outs = outs[1:]
+    split(hidden, keep, down_ref, outs)
+
+
+def down(hidden, give, near, keep, w_down, width, cut):
     rows, hid = hidden.shape
-    count = len(give) + len(keep)
+    count = len(give) + len(near) + len(keep)
+    sizes = (cut, rows - cut)
     outs = []
     if give:
-        outs += [jax.ShapeDtypeStruct((len(give), rows // 2, width), jnp.bfloat16)] * 2
-    outs += [jax.ShapeDtypeStruct((len(keep), rows // 2, width), jnp.float32)] * 2
-    return pl.pallas_call(
-        functools.partial(down_kernel, give, keep),
+        outs += [jax.ShapeDtypeStruct((len(give), n, width), jnp.bfloat16) for n in sizes]
+    if near:
+        outs += [jax.ShapeDtypeStruct((len(near), cut, width), jnp.bfloat16)]
+    outs += [jax.ShapeDtypeStruct((len(keep), n, width), jnp.float32) for n in sizes]
+    return pl.pallas_call(
+        functools.partial(down_kernel, give, near, keep),
         out_shape=outs,
         in_specs=whole(2),
         out_specs=whole(len(outs)),
@@ -323,43 +329,53 @@
     top = stages - 1
 
     ids = expert_ids.T
-    outgoing = route(stashed, ids, experts, capacity)
+    pick = select(ids, experts, capacity)
+    outgoing = route(stashed, pick, experts, capacity)
     arrived = [outgoing[0]]
     for j in range(1, experts):
         arrived.append(across(outgoing[j], j))
-    high, low = mixer(ids, combine_weight.T, experts, capacity)
+    high, low = mixer(pick, ids, combine_weight.T, capacity)
+
+    last = subsets - 1
+    x = arrived[0][None]
+    first, first_moved = [], []
+    for stage in range(stages):
+        got = hop(x, stage)
+        x = jnp.concatenate([x, got], axis=0)
+        first.append(x if stage == 0 else got)
+        first_moved.append(swap(first[-1]))
+    pieces = [jnp.concatenate(arrived[1:], axis=0)]
+    for stage in range(stages):
+        for k in range(1 << stage):
+            pieces.append(hop(pieces[k], stage))
+    moved = []
+    for piece in pieces:
+        moved.append(swap(piece))
+
+    sums = None
+    for k in range(subsets):
+        b = max(k.bit_length() - 1, 0)
+        place = k - batches[b][0]
+        here, there = (first[b], place, pieces[k]), (first_moved[b], place, moved[k])
+        if k < last:
+            sums = gate_up([here, there], [mine[k], theirs[k]], w_gate, w_up, sums)
+        else:
+            sums = gate_up([here], [mine[k]], w_gate, w_up, sums)
 
     near = experts // 2
-    own, other = [], []
-    for h in (0, 1):
-        x = jnp.concatenate(arrived[h * near : (h + 1) * near], axis=0)[None]
-        made, moved = [], []
-        for stage in range(stages):
-            got = hop(x, stage)
-            x = jnp.concatenate([x, got], axis=0)
-            made.append(x if stage == 0 else got)
-            moved.append(swap(made[-1]))
-        own.append(made)
-        other.append(moved)
-
-    sums = None
-    for b, batch in enumerate(batches):
-        sums = gate_up(
-            [own[0][b], own[1][b]], [mine[k] for k in batch], w_gate, w_up, sums
-        )
-        halves, picks = [other[0][b], other[1][b]], [theirs[k] for k in batch]
-        if b < top:
-            sums = gate_up(halves, picks, w_gate, w_up, sums)
-    hidden, *given = gate_up(halves, picks, w_gate, w_up, sums, w_down, picks)
+    cut = near * capacity
+    give = [theirs[k] for k in batches[top]]
+    hidden, far_given = gate_up([there], [theirs[last]], w_gate, w_up, sums, w_down, give, cut)
 
     totals = [[None] * subsets, [None] * subsets]
     for b in reversed(range(stages)):
         keep = [mine[k] for k in batches[b]]
         if b == top:
-            kept = down(hidden, [], keep, w_down, width)
+            near_given, *kept = down(hidden, [], give, keep, w_down, width, cut)
+            given = [near_given, far_given]
         else:
             give = [theirs[k] for k in batches[b]]
-            *given, kept0, kept1 = down(hidden, give, keep, w_down, width)
+            *given, kept0, kept1 = down(hidden, give, [], keep, w_down, width, cut)
             kept = [kept0, kept1]
         for h in (1, 0):
             got = swap(given[h])
@@ -373,7 +389,8 @@
             sent = jnp.stack(total[1 << stage :]).astype(jnp.bfloat16)
             got = hop(sent, stage)
             totals[h] = [t + got[i].astype(jnp.float32) for i, t in enumerate(total[: 1 << stage])]
-    result = [half[0].astype(jnp.bfloat16) for half in totals]
+            if stage == 0:
+                result[h] = totals[h][0].astype(jnp.bfloat16)
     parts = [
         result[j // near][j % near * capacity : (j % near + 1) * capacity]
         for j in range(experts)

time: 65 us -> 58.8 us (0.905)
  local copies, waits for them, and re-layouts: 6.98 us -> 1.48 us
  starting transfers between devices: 19.7 us -> 22.3 us
  Pallas kernels: 10.8 us -> 9.5 us
  waiting for transfers between devices: 25.7 us -> 24.6 us
  other arithmetic: 1.38 us -> 0.46 us
    unnamed x12 -> x18, local copies, waits for them, and re-layouts: 6.95 us -> 1.45 us
    ppermute x8 -> x9, starting transfers between devices: 8.66 us -> 11.8 us  [hop(): return lax.ppermute(value, 'tensor', pairs)]
    ppermute x8 -> x9, waiting for transfers between devices: 16.7 us -> 14.1 us  [hop(): return lax.ppermute(value, 'tensor', pairs)]
    ppermute x6, waiting for transfers between devices: 9 us -> 10.5 us  [across(): return lax.ppermute(value, 'expert', [(i, i ^ by) for i in range(experts)])]
    pallas_call x8 -> x10, Pallas kernels: 9.92 us -> 8.64 us  [the longest x5 5.82 us: gate_up(): pl.pallas_call(functools.partial(gate_up_kernel, picks, places, give, fre...]
    broadcast_in_dim x2 -> x0, other arithmetic: 0.86 us -> none  [shards(): x = jnp.concatenate(arrived[h * near:(h + 1) * near], axis=0)[None]]
    ppermute x6, starting transfers between devices: 9.32 us -> 8.49 us  [across(): return lax.ppermute(value, 'expert', [(i, i ^ by) for i in range(experts)])]
    ppermute x8 -> x10, starting transfers between devices: 1.7 us -> 2.06 us  [swap(): return lax.ppermute(value, 'tensor', [(i, i ^ 1) for i in range(tensor)])]
  transfers between devices with their start and end apart: 22 -> 25, of which waited for: 13 -> 12; matrix products, arithmetic and copies ran while one was open for 2% -> 1% of each run, Pallas kernels for 10% -> 12%
where the time goes in v4:
time: 58.8 us; the launch traced here: 58.7 us
  waiting for transfers between devices  24.6 us (42%)
  starting transfers between devices  22.3 us (38%)
  Pallas kernels  9.5 us (16%)
  local copies, waits for them, and re-layouts  1.48 us (3%)
    ppermute x9, waiting for transfers between devices, hop(): return lax.ppermute(value, 'tensor', pairs)  14.1 us
    ppermute x9, starting transfers between devices, hop(): return lax.ppermute(value, 'tensor', pairs)  11.8 us
    ppermute x6, waiting for transfers between devices, across(): return lax.ppermute(value, 'expert', [(i, i ^ by) for i in range(experts)])  10.5 us
    ppermute x6, starting transfers between devices, across(): return lax.ppermute(value, 'expert', [(i, i ^ by) for i in range(experts)])  8.49 us
    pallas_call x5, Pallas kernels, gate_up(): pl.pallas_call(functools.partial(gate_up_kernel, picks, places, give, fre...  5.82 us
    pallas_call x2, Pallas kernels, down(): pl.pallas_call(functools.partial(down_kernel, give, near, keep), out_shap...  2.25 us
    ppermute x10, starting transfers between devices, swap(): return lax.ppermute(value, 'tensor', [(i, i ^ 1) for i in range(tensor)])  2.06 us
    unnamed x18, local copies, waits for them, and re-layouts  1.45 us
  transfers between devices with their start and end apart: 25, of which 12 were waited for; matrix products, arithmetic and copies ran while one was open for 1% of the time, Pallas kernels for 12%

profile of v4, /device:TPU:0, one launch (start us, length us, event | category | flops | bytes accessed | tf_op | source)
XLA Modules:
  0.0 58.7 jit_solution(7603169655492788986)
XLA Ops:
  0.0 0.7 %copy-done.3 = s32[96,2]{0,1:T(2,128)S(1)} copy-done((s32[96,2]{0,1:T(2,128)S(1)}, s32[96,2]{0,1:T(2,128)}, u32[]{:S(2)}) %copy-start.3) | copy-done | bytes 792
  0.8 0.7 %copy-done.2 = bf16[96,512]{1,0:T(8,128)(2,1)S(1)} copy-done((bf16[96,512]{1,0:T(8,128)(2,1)S(1)}, bf16[96,512]{1,0:T(8,128)(2,1)}, u32[]{:S(2)}) %copy-start.2) | copy-done | bytes 98328
  1.8 3.1 %collective-permute-start.3 = (bf16[64,512]{1,0:T(8,128)(2,1)S(1)}, bf16[64,512]{1,0:T(8,128)(2,1)S(1)}, u32[]{:S(2)}, u32[]{:S(2)}) collective-permute-start(bf16[64,512]{1,0:T(8,128)(2,1)S(1)} %get-tuple-element.31), channel_id=1, source_target_pairs={{0,8},{8,0},{16,24},{24,16},{1,9},{9,1},{17,25},{25,17},{2,10},{10... | collective-permute-start | bytes 196616 | tf_op jit(solution)/shard_map/ppermute | solution.py:312
  4.9 2.6 %collective-permute-start.4 = (bf16[64,512]{1,0:T(8,128)(2,1)S(1)}, bf16[64,512]{1,0:T(8,128)(2,1)S(1)}, u32[]{:S(2)}, u32[]{:S(2)}) collective-permute-start(bf16[64,512]{1,0:T(8,128)(2,1)S(1)} %get-tuple-element.32), channel_id=1, source_target_pairs={{0,16},{8,24},{16,0},{24,8},{1,17},{9,25},{17,1},{25,9},{2,18},{10... | collective-permute-start | bytes 196616 | tf_op jit(solution)/shard_map/ppermute | solution.py:312
  7.5 4.7 %collective-permute-done.4 = bf16[64,512]{1,0:T(8,128)(2,1)S(1)} collective-permute-done((bf16[64,512]{1,0:T(8,128)(2,1)S(1)}, bf16[64,512]{1,0:T(8,128)(2,1)S(1)}, u32[]{:S(2)}, u32[]{:S(2)}) %collective-permute-start.4) | collective-permute-done | bytes 65568 | tf_op jit(solution)/shard_map/ppermute | solution.py:312
  12.2 1.4 %collective-permute-done.5 = bf16[64,512]{1,0:T(8,128)(2,1)S(1)} collective-permute-done((bf16[64,512]{1,0:T(8,128)(2,1)S(1)}, bf16[64,512]{1,0:T(8,128)(2,1)S(1)}, u32[]{:S(2)}, u32[]{:S(2)}) %collective-permute-start.5) | collective-permute-done | bytes 65568 | tf_op jit(solution)/shard_map/ppermute | solution.py:312
  13.6 1.5 %collective-permute-start.6 = (bf16[192,512]{1,0:T(8,128)(2,1)S(1)}, bf16[192,512]{1,0:T(8,128)(2,1)S(1)}, u32[]{:S(2)}, u32[]{:S(2)}) collective-permute-start(bf16[192,512]{1,0:T(8,128)(2,1)S(1)} %constant_dynamic-update-slice_fusion.refs_1_), channel_id=1, source_target_pairs={{0,2},{1,5},{2,0},{3,7},{4,6},{5,1},{6,4},{7,3},{8,10},{9,13},{10,... | collective-permute-start | bytes 589832 | tf_op jit(solution)/shard_map/ppermute | solution.py:319
  15.6 1.5 %collective-permute-start.9 = (bf16[192,512]{1,0:T(8,128)(2,1)S(1)}, bf16[192,512]{1,0:T(8,128)(2,1)S(1)}, u32[]{:S(2)}, u32[]{:S(2)}) collective-permute-start(bf16[192,512]{1,0:T(8,128)(2,1)S(1)} %constant_dynamic-update-slice_fusion.refs_1_), channel_id=1, source_target_pairs={{0,4},{1,3},{2,6},{3,1},{4,0},{5,7},{6,2},{7,5},{8,12},{9,11},{10,... | collective-permute-start | bytes 589832 | tf_op jit(solution)/shard_map/ppermute | solution.py:319
  17.1 4.1 %collective-permute-done.6.refs_1_ = bf16[192,512]{1,0:T(8,128)(2,1)S(1)} collective-permute-done((bf16[192,512]{1,0:T(8,128)(2,1)S(1)}, bf16[192,512]{1,0:T(8,128)(2,1)S(1)}, u32[]{:S(2)}, u32[]{:S(2)}) %collective-permute-start.6) | collective-permute-done | bytes 196640 | tf_op jit(solution)/shard_map/ppermute | solution.py:319
  21.2 1.5 %collective-permute-start.7 = (bf16[192,512]{1,0:T(8,128)(2,1)S(1)}, bf16[192,512]{1,0:T(8,128)(2,1)S(1)}, u32[]{:S(2)}, u32[]{:S(2)}) collective-permute-start(bf16[192,512]{1,0:T(8,128)(2,1)S(1)} %collective-permute-done.6.refs_1_), channel_id=1, source_target_pairs={{0,4},{1,3},{2,6},{3,1},{4,0},{5,7},{6,2},{7,5},{8,12},{9,11},{10,... | collective-permute-start | bytes 589832 | tf_op jit(solution)/shard_map/ppermute | solution.py:319
  22.8 1.5 %collective-permute-start.1 = (bf16[2,64,512]{2,1,0:T(8,128)(2,1)S(1)}, bf16[2,64,512]{2,1,0:T(8,128)(2,1)S(1)}, u32[]{:S(2)}, u32[]{:S(2)}) collective-permute-start(bf16[2,64,512]{2,1,0:T(8,128)(2,1)S(1)} %pad_maximum_fusion.refs_0_), channel_id=1, source_target_pairs={{0,4},{1,3},{2,6},{3,1},{4,0},{5,7},{6,2},{7,5},{8,12},{9,11},{10,... | collective-permute-start | bytes 393224 | tf_op jit(solution)/shard_map/ppermute | solution.py:319
  25.1 1.8 %collective-permute-done.7.refs_1_ = bf16[192,512]{1,0:T(8,128)(2,1)S(1)} collective-permute-done((bf16[192,512]{1,0:T(8,128)(2,1)S(1)}, bf16[192,512]{1,0:T(8,128)(2,1)S(1)}, u32[]{:S(2)}, u32[]{:S(2)}) %collective-permute-start.7) | collective-permute-done | bytes 196640 | tf_op jit(solution)/shard_map/ppermute | solution.py:319
  26.9 1.4 %collective-permute-done.1.refs_0_ = bf16[2,64,512]{2,1,0:T(8,128)(2,1)S(1)} collective-permute-done((bf16[2,64,512]{2,1,0:T(8,128)(2,1)S(1)}, bf16[2,64,512]{2,1,0:T(8,128)(2,1)S(1)}, u32[]{:S(2)}, u32[]{:S(2)}) %collective-permute-start.1) | collective-permute-done | bytes 131104 | tf_op jit(solution)/shard_map/ppermute | solution.py:319
  28.3 1.3 %gate_up.5 = (f32[256,896]{1,0:T(8,128)S(1)}, f32[256,896]{1,0:T(8,128)S(1)}) custom-call(bf16[1,896,4096]{2,1,0:T(8,128)(2,1)S(1)} %copy-done, bf16[1,896,4096]{2,1,0:T(8,128)(2,1)S(1)} %copy-done.1, bf16[2,64,512]{2,1,0:T(8,128)(2,1)S(1)} %pad_maximum_fusion.refs_0_, bf16[192,512]{1,0:T(8,128)(2,1)S(1)} %constant_dynamic-update-slice_fusion.refs_1_, ...), custom_call_target="tpu_custom_call" | custom-call | flops 14680064 | tf_op jit(solution)/shard_map/gate_up/pallas_call | solution.py:223
  29.6 1.3 %gate_up.6 = (f32[256,896]{1,0:T(8,128)S(1)}, f32[256,896]{1,0:T(8,128)S(1)}) custom-call(bf16[1,896,4096]{2,1,0:T(8,128)(2,1)S(1)} %copy-done, bf16[1,896,4096]{2,1,0:T(8,128)(2,1)S(1)} %copy-done.1, bf16[2,64,512]{2,1,0:T(8,128)(2,1)S(1)} %pad_maximum_fusion.refs_0_, bf16[192,512]{1,0:T(8,128)(2,1)S(1)} %collective-permute-done.6.refs_1_, ...), custom_call_target="tpu_custom_call" | custom-call | flops 14680064 | tf_op jit(solution)/shard_map/gate_up/pallas_call | solution.py:223
  31.0 1.3 %gate_up.7 = (f32[256,896]{1,0:T(8,128)S(1)}, f32[256,896]{1,0:T(8,128)S(1)}) custom-call(bf16[1,896,4096]{2,1,0:T(8,128)(2,1)S(1)} %copy-done, bf16[1,896,4096]{2,1,0:T(8,128)(2,1)S(1)} %copy-done.1, bf16[2,64,512]{2,1,0:T(8,128)(2,1)S(1)} %collective-permute-done.1.refs_0_, bf16[192,512]{1,0:T(8,128)(2,1)S(1)} %collective-permute-done.9.refs_1_, ...), custom_call_target="tpu_custom_call" | custom-call | flops 14680064 | tf_op jit(solution)/shard_map/gate_up/pallas_call | solution.py:223
  32.3 0.8 %gate_up.8 = (f32[256,896]{1,0:T(8,128)S(1)}, f32[256,896]{1,0:T(8,128)S(1)}) custom-call(bf16[1,896,4096]{2,1,0:T(8,128)(2,1)S(1)} %copy-done, bf16[1,896,4096]{2,1,0:T(8,128)(2,1)S(1)} %copy-done.1, bf16[2,64,512]{2,1,0:T(8,128)(2,1)S(1)} %collective-permute-done.1.refs_0_, bf16[192,512]{1,0:T(8,128)(2,1)S(1)} %collective-permute-done.7.refs_1_, ...), custom_call_target="tpu_custom_call" | custom-call | flops 7340032 | tf_op jit(solution)/shard_map/gate_up/pallas_call | solution.py:223
  33.1 1.2 %gate_up.9 = (bf16[256,896]{1,0:T(8,128)(2,1)S(1)}, bf16[2,128,512]{2,1,0:T(8,128)(2,1)S(1)}) custom-call(bf16[1,896,4096]{2,1,0:T(8,128)(2,1)S(1)} %copy-done, bf16[1,896,4096]{2,1,0:T(8,128)(2,1)S(1)} %copy-done.1, bf16[1,896,4096]{2,1,0:T(8,128)(2,1)S(1)} %bitcast.12, bf16[2,64,512]{2,1,0:T(8,128)(2,1)S(1)} %collective-permute-done.2.refs_2_.refs_1_, ...), custom_call_target="tpu_custom_call" | custom-call | flops 7340032 | tf_op jit(solution)/shard_map/gate_up/pallas_call | solution.py:223
  34.8 1.0 %down.3 = (bf16[2,128,512]{2,1,0:T(8,128)(2,1)S(1)}, f32[2,128,512]{2,1,0:T(8,128)S(1)}, f32[2,128,512]{2,1,0:T(8,128)S(1)}) custom-call(bf16[1,896,4096]{2,1,0:T(8,128)(2,1)S(1)} %bitcast.12, bf16[256,896]{1,0:T(8,128)(2,1)S(1)} %get-tuple-element.42.hidden_ref), custom_call_target="tpu_custom_call" | custom-call | flops 939524096 | bytes 3670016 | tf_op jit(solution)/shard_map/down/pallas_call | solution.py:261
  35.9 1.3 %down.2 = (bf16[2,128,512]{2,1,0:T(8,128)(2,1)S(1)}, bf16[2,128,512]{2,1,0:T(8,128)(2,1)S(1)}, f32[2,128,512]{2,1,0:T(8,128)S(1)}, f32[2,128,512]{2,1,0:T(8,128)S(1)}) custom-call(bf16[1,896,4096]{2,1,0:T(8,128)(2,1)S(1)} %bitcast.12, bf16[256,896]{1,0:T(8,128)(2,1)S(1)} %get-tuple-element.42.hidden_ref), custom_call_target="tpu_custom_call" | custom-call | flops 939524096 | bytes 3670016 | tf_op jit(solution)/shard_map/down/pallas_call | solution.py:261
  37.9 1.6 %collective-permute-start.21 = (bf16[2,128,512]{2,1,0:T(8,128)(2,1)S(1)}, bf16[2,128,512]{2,1,0:T(8,128)(2,1)S(1)}, u32[]{:S(2)}, u32[]{:S(2)}) collective-permute-start(bf16[2,128,512]{2,1,0:T(8,128)(2,1)S(1)} %add_convert_fusion), channel_id=1, source_target_pairs={{0,4},{1,3},{2,6},{3,1},{4,0},{5,7},{6,2},{7,5},{8,12},{9,11},{10,... | collective-permute-start | bytes 786440 | tf_op jit(solution)/shard_map/ppermute | solution.py:319
  39.5 0.6 collective-permute-start.16
  40.3 4.0 %collective-permute-done.21 = bf16[2,128,512]{2,1,0:T(8,128)(2,1)S(1)} collective-permute-done((bf16[2,128,512]{2,1,0:T(8,128)(2,1)S(1)}, bf16[2,128,512]{2,1,0:T(8,128)(2,1)S(1)}, u32[]{:S(2)}, u32[]{:S(2)}) %collective-permute-start.21) | collective-permute-done | bytes 262176 | tf_op jit(solution)/shard_map/ppermute | solution.py:319
  44.3 1.6 %collective-permute-start.22 = (bf16[1,128,512]{2,1,0:T(8,128)(2,1)S(1)}, bf16[1,128,512]{2,1,0:T(8,128)(2,1)S(1)}, u32[]{:S(2)}, u32[]{:S(2)}) collective-permute-start(bf16[1,128,512]{2,1,0:T(8,128)(2,1)S(1)} %fusion), channel_id=1, source_target_pairs={{0,2},{1,5},{2,0},{3,7},{4,6},{5,1},{6,4},{7,3},{8,10},{9,13},{10,... | collective-permute-start | bytes 393224 | tf_op jit(solution)/shard_map/ppermute | solution.py:319
  45.9 1.8 %collective-permute-done.16 = bf16[2,128,512]{2,1,0:T(8,128)(2,1)S(1)} collective-permute-done((bf16[2,128,512]{2,1,0:T(8,128)(2,1)S(1)}, bf16[2,128,512]{2,1,0:T(8,128)(2,1)S(1)}, u32[]{:S(2)}, u32[]{:S(2)}) %collective-permute-start.16) | collective-permute-done | bytes 262176 | tf_op jit(solution)/shard_map/ppermute | solution.py:319
  47.7 1.6 %collective-permute-start.17 = (bf16[1,128,512]{2,1,0:T(8,128)(2,1)S(1)}, bf16[1,128,512]{2,1,0:T(8,128)(2,1)S(1)}, u32[]{:S(2)}, u32[]{:S(2)}) collective-permute-start(bf16[1,128,512]{2,1,0:T(8,128)(2,1)S(1)} %fusion.3), channel_id=1, source_target_pairs={{0,2},{1,5},{2,0},{3,7},{4,6},{5,1},{6,4},{7,3},{8,10},{9,13},{10,... | collective-permute-start | bytes 393224 | tf_op jit(solution)/shard_map/ppermute | solution.py:319
  49.4 1.8 %collective-permute-start.23 = (bf16[64,512]{1,0:T(8,128)(2,1)S(1)}, bf16[64,512]{1,0:T(8,128)(2,1)S(1)}, u32[]{:S(2)}, u32[]{:S(2)}) collective-permute-start(bf16[64,512]{1,0:T(8,128)(2,1)S(1)} %get-tuple-element.52), channel_id=1, source_target_pairs={{0,16},{8,24},{16,0},{24,8},{1,17},{9,25},{17,1},{25,9},{2,18},{10... | collective-permute-start | bytes 196616 | tf_op jit(solution)/shard_map/ppermute | solution.py:312
  51.2 0.7 %collective-permute-start.24 = (bf16[64,512]{1,0:T(8,128)(2,1)S(1)}, bf16[64,512]{1,0:T(8,128)(2,1)S(1)}, u32[]{:S(2)}, u32[]{:S(2)}) collective-permute-start(bf16[64,512]{1,0:T(8,128)(2,1)S(1)} %get-tuple-element.51), channel_id=1, source_target_pairs={{0,24},{8,16},{16,8},{24,0},{1,25},{9,17},{17,9},{25,1},{2,26},{10... | collective-permute-start | bytes 196616 | tf_op jit(solution)/shard_map/ppermute | solution.py:312
  51.9 0.8 %collective-permute-done.17 = bf16[1,128,512]{2,1,0:T(8,128)(2,1)S(1)} collective-permute-done((bf16[1,128,512]{2,1,0:T(8,128)(2,1)S(1)}, bf16[1,128,512]{2,1,0:T(8,128)(2,1)S(1)}, u32[]{:S(2)}, u32[]{:S(2)}) %collective-permute-start.17) | collective-permute-done | bytes 131104 | tf_op jit(solution)/shard_map/ppermute | solution.py:319
  53.3 2.6 %collective-permute-done.23.refs_2_ = bf16[64,512]{1,0:T(8,128)(2,1)S(1)} collective-permute-done((bf16[64,512]{1,0:T(8,128)(2,1)S(1)}, bf16[64,512]{1,0:T(8,128)(2,1)S(1)}, u32[]{:S(2)}, u32[]{:S(2)}) %collective-permute-start.23) | collective-permute-done | bytes 65568 | tf_op jit(solution)/shard_map/ppermute | solution.py:312
  55.9 1.5 %collective-permute-done.24.refs_3_ = bf16[64,512]{1,0:T(8,128)(2,1)S(1)} collective-permute-done((bf16[64,512]{1,0:T(8,128)(2,1)S(1)}, bf16[64,512]{1,0:T(8,128)(2,1)S(1)}, u32[]{:S(2)}, u32[]{:S(2)}) %collective-permute-start.24) | collective-permute-done | bytes 65568 | tf_op jit(solution)/shard_map/ppermute | solution.py:312
  57.8 0.9 %combine.1 = bf16[96,512]{1,0:T(8,128)(2,1)} custom-call(bf16[96,256]{1,0:T(8,128)(2,1)S(1)} %get-tuple-element.28.high_ref, bf16[96,256]{1,0:T(8,128)(2,1)S(1)} %get-tuple-element.29.low_ref, bf16[64,512]{1,0:T(8,128)(2,1)S(1)} %get-tuple-element.54.refs_0_, bf16[64,512]{1,0:T(8,128)(2,1)S(1)} %collective-permute-done.18.refs_1_, ...), custom_call_target="tpu_custom_call" | custom-call | tf_op jit(solution)/shard_map/combine/pallas_call | solution.py:285
  (60 shorter events, 4.7 us)
Async XLA Ops:
  0.7 0.9 %copy-start.2 = (bf16[96,512]{1,0:T(8,128)(2,1)S(1)}, bf16[96,512]{1,0:T(8,128)(2,1)}, u32[]{:S(2)}) copy-start(bf16[96,512]{1,0:T(8,128)(2,1)} %x_ref.1) | copy-start | bytes 294916
  0.7 27.6 %copy-start = (bf16[1,896,4096]{2,1,0:T(8,128)(2,1)S(1)}, bf16[1,896,4096]{2,1,0:T(8,128)(2,1)}, u32[]{:S(2)}) copy-start(bf16[1,896,4096]{2,1,0:T(8,128)(2,1)} %gate_ref.9) | copy-start | bytes 22020100
  0.7 27.6 %copy-start.1 = (bf16[1,896,4096]{2,1,0:T(8,128)(2,1)S(1)}, bf16[1,896,4096]{2,1,0:T(8,128)(2,1)}, u32[]{:S(2)}) copy-start(bf16[1,896,4096]{2,1,0:T(8,128)(2,1)} %up_ref.9) | copy-start | bytes 22020100
  1.8 5.7 %collective-permute-start.3 = (bf16[64,512]{1,0:T(8,128)(2,1)S(1)}, bf16[64,512]{1,0:T(8,128)(2,1)S(1)}, u32[]{:S(2)}, u32[]{:S(2)}) collective-permute-start(bf16[64,512]{1,0:T(8,128)(2,1)S(1)} %get-tuple-element.31), channel_id=1, source_target_pairs={{0,8},{8,0},{16,24},{24,16},{1,9},{9,1},{17,25},{25,17},{2,10},{10... | collective-permute-start | bytes 196616 | tf_op jit(solution)/shard_map/ppermute | solution.py:312
  4.9 7.3 %collective-permute-start.4 = (bf16[64,512]{1,0:T(8,128)(2,1)S(1)}, bf16[64,512]{1,0:T(8,128)(2,1)S(1)}, u32[]{:S(2)}, u32[]{:S(2)}) collective-permute-start(bf16[64,512]{1,0:T(8,128)(2,1)S(1)} %get-tuple-element.32), channel_id=1, source_target_pairs={{0,16},{8,24},{16,0},{24,8},{1,17},{9,25},{17,1},{25,9},{2,18},{10... | collective-permute-start | bytes 196616 | tf_op jit(solution)/shard_map/ppermute | solution.py:312
  7.5 6.1 %collective-permute-start.5 = (bf16[64,512]{1,0:T(8,128)(2,1)S(1)}, bf16[64,512]{1,0:T(8,128)(2,1)S(1)}, u32[]{:S(2)}, u32[]{:S(2)}) collective-permute-start(bf16[64,512]{1,0:T(8,128)(2,1)S(1)} %get-tuple-element.33), channel_id=1, source_target_pairs={{0,24},{8,16},{16,8},{24,0},{1,25},{9,17},{17,9},{25,1},{2,26},{10... | collective-permute-start | bytes 196616 | tf_op jit(solution)/shard_map/ppermute | solution.py:312
  13.6 7.6 %collective-permute-start.6 = (bf16[192,512]{1,0:T(8,128)(2,1)S(1)}, bf16[192,512]{1,0:T(8,128)(2,1)S(1)}, u32[]{:S(2)}, u32[]{:S(2)}) collective-permute-start(bf16[192,512]{1,0:T(8,128)(2,1)S(1)} %constant_dynamic-update-slice_fusion.refs_1_), channel_id=1, source_target_pairs={{0,2},{1,5},{2,0},{3,7},{4,6},{5,1},{6,4},{7,3},{8,10},{9,13},{10,... | collective-permute-start | bytes 589832 | tf_op jit(solution)/shard_map/ppermute | solution.py:319
  15.1 7.7 %collective-permute-start = (bf16[1,64,512]{2,1,0:T(8,128)(2,1)S(1)}, bf16[1,64,512]{2,1,0:T(8,128)(2,1)S(1)}, u32[]{:S(2)}, u32[]{:S(2)}) collective-permute-start(bf16[1,64,512]{2,1,0:T(8,128)(2,1)S(1)} %bitcast.13), channel_id=1, source_target_pairs={{0,2},{1,5},{2,0},{3,7},{4,6},{5,1},{6,4},{7,3},{8,10},{9,13},{10,... | collective-permute-start | bytes 196616 | tf_op jit(solution)/shard_map/ppermute | solution.py:319
  15.6 9.2 %collective-permute-start.9 = (bf16[192,512]{1,0:T(8,128)(2,1)S(1)}, bf16[192,512]{1,0:T(8,128)(2,1)S(1)}, u32[]{:S(2)}, u32[]{:S(2)}) collective-permute-start(bf16[192,512]{1,0:T(8,128)(2,1)S(1)} %constant_dynamic-update-slice_fusion.refs_1_), channel_id=1, source_target_pairs={{0,4},{1,3},{2,6},{3,1},{4,0},{5,7},{6,2},{7,5},{8,12},{9,11},{10,... | collective-permute-start | bytes 589832 | tf_op jit(solution)/shard_map/ppermute | solution.py:319
  21.2 5.7 %collective-permute-start.7 = (bf16[192,512]{1,0:T(8,128)(2,1)S(1)}, bf16[192,512]{1,0:T(8,128)(2,1)S(1)}, u32[]{:S(2)}, u32[]{:S(2)}) collective-permute-start(bf16[192,512]{1,0:T(8,128)(2,1)S(1)} %collective-permute-done.6.refs_1_), channel_id=1, source_target_pairs={{0,4},{1,3},{2,6},{3,1},{4,0},{5,7},{6,2},{7,5},{8,12},{9,11},{10,... | collective-permute-start | bytes 589832 | tf_op jit(solution)/shard_map/ppermute | solution.py:319
  22.8 1.8 %collective-permute-start.11 = (bf16[2,64,512]{2,1,0:T(8,128)(2,1)S(1)}, bf16[2,64,512]{2,1,0:T(8,128)(2,1)S(1)}, u32[]{:S(2)}, u32[]{:S(2)}) collective-permute-start(bf16[2,64,512]{2,1,0:T(8,128)(2,1)S(1)} %pad_maximum_fusion.refs_0_), channel_id=1, source_target_pairs={{0,1},{1,0},{2,3},{3,2},{4,5},{5,4},{6,7},{7,6},{8,9},{9,8},{10,11... | collective-permute-start | bytes 393224 | tf_op jit(solution)/shard_map/ppermute | solution.py:315
  22.8 5.5 %collective-permute-start.1 = (bf16[2,64,512]{2,1,0:T(8,128)(2,1)S(1)}, bf16[2,64,512]{2,1,0:T(8,128)(2,1)S(1)}, u32[]{:S(2)}, u32[]{:S(2)}) collective-permute-start(bf16[2,64,512]{2,1,0:T(8,128)(2,1)S(1)} %pad_maximum_fusion.refs_0_), channel_id=1, source_target_pairs={{0,4},{1,3},{2,6},{3,1},{4,0},{5,7},{6,2},{7,5},{8,12},{9,11},{10,... | collective-permute-start | bytes 393224 | tf_op jit(solution)/shard_map/ppermute | solution.py:319
  24.3 4.0 %collective-permute-start.13 = (bf16[192,512]{1,0:T(8,128)(2,1)S(1)}, bf16[192,512]{1,0:T(8,128)(2,1)S(1)}, u32[]{:S(2)}, u32[]{:S(2)}) collective-permute-start(bf16[192,512]{1,0:T(8,128)(2,1)S(1)} %constant_dynamic-update-slice_fusion.refs_1_), channel_id=1, source_target_pairs={{0,1},{1,0},{2,3},{3,2},{4,5},{5,4},{6,7},{7,6},{8,9},{9,8},{10,11... | collective-permute-start | bytes 589832 | tf_op jit(solution)/shard_map/ppermute | solution.py:315
  24.6 5.1 %collective-permute-start.12 = (bf16[192,512]{1,0:T(8,128)(2,1)S(1)}, bf16[192,512]{1,0:T(8,128)(2,1)S(1)}, u32[]{:S(2)}, u32[]{:S(2)}) collective-permute-start(bf16[192,512]{1,0:T(8,128)(2,1)S(1)} %collective-permute-done.6.refs_1_), channel_id=1, source_target_pairs={{0,1},{1,0},{2,3},{3,2},{4,5},{5,4},{6,7},{7,6},{8,9},{9,8},{10,11... | collective-permute-start | bytes 589832 | tf_op jit(solution)/shard_map/ppermute | solution.py:315
  24.8 6.1 %collective-permute-start.10 = (bf16[192,512]{1,0:T(8,128)(2,1)S(1)}, bf16[192,512]{1,0:T(8,128)(2,1)S(1)}, u32[]{:S(2)}, u32[]{:S(2)}) collective-permute-start(bf16[192,512]{1,0:T(8,128)(2,1)S(1)} %collective-permute-done.9.refs_1_), channel_id=1, source_target_pairs={{0,1},{1,0},{2,3},{3,2},{4,5},{5,4},{6,7},{7,6},{8,9},{9,8},{10,11... | collective-permute-start | bytes 589832 | tf_op jit(solution)/shard_map/ppermute | solution.py:315
  26.9 6.2 %collective-permute-start.8 = (bf16[192,512]{1,0:T(8,128)(2,1)S(1)}, bf16[192,512]{1,0:T(8,128)(2,1)S(1)}, u32[]{:S(2)}, u32[]{:S(2)}) collective-permute-start(bf16[192,512]{1,0:T(8,128)(2,1)S(1)} %collective-permute-done.7.refs_1_), channel_id=1, source_target_pairs={{0,1},{1,0},{2,3},{3,2},{4,5},{5,4},{6,7},{7,6},{8,9},{9,8},{10,11... | collective-permute-start | bytes 589832 | tf_op jit(solution)/shard_map/ppermute | solution.py:315
  28.3 2.7 %collective-permute-start.2 = (bf16[2,64,512]{2,1,0:T(8,128)(2,1)S(1)}, bf16[2,64,512]{2,1,0:T(8,128)(2,1)S(1)}, u32[]{:S(2)}, u32[]{:S(2)}) collective-permute-start(bf16[2,64,512]{2,1,0:T(8,128)(2,1)S(1)} %collective-permute-done.1.refs_0_), channel_id=1, source_target_pairs={{0,1},{1,0},{2,3},{3,2},{4,5},{5,4},{6,7},{7,6},{8,9},{9,8},{10,11... | collective-permute-start | bytes 393224 | tf_op jit(solution)/shard_map/ppermute | solution.py:315
  29.6 3.4 %slice-start = ((s8[7340032]{0:T(1024)(128)(4,1)}), s8[4194304]{0:T(1024)(128)(4,1)S(1)}, s32[]{:S(2)}) async-start(s8[7340032]{0:T(1024)(128)(4,1)} %bitcast.11), calls=%async_computation | async-start | bytes 8388608
  31.0 2.1 %slice-start.1 = ((s8[7340032]{0:T(1024)(128)(4,1)}), s8[3145728]{0:T(1024)(128)(4,1)S(1)}, s32[]{:S(2)}) async-start(s8[7340032]{0:T(1024)(128)(4,1)} %bitcast.11), calls=%async_computation.1 | async-start | bytes 6291456
  34.3 3.5 %collective-permute-start.20 = (bf16[2,128,512]{2,1,0:T(8,128)(2,1)S(1)}, bf16[2,128,512]{2,1,0:T(8,128)(2,1)S(1)}, u32[]{:S(2)}, u32[]{:S(2)}) collective-permute-start(bf16[2,128,512]{2,1,0:T(8,128)(2,1)S(1)} %get-tuple-element.50), channel_id=1, source_target_pairs={{0,1},{1,0},{2,3},{3,2},{4,5},{5,4},{6,7},{7,6},{8,9},{9,8},{10,11... | collective-permute-start | bytes 786440 | tf_op jit(solution)/shard_map/ppermute | solution.py:315
  35.8 17.4 %copy-start.4 = (s32[96,2]{0,1:T(2,128)S(1)}, s32[96,2]{0,1:T(2,128)}, u32[]{:S(2)}) copy-start(s32[96,2]{0,1:T(2,128)} %param.7) | copy-start | bytes 2308
  35.8 17.4 %copy-start.5 = (f32[96,2]{0,1:T(2,128)S(1)}, f32[96,2]{0,1:T(2,128)}, u32[]{:S(2)}) copy-start(f32[96,2]{0,1:T(2,128)} %param.8) | copy-start | bytes 2308
  35.8 3.7 %collective-permute-start.15 = (bf16[2,128,512]{2,1,0:T(8,128)(2,1)S(1)}, bf16[2,128,512]{2,1,0:T(8,128)(2,1)S(1)}, u32[]{:S(2)}, u32[]{:S(2)}) collective-permute-start(bf16[2,128,512]{2,1,0:T(8,128)(2,1)S(1)} %get-tuple-element.46), channel_id=1, source_target_pairs={{0,1},{1,0},{2,3},{3,2},{4,5},{5,4},{6,7},{7,6},{8,9},{9,8},{10,11... | collective-permute-start | bytes 786440 | tf_op jit(solution)/shard_map/ppermute | solution.py:315
  37.2 2.9 %collective-permute-start.19 = (bf16[2,128,512]{2,1,0:T(8,128)(2,1)S(1)}, bf16[2,128,512]{2,1,0:T(8,128)(2,1)S(1)}, u32[]{:S(2)}, u32[]{:S(2)}) collective-permute-start(bf16[2,128,512]{2,1,0:T(8,128)(2,1)S(1)} %get-tuple-element.48), channel_id=1, source_target_pairs={{0,1},{1,0},{2,3},{3,2},{4,5},{5,4},{6,7},{7,6},{8,9},{9,8},{10,11... | collective-permute-start | bytes 786440 | tf_op jit(solution)/shard_map/ppermute | solution.py:315
  37.7 2.5 %collective-permute-start.14 = (bf16[2,128,512]{2,1,0:T(8,128)(2,1)S(1)}, bf16[2,128,512]{2,1,0:T(8,128)(2,1)S(1)}, u32[]{:S(2)}, u32[]{:S(2)}) collective-permute-start(bf16[2,128,512]{2,1,0:T(8,128)(2,1)S(1)} %get-tuple-element.44), channel_id=1, source_target_pairs={{0,1},{1,0},{2,3},{3,2},{4,5},{5,4},{6,7},{7,6},{8,9},{9,8},{10,11... | collective-permute-start | bytes 786440 | tf_op jit(solution)/shard_map/ppermute | solution.py:315
  37.9 6.4 %collective-permute-start.21 = (bf16[2,128,512]{2,1,0:T(8,128)(2,1)S(1)}, bf16[2,128,512]{2,1,0:T(8,128)(2,1)S(1)}, u32[]{:S(2)}, u32[]{:S(2)}) collective-permute-start(bf16[2,128,512]{2,1,0:T(8,128)(2,1)S(1)} %add_convert_fusion), channel_id=1, source_target_pairs={{0,4},{1,3},{2,6},{3,1},{4,0},{5,7},{6,2},{7,5},{8,12},{9,11},{10,... | collective-permute-start | bytes 786440 | tf_op jit(solution)/shard_map/ppermute | solution.py:319
  39.5 8.1 %collective-permute-start.16 = (bf16[2,128,512]{2,1,0:T(8,128)(2,1)S(1)}, bf16[2,128,512]{2,1,0:T(8,128)(2,1)S(1)}, u32[]{:S(2)}, u32[]{:S(2)}) collective-permute-start(bf16[2,128,512]{2,1,0:T(8,128)(2,1)S(1)} %add_convert_fusion.1), channel_id=1, source_target_pairs={{0,4},{1,3},{2,6},{3,1},{4,0},{5,7},{6,2},{7,5},{8,12},{9,11},{10,... | collective-permute-start | bytes 786440 | tf_op jit(solution)/shard_map/ppermute | solution.py:319
  44.3 5.0 %collective-permute-start.22 = (bf16[1,128,512]{2,1,0:T(8,128)(2,1)S(1)}, bf16[1,128,512]{2,1,0:T(8,128)(2,1)S(1)}, u32[]{:S(2)}, u32[]{:S(2)}) collective-permute-start(bf16[1,128,512]{2,1,0:T(8,128)(2,1)S(1)} %fusion), channel_id=1, source_target_pairs={{0,2},{1,5},{2,0},{3,7},{4,6},{5,1},{6,4},{7,3},{8,10},{9,13},{10,... | collective-permute-start | bytes 393224 | tf_op jit(solution)/shard_map/ppermute | solution.py:319
  47.7 5.0 %collective-permute-start.17 = (bf16[1,128,512]{2,1,0:T(8,128)(2,1)S(1)}, bf16[1,128,512]{2,1,0:T(8,128)(2,1)S(1)}, u32[]{:S(2)}, u32[]{:S(2)}) collective-permute-start(bf16[1,128,512]{2,1,0:T(8,128)(2,1)S(1)} %fusion.3), channel_id=1, source_target_pairs={{0,2},{1,5},{2,0},{3,7},{4,6},{5,1},{6,4},{7,3},{8,10},{9,13},{10,... | collective-permute-start | bytes 393224 | tf_op jit(solution)/shard_map/ppermute | solution.py:319
  49.4 6.5 %collective-permute-start.23 = (bf16[64,512]{1,0:T(8,128)(2,1)S(1)}, bf16[64,512]{1,0:T(8,128)(2,1)S(1)}, u32[]{:S(2)}, u32[]{:S(2)}) collective-permute-start(bf16[64,512]{1,0:T(8,128)(2,1)S(1)} %get-tuple-element.52), channel_id=1, source_target_pairs={{0,16},{8,24},{16,0},{24,8},{1,17},{9,25},{17,1},{25,9},{2,18},{10... | collective-permute-start | bytes 196616 | tf_op jit(solution)/shard_map/ppermute | solution.py:312
  51.2 6.2 %collective-permute-start.24 = (bf16[64,512]{1,0:T(8,128)(2,1)S(1)}, bf16[64,512]{1,0:T(8,128)(2,1)S(1)}, u32[]{:S(2)}, u32[]{:S(2)}) collective-permute-start(bf16[64,512]{1,0:T(8,128)(2,1)S(1)} %get-tuple-element.51), channel_id=1, source_target_pairs={{0,24},{8,16},{16,8},{24,0},{1,25},{9,17},{17,9},{25,1},{2,26},{10... | collective-permute-start | bytes 196616 | tf_op jit(solution)/shard_map/ppermute | solution.py:312
  52.8 5.0 %collective-permute-start.18 = (bf16[64,512]{1,0:T(8,128)(2,1)S(1)}, bf16[64,512]{1,0:T(8,128)(2,1)S(1)}, u32[]{:S(2)}, u32[]{:S(2)}) collective-permute-start(bf16[64,512]{1,0:T(8,128)(2,1)S(1)} %get-tuple-element.53), channel_id=1, source_target_pairs={{0,8},{8,0},{16,24},{24,16},{1,9},{9,1},{17,25},{25,17},{2,10},{10... | collective-permute-start | bytes 196616 | tf_op jit(solution)/shard_map/ppermute | solution.py:312
  (1 other events, 0.7 us)

commit v5 on v4

--- a/solution.py
+++ b/solution.py
@@ -71,16 +71,33 @@
     return combined.astype(jnp.bfloat16)
 
 
-def selection(ids, first_expert, experts, capacity):
+def order_kernel(earlier_ref):
+    down = lax.broadcasted_iota(jnp.int32, earlier_ref.shape, 0)
+    across = lax.broadcasted_iota(jnp.int32, earlier_ref.shape, 1)
+    earlier_ref[...] = jnp.where(down < across, 1.0, 0.0).astype(jnp.bfloat16)
+
+
+def order(tokens):
+    return pl.pallas_call(
+        order_kernel,
+        out_shape=jax.ShapeDtypeStruct((tokens, tokens), jnp.bfloat16),
+        in_specs=[],
+        out_specs=pl.BlockSpec(memory_space=VM),
+        compiler_params=params(8),
+        cost_estimate=pl.CostEstimate(
+            flops=20_000_000_000, bytes_accessed=0, transcendentals=0
+        ),
+        name="order",
+    )()
+
+
+def selection(ids, earlier, first_expert, experts, capacity):
     tokens = ids.shape[1]
     rows = experts * capacity
     row = lax.broadcasted_iota(jnp.int32, (rows, tokens), 0)
     expert = first_expert ^ (row // capacity)
     slot = row % capacity
     named = jnp.logical_or(ids[0:1, :] == expert, ids[1:2, :] == expert)
-    down = lax.broadcasted_iota(jnp.int32, (tokens, tokens), 0)
-    across = lax.broadcasted_iota(jnp.int32, (tokens, tokens), 1)
-    earlier = jnp.where(down < across, 1.0, 0.0).astype(jnp.bfloat16)
     before = jnp.dot(
         jnp.where(named, 1.0, 0.0).astype(jnp.bfloat16),
         earlier,
@@ -89,23 +106,22 @@
     return jnp.logical_and(named, before == slot.astype(jnp.float32))
 
 
-def select_kernel(experts, capacity, ids_ref, pick_ref):
-    chosen = selection(ids_ref[...], lax.axis_index("expert"), experts, capacity)
+def select_kernel(experts, capacity, ids_ref, earlier_ref, pick_ref):
+    chosen = selection(
+        ids_ref[...], earlier_ref[...], lax.axis_index("expert"), experts, capacity
+    )
     pick_ref[...] = jnp.where(chosen, 1.0, 0.0).astype(jnp.bfloat16)
 
 
-def select(ids, experts, capacity):
+def select(ids, earlier, experts, capacity):
     return pl.pallas_call(
         functools.partial(select_kernel, experts, capacity),
         out_shape=jax.ShapeDtypeStruct((experts * capacity, ids.shape[1]), jnp.bfloat16),
-        in_specs=whole(1),
+        in_specs=whole(2),
         out_specs=pl.BlockSpec(memory_space=VM),
         compiler_params=params(8),
-        cost_estimate=pl.CostEstimate(
-            flops=20_000_000_000, bytes_accessed=0, transcendentals=0
-        ),
         name="select",
-    )(ids)
+    )(ids, earlier)
 
 
 def route_kernel(capacity, pick_ref, x_ref, *outs):
@@ -296,9 +312,25 @@
     return min(tokens, 8 * tokens // (3 * experts))
 
 
-def stage_bits(tensor, core):
-    bits = list(range(1, tensor.bit_length() - 1))
-    return bits if core == 0 else bits[::-1]
+def stage_masks(tensor, core):
+    bits = [1 << b for b in range(1, tensor.bit_length() - 1)]
+    bits = bits if core == 0 else bits[::-1]
+    if len(bits) != 2:
+        return bits, bits
+    return [bits[0], bits[1] ^ 1], [bits[0], bits[0] ^ 1]
+
+
+def reach(tensor, core):
+    masks = [0]
+    for mask, turned in zip(*stage_masks(tensor, core)):
+        step = turned if mask == turned else stage_masks(tensor, 1 - core)[0][-1]
+        base = masks if mask == turned else reach_first(tensor, 1 - core)
+        masks = masks + [step ^ m for m in base]
+    return masks
+
+
+def reach_first(tensor, core):
+    return [0, stage_masks(tensor, core)[0][0]]
 
 
 def shards(tensor, stashed, expert_ids, combine_weight, w_gate, w_up, w_down):
@@ -314,22 +346,18 @@
     def swap(value):
         return lax.ppermute(value, "tensor", [(i, i ^ 1) for i in range(tensor)])
 
-    def hop(value, stage):
-        pairs = [(i, i ^ (1 << stage_bits(tensor, i & 1)[stage])) for i in range(tensor)]
+    def hop(value, stage, back=0):
+        pairs = [(i, i ^ stage_masks(tensor, i & 1)[back][stage]) for i in range(tensor)]
         return lax.ppermute(value, "tensor", pairs)
 
-    def reach(core):
-        bits = stage_bits(tensor, core)
-        return [sum(1 << bits[s] for s in range(stages) if k >> s & 1) for k in range(subsets)]
-
-    ahead = list(zip(reach(0), reach(1)))
+    ahead = list(zip(reach(tensor, 0), reach(tensor, 1)))
     mine = [(0, a, b) for a, b in ahead]
     theirs = [(1, b, a) for a, b in ahead]
     batches = [range(0, 2)] + [range(1 << s, 2 << s) for s in range(1, stages)]
     top = stages - 1
 
     ids = expert_ids.T
-    pick = select(ids, experts, capacity)
+    pick = select(ids, order(tokens), experts, capacity)
     outgoing = route(stashed, pick, experts, capacity)
     arrived = [outgoing[0]]
     for j in range(1, experts):
@@ -387,7 +415,7 @@
         for h in (1, 0):
             total = totals[h]
             sent = jnp.stack(total[1 << stage :]).astype(jnp.bfloat16)
-            got = hop(sent, stage)
+            got = hop(sent, stage, 1)
             totals[h] = [t + got[i].astype(jnp.float32) for i, t in enumerate(total[: 1 << stage])]
             if stage == 0:
                 result[h] = totals[h][0].astype(jnp.bfloat16)

time: 58.8 us -> 55.7 us (0.947)
  starting transfers between devices: 22.3 us -> 20.7 us
  waiting for transfers between devices: 24.6 us -> 23.9 us
  local copies, waits for them, and re-layouts: 1.48 us -> 0.79 us
    ppermute x9, starting transfers between devices: 11.8 us -> 9.4 us  [hop(): return lax.ppermute(value, 'tensor', pairs)]
    ppermute x9, waiting for transfers between devices: 14.1 us -> 13.4 us  [hop(): return lax.ppermute(value, 'tensor', pairs)]
    unnamed x18 -> x16, local copies, waits for them, and re-layouts: 1.45 us -> 0.76 us
  transfers between devices with their start and end apart: 25 -> 25, of which waited for: 12 -> 13; matrix products, arithmetic and copies ran while one was open for 1% -> 1% of each run, Pallas kernels for 12% -> 13%
where the time goes in v5:
time: 55.7 us; the launch traced here: 55.6 us
  waiting for transfers between devices  23.9 us (43%)
  starting transfers between devices  20.7 us (37%)
  Pallas kernels  9.48 us (17%)
  local copies, waits for them, and re-layouts  0.79 us (1%)
    ppermute x9, waiting for transfers between devices, hop(): return lax.ppermute(value, 'tensor', pairs)  13.4 us
    ppermute x6, waiting for transfers between devices, across(): return lax.ppermute(value, 'expert', [(i, i ^ by) for i in range(experts)])  10.5 us
    ppermute x9, starting transfers between devices, hop(): return lax.ppermute(value, 'tensor', pairs)  9.4 us
    ppermute x6, starting transfers between devices, across(): return lax.ppermute(value, 'expert', [(i, i ^ by) for i in range(experts)])  8.9 us
    pallas_call x5, Pallas kernels, gate_up(): pl.pallas_call(functools.partial(gate_up_kernel, picks, places, give, fre...  5.78 us
    ppermute x10, starting transfers between devices, swap(): return lax.ppermute(value, 'tensor', [(i, i ^ 1) for i in range(tensor)])  2.38 us
    pallas_call x2, Pallas kernels, down(): pl.pallas_call(functools.partial(down_kernel, give, near, keep), out_shap...  2.26 us
  transfers between devices with their start and end apart: 25, of which 13 were waited for; matrix products, arithmetic and copies ran while one was open for 1% of the time, Pallas kernels for 13%

profile of v5, /device:TPU:0, one launch (start us, length us, event | category | flops | bytes accessed | tf_op | source)
XLA Modules:
  0.0 55.6 jit_solution(16868727249731047499)
XLA Ops:
  0.0 0.7 %copy-done.3 = s32[96,2]{0,1:T(2,128)S(1)} copy-done((s32[96,2]{0,1:T(2,128)S(1)}, s32[96,2]{0,1:T(2,128)}, u32[]{:S(2)}) %copy-start.3) | copy-done | bytes 792
  1.1 3.1 %collective-permute-start.3 = (bf16[64,512]{1,0:T(8,128)(2,1)S(1)}, bf16[64,512]{1,0:T(8,128)(2,1)S(1)}, u32[]{:S(2)}, u32[]{:S(2)}) collective-permute-start(bf16[64,512]{1,0:T(8,128)(2,1)S(1)} %get-tuple-element.31), channel_id=1, source_target_pairs={{0,8},{8,0},{16,24},{24,16},{1,9},{9,1},{17,25},{25,17},{2,10},{10... | collective-permute-start | bytes 196616 | tf_op jit(solution)/shard_map/ppermute | solution.py:344
  4.2 2.6 %collective-permute-start.4 = (bf16[64,512]{1,0:T(8,128)(2,1)S(1)}, bf16[64,512]{1,0:T(8,128)(2,1)S(1)}, u32[]{:S(2)}, u32[]{:S(2)}) collective-permute-start(bf16[64,512]{1,0:T(8,128)(2,1)S(1)} %get-tuple-element.32), channel_id=1, source_target_pairs={{0,16},{8,24},{16,0},{24,8},{1,17},{9,25},{17,1},{25,9},{2,18},{10... | collective-permute-start | bytes 196616 | tf_op jit(solution)/shard_map/ppermute | solution.py:344
  6.8 4.7 %collective-permute-done.4 = bf16[64,512]{1,0:T(8,128)(2,1)S(1)} collective-permute-done((bf16[64,512]{1,0:T(8,128)(2,1)S(1)}, bf16[64,512]{1,0:T(8,128)(2,1)S(1)}, u32[]{:S(2)}, u32[]{:S(2)}) %collective-permute-start.4) | collective-permute-done | bytes 65568 | tf_op jit(solution)/shard_map/ppermute | solution.py:344
  11.5 1.4 %collective-permute-done.5 = bf16[64,512]{1,0:T(8,128)(2,1)S(1)} collective-permute-done((bf16[64,512]{1,0:T(8,128)(2,1)S(1)}, bf16[64,512]{1,0:T(8,128)(2,1)S(1)}, u32[]{:S(2)}, u32[]{:S(2)}) %collective-permute-start.5) | collective-permute-done | bytes 65568 | tf_op jit(solution)/shard_map/ppermute | solution.py:344
  12.9 1.5 %collective-permute-start.6 = (bf16[192,512]{1,0:T(8,128)(2,1)S(1)}, bf16[192,512]{1,0:T(8,128)(2,1)S(1)}, u32[]{:S(2)}, u32[]{:S(2)}) collective-permute-start(bf16[192,512]{1,0:T(8,128)(2,1)S(1)} %constant_dynamic-update-slice_fusion.refs_1_), channel_id=1, source_target_pairs={{0,2},{1,5},{2,0},{3,7},{4,6},{5,1},{6,4},{7,3},{8,10},{9,13},{10,... | collective-permute-start | bytes 589832 | tf_op jit(solution)/shard_map/ppermute | solution.py:351
  14.4 0.5 collective-permute-start
  14.9 4.3 %collective-permute-done.6.refs_1_ = bf16[192,512]{1,0:T(8,128)(2,1)S(1)} collective-permute-done((bf16[192,512]{1,0:T(8,128)(2,1)S(1)}, bf16[192,512]{1,0:T(8,128)(2,1)S(1)}, u32[]{:S(2)}, u32[]{:S(2)}) %collective-permute-start.6) | collective-permute-done | bytes 196640 | tf_op jit(solution)/shard_map/ppermute | solution.py:351
  19.2 1.4 %collective-permute-done = bf16[1,64,512]{2,1,0:T(8,128)(2,1)S(1)} collective-permute-done((bf16[1,64,512]{2,1,0:T(8,128)(2,1)S(1)}, bf16[1,64,512]{2,1,0:T(8,128)(2,1)S(1)}, u32[]{:S(2)}, u32[]{:S(2)}) %collective-permute-start) | collective-permute-done | bytes 65568 | tf_op jit(solution)/shard_map/ppermute | solution.py:351
  20.9 1.4 %collective-permute-start.1 = (bf16[2,64,512]{2,1,0:T(8,128)(2,1)S(1)}, bf16[2,64,512]{2,1,0:T(8,128)(2,1)S(1)}, u32[]{:S(2)}, u32[]{:S(2)}) collective-permute-start(bf16[2,64,512]{2,1,0:T(8,128)(2,1)S(1)} %pad_maximum_fusion.refs_0_), channel_id=1, source_target_pairs={{0,5},{1,2},{2,7},{3,0},{4,1},{5,6},{6,3},{7,4},{8,13},{9,10},{10,... | collective-permute-start | bytes 393224 | tf_op jit(solution)/shard_map/ppermute | solution.py:351
  22.9 1.4 %collective-permute-done.7.refs_1_ = bf16[192,512]{1,0:T(8,128)(2,1)S(1)} collective-permute-done((bf16[192,512]{1,0:T(8,128)(2,1)S(1)}, bf16[192,512]{1,0:T(8,128)(2,1)S(1)}, u32[]{:S(2)}, u32[]{:S(2)}) %collective-permute-start.7) | collective-permute-done | bytes 196640 | tf_op jit(solution)/shard_map/ppermute | solution.py:351
  24.5 1.2 %collective-permute-done.1.refs_0_ = bf16[2,64,512]{2,1,0:T(8,128)(2,1)S(1)} collective-permute-done((bf16[2,64,512]{2,1,0:T(8,128)(2,1)S(1)}, bf16[2,64,512]{2,1,0:T(8,128)(2,1)S(1)}, u32[]{:S(2)}, u32[]{:S(2)}) %collective-permute-start.1) | collective-permute-done | bytes 131104 | tf_op jit(solution)/shard_map/ppermute | solution.py:351
  25.9 1.3 %gate_up.5 = (f32[256,896]{1,0:T(8,128)S(1)}, f32[256,896]{1,0:T(8,128)S(1)}) custom-call(bf16[1,896,4096]{2,1,0:T(8,128)(2,1)S(1)} %copy-done, bf16[1,896,4096]{2,1,0:T(8,128)(2,1)S(1)} %copy-done.1, bf16[2,64,512]{2,1,0:T(8,128)(2,1)S(1)} %pad_maximum_fusion.refs_0_, bf16[192,512]{1,0:T(8,128)(2,1)S(1)} %constant_dynamic-update-slice_fusion.refs_1_, ...), custom_call_target="tpu_custom_call" | custom-call | flops 14680064 | tf_op jit(solution)/shard_map/gate_up/pallas_call | solution.py:239
  27.2 1.3 %gate_up.6 = (f32[256,896]{1,0:T(8,128)S(1)}, f32[256,896]{1,0:T(8,128)S(1)}) custom-call(bf16[1,896,4096]{2,1,0:T(8,128)(2,1)S(1)} %copy-done, bf16[1,896,4096]{2,1,0:T(8,128)(2,1)S(1)} %copy-done.1, bf16[2,64,512]{2,1,0:T(8,128)(2,1)S(1)} %pad_maximum_fusion.refs_0_, bf16[192,512]{1,0:T(8,128)(2,1)S(1)} %collective-permute-done.6.refs_1_, ...), custom_call_target="tpu_custom_call" | custom-call | flops 14680064 | tf_op jit(solution)/shard_map/gate_up/pallas_call | solution.py:239
  28.5 1.3 %gate_up.7 = (f32[256,896]{1,0:T(8,128)S(1)}, f32[256,896]{1,0:T(8,128)S(1)}) custom-call(bf16[1,896,4096]{2,1,0:T(8,128)(2,1)S(1)} %copy-done, bf16[1,896,4096]{2,1,0:T(8,128)(2,1)S(1)} %copy-done.1, bf16[2,64,512]{2,1,0:T(8,128)(2,1)S(1)} %collective-permute-done.1.refs_0_, bf16[192,512]{1,0:T(8,128)(2,1)S(1)} %collective-permute-done.9.refs_1_, ...), custom_call_target="tpu_custom_call" | custom-call | flops 14680064 | tf_op jit(solution)/shard_map/gate_up/pallas_call | solution.py:239
  29.8 0.8 %gate_up.8 = (f32[256,896]{1,0:T(8,128)S(1)}, f32[256,896]{1,0:T(8,128)S(1)}) custom-call(bf16[1,896,4096]{2,1,0:T(8,128)(2,1)S(1)} %copy-done, bf16[1,896,4096]{2,1,0:T(8,128)(2,1)S(1)} %copy-done.1, bf16[2,64,512]{2,1,0:T(8,128)(2,1)S(1)} %collective-permute-done.1.refs_0_, bf16[192,512]{1,0:T(8,128)(2,1)S(1)} %collective-permute-done.7.refs_1_, ...), custom_call_target="tpu_custom_call" | custom-call | flops 7340032 | tf_op jit(solution)/shard_map/gate_up/pallas_call | solution.py:239
  30.6 1.1 %gate_up.9 = (bf16[256,896]{1,0:T(8,128)(2,1)S(1)}, bf16[2,128,512]{2,1,0:T(8,128)(2,1)S(1)}) custom-call(bf16[1,896,4096]{2,1,0:T(8,128)(2,1)S(1)} %copy-done, bf16[1,896,4096]{2,1,0:T(8,128)(2,1)S(1)} %copy-done.1, bf16[1,896,4096]{2,1,0:T(8,128)(2,1)S(1)} %bitcast.12, bf16[2,64,512]{2,1,0:T(8,128)(2,1)S(1)} %collective-permute-done.2.refs_2_.refs_1_, ...), custom_call_target="tpu_custom_call" | custom-call | flops 7340032 | tf_op jit(solution)/shard_map/gate_up/pallas_call | solution.py:239
  32.3 1.0 %down.3 = (bf16[2,128,512]{2,1,0:T(8,128)(2,1)S(1)}, f32[2,128,512]{2,1,0:T(8,128)S(1)}, f32[2,128,512]{2,1,0:T(8,128)S(1)}) custom-call(bf16[1,896,4096]{2,1,0:T(8,128)(2,1)S(1)} %bitcast.12, bf16[256,896]{1,0:T(8,128)(2,1)S(1)} %get-tuple-element.42.hidden_ref), custom_call_target="tpu_custom_call" | custom-call | flops 939524096 | bytes 3670016 | tf_op jit(solution)/shard_map/down/pallas_call | solution.py:277
  33.4 1.3 %down.2 = (bf16[2,128,512]{2,1,0:T(8,128)(2,1)S(1)}, bf16[2,128,512]{2,1,0:T(8,128)(2,1)S(1)}, f32[2,128,512]{2,1,0:T(8,128)S(1)}, f32[2,128,512]{2,1,0:T(8,128)S(1)}) custom-call(bf16[1,896,4096]{2,1,0:T(8,128)(2,1)S(1)} %bitcast.12, bf16[256,896]{1,0:T(8,128)(2,1)S(1)} %get-tuple-element.42.hidden_ref), custom_call_target="tpu_custom_call" | custom-call | flops 939524096 | bytes 3670016 | tf_op jit(solution)/shard_map/down/pallas_call | solution.py:277
  35.4 1.6 %collective-permute-start.21 = (bf16[2,128,512]{2,1,0:T(8,128)(2,1)S(1)}, bf16[2,128,512]{2,1,0:T(8,128)(2,1)S(1)}, u32[]{:S(2)}, u32[]{:S(2)}) collective-permute-start(bf16[2,128,512]{2,1,0:T(8,128)(2,1)S(1)} %add_convert_fusion), channel_id=1, source_target_pairs={{0,3},{1,4},{2,1},{3,6},{4,7},{5,0},{6,5},{7,2},{8,11},{9,12},{10,... | collective-permute-start | bytes 786440 | tf_op jit(solution)/shard_map/ppermute | solution.py:351
  37.0 1.3 %collective-permute-start.16 = (bf16[2,128,512]{2,1,0:T(8,128)(2,1)S(1)}, bf16[2,128,512]{2,1,0:T(8,128)(2,1)S(1)}, u32[]{:S(2)}, u32[]{:S(2)}) collective-permute-start(bf16[2,128,512]{2,1,0:T(8,128)(2,1)S(1)} %add_convert_fusion.1), channel_id=1, source_target_pairs={{0,3},{1,4},{2,1},{3,6},{4,7},{5,0},{6,5},{7,2},{8,11},{9,12},{10,... | collective-permute-start | bytes 786440 | tf_op jit(solution)/shard_map/ppermute | solution.py:351
  38.4 2.8 %collective-permute-done.21 = bf16[2,128,512]{2,1,0:T(8,128)(2,1)S(1)} collective-permute-done((bf16[2,128,512]{2,1,0:T(8,128)(2,1)S(1)}, bf16[2,128,512]{2,1,0:T(8,128)(2,1)S(1)}, u32[]{:S(2)}, u32[]{:S(2)}) %collective-permute-start.21) | collective-permute-done | bytes 262176 | tf_op jit(solution)/shard_map/ppermute | solution.py:351
  41.2 1.6 %collective-permute-start.22 = (bf16[1,128,512]{2,1,0:T(8,128)(2,1)S(1)}, bf16[1,128,512]{2,1,0:T(8,128)(2,1)S(1)}, u32[]{:S(2)}, u32[]{:S(2)}) collective-permute-start(bf16[1,128,512]{2,1,0:T(8,128)(2,1)S(1)} %fusion), channel_id=1, source_target_pairs={{0,2},{1,5},{2,0},{3,7},{4,6},{5,1},{6,4},{7,3},{8,10},{9,13},{10,... | collective-permute-start | bytes 393224 | tf_op jit(solution)/shard_map/ppermute | solution.py:351
  42.8 1.2 %collective-permute-done.16 = bf16[2,128,512]{2,1,0:T(8,128)(2,1)S(1)} collective-permute-done((bf16[2,128,512]{2,1,0:T(8,128)(2,1)S(1)}, bf16[2,128,512]{2,1,0:T(8,128)(2,1)S(1)}, u32[]{:S(2)}, u32[]{:S(2)}) %collective-permute-start.16) | collective-permute-done | bytes 262176 | tf_op jit(solution)/shard_map/ppermute | solution.py:351
  44.0 1.6 %collective-permute-start.17 = (bf16[1,128,512]{2,1,0:T(8,128)(2,1)S(1)}, bf16[1,128,512]{2,1,0:T(8,128)(2,1)S(1)}, u32[]{:S(2)}, u32[]{:S(2)}) collective-permute-start(bf16[1,128,512]{2,1,0:T(8,128)(2,1)S(1)} %fusion.3), channel_id=1, source_target_pairs={{0,2},{1,5},{2,0},{3,7},{4,6},{5,1},{6,4},{7,3},{8,10},{9,13},{10,... | collective-permute-start | bytes 393224 | tf_op jit(solution)/shard_map/ppermute | solution.py:351
  45.6 0.7 %collective-permute-done.22 = bf16[1,128,512]{2,1,0:T(8,128)(2,1)S(1)} collective-permute-done((bf16[1,128,512]{2,1,0:T(8,128)(2,1)S(1)}, bf16[1,128,512]{2,1,0:T(8,128)(2,1)S(1)}, u32[]{:S(2)}, u32[]{:S(2)}) %collective-permute-start.22) | collective-permute-done | bytes 131104 | tf_op jit(solution)/shard_map/ppermute | solution.py:351
  46.3 1.6 %collective-permute-start.23 = (bf16[64,512]{1,0:T(8,128)(2,1)S(1)}, bf16[64,512]{1,0:T(8,128)(2,1)S(1)}, u32[]{:S(2)}, u32[]{:S(2)}) collective-permute-start(bf16[64,512]{1,0:T(8,128)(2,1)S(1)} %get-tuple-element.52), channel_id=1, source_target_pairs={{0,16},{8,24},{16,0},{24,8},{1,17},{9,25},{17,1},{25,9},{2,18},{10... | collective-permute-start | bytes 196616 | tf_op jit(solution)/shard_map/ppermute | solution.py:344
  48.0 0.7 %collective-permute-start.24 = (bf16[64,512]{1,0:T(8,128)(2,1)S(1)}, bf16[64,512]{1,0:T(8,128)(2,1)S(1)}, u32[]{:S(2)}, u32[]{:S(2)}) collective-permute-start(bf16[64,512]{1,0:T(8,128)(2,1)S(1)} %get-tuple-element.51), channel_id=1, source_target_pairs={{0,24},{8,16},{16,8},{24,0},{1,25},{9,17},{17,9},{25,1},{2,26},{10... | collective-permute-start | bytes 196616 | tf_op jit(solution)/shard_map/ppermute | solution.py:344
  49.2 0.9 %collective-permute-start.18 = (bf16[64,512]{1,0:T(8,128)(2,1)S(1)}, bf16[64,512]{1,0:T(8,128)(2,1)S(1)}, u32[]{:S(2)}, u32[]{:S(2)}) collective-permute-start(bf16[64,512]{1,0:T(8,128)(2,1)S(1)} %get-tuple-element.53), channel_id=1, source_target_pairs={{0,8},{8,0},{16,24},{24,16},{1,9},{9,1},{17,25},{25,17},{2,10},{10... | collective-permute-start | bytes 196616 | tf_op jit(solution)/shard_map/ppermute | solution.py:344
  50.2 2.7 %collective-permute-done.23.refs_2_ = bf16[64,512]{1,0:T(8,128)(2,1)S(1)} collective-permute-done((bf16[64,512]{1,0:T(8,128)(2,1)S(1)}, bf16[64,512]{1,0:T(8,128)(2,1)S(1)}, u32[]{:S(2)}, u32[]{:S(2)}) %collective-permute-start.23) | collective-permute-done | bytes 65568 | tf_op jit(solution)/shard_map/ppermute | solution.py:344
  53.0 1.2 %collective-permute-done.24.refs_3_ = bf16[64,512]{1,0:T(8,128)(2,1)S(1)} collective-permute-done((bf16[64,512]{1,0:T(8,128)(2,1)S(1)}, bf16[64,512]{1,0:T(8,128)(2,1)S(1)}, u32[]{:S(2)}, u32[]{:S(2)}) %collective-permute-start.24) | collective-permute-done | bytes 65568 | tf_op jit(solution)/shard_map/ppermute | solution.py:344
  54.7 0.9 %combine.1 = bf16[96,512]{1,0:T(8,128)(2,1)} custom-call(bf16[96,256]{1,0:T(8,128)(2,1)S(1)} %get-tuple-element.28.high_ref, bf16[96,256]{1,0:T(8,128)(2,1)S(1)} %get-tuple-element.29.low_ref, bf16[64,512]{1,0:T(8,128)(2,1)S(1)} %get-tuple-element.54.refs_0_, bf16[64,512]{1,0:T(8,128)(2,1)S(1)} %collective-permute-done.18.refs_1_, ...), custom_call_target="tpu_custom_call" | custom-call | tf_op jit(solution)/shard_map/combine/pallas_call | solution.py:301
  (59 shorter events, 4.5 us)
Async XLA Ops:
  0.0 0.7 %copy-start.3 = (s32[96,2]{0,1:T(2,128)S(1)}, s32[96,2]{0,1:T(2,128)}, u32[]{:S(2)}) copy-start(s32[96,2]{0,1:T(2,128)} %param.7) | copy-start | bytes 2308
  0.0 0.9 %copy-start.2 = (bf16[96,512]{1,0:T(8,128)(2,1)S(1)}, bf16[96,512]{1,0:T(8,128)(2,1)}, u32[]{:S(2)}) copy-start(bf16[96,512]{1,0:T(8,128)(2,1)} %x_ref.1) | copy-start | bytes 294916
  0.0 25.9 %copy-start.1 = (bf16[1,896,4096]{2,1,0:T(8,128)(2,1)S(1)}, bf16[1,896,4096]{2,1,0:T(8,128)(2,1)}, u32[]{:S(2)}) copy-start(bf16[1,896,4096]{2,1,0:T(8,128)(2,1)} %up_ref.9) | copy-start | bytes 22020100
  0.0 25.9 %copy-start = (bf16[1,896,4096]{2,1,0:T(8,128)(2,1)S(1)}, bf16[1,896,4096]{2,1,0:T(8,128)(2,1)}, u32[]{:S(2)}) copy-start(bf16[1,896,4096]{2,1,0:T(8,128)(2,1)} %gate_ref.9) | copy-start | bytes 22020100
  1.1 5.7 %collective-permute-start.3 = (bf16[64,512]{1,0:T(8,128)(2,1)S(1)}, bf16[64,512]{1,0:T(8,128)(2,1)S(1)}, u32[]{:S(2)}, u32[]{:S(2)}) collective-permute-start(bf16[64,512]{1,0:T(8,128)(2,1)S(1)} %get-tuple-element.31), channel_id=1, source_target_pairs={{0,8},{8,0},{16,24},{24,16},{1,9},{9,1},{17,25},{25,17},{2,10},{10... | collective-permute-start | bytes 196616 | tf_op jit(solution)/shard_map/ppermute | solution.py:344
  4.2 7.3 %collective-permute-start.4 = (bf16[64,512]{1,0:T(8,128)(2,1)S(1)}, bf16[64,512]{1,0:T(8,128)(2,1)S(1)}, u32[]{:S(2)}, u32[]{:S(2)}) collective-permute-start(bf16[64,512]{1,0:T(8,128)(2,1)S(1)} %get-tuple-element.32), channel_id=1, source_target_pairs={{0,16},{8,24},{16,0},{24,8},{1,17},{9,25},{17,1},{25,9},{2,18},{10... | collective-permute-start | bytes 196616 | tf_op jit(solution)/shard_map/ppermute | solution.py:344
  6.8 6.1 %collective-permute-start.5 = (bf16[64,512]{1,0:T(8,128)(2,1)S(1)}, bf16[64,512]{1,0:T(8,128)(2,1)S(1)}, u32[]{:S(2)}, u32[]{:S(2)}) collective-permute-start(bf16[64,512]{1,0:T(8,128)(2,1)S(1)} %get-tuple-element.33), channel_id=1, source_target_pairs={{0,24},{8,16},{16,8},{24,0},{1,25},{9,17},{17,9},{25,1},{2,26},{10... | collective-permute-start | bytes 196616 | tf_op jit(solution)/shard_map/ppermute | solution.py:344
  12.9 6.3 %collective-permute-start.6 = (bf16[192,512]{1,0:T(8,128)(2,1)S(1)}, bf16[192,512]{1,0:T(8,128)(2,1)S(1)}, u32[]{:S(2)}, u32[]{:S(2)}) collective-permute-start(bf16[192,512]{1,0:T(8,128)(2,1)S(1)} %constant_dynamic-update-slice_fusion.refs_1_), channel_id=1, source_target_pairs={{0,2},{1,5},{2,0},{3,7},{4,6},{5,1},{6,4},{7,3},{8,10},{9,13},{10,... | collective-permute-start | bytes 589832 | tf_op jit(solution)/shard_map/ppermute | solution.py:351
  14.4 6.2 %collective-permute-start = (bf16[1,64,512]{2,1,0:T(8,128)(2,1)S(1)}, bf16[1,64,512]{2,1,0:T(8,128)(2,1)S(1)}, u32[]{:S(2)}, u32[]{:S(2)}) collective-permute-start(bf16[1,64,512]{2,1,0:T(8,128)(2,1)S(1)} %bitcast.13), channel_id=1, source_target_pairs={{0,2},{1,5},{2,0},{3,7},{4,6},{5,1},{6,4},{7,3},{8,10},{9,13},{10,... | collective-permute-start | bytes 196616 | tf_op jit(solution)/shard_map/ppermute | solution.py:351
  14.9 7.9 %collective-permute-start.9 = (bf16[192,512]{1,0:T(8,128)(2,1)S(1)}, bf16[192,512]{1,0:T(8,128)(2,1)S(1)}, u32[]{:S(2)}, u32[]{:S(2)}) collective-permute-start(bf16[192,512]{1,0:T(8,128)(2,1)S(1)} %constant_dynamic-update-slice_fusion.refs_1_), channel_id=1, source_target_pairs={{0,5},{1,2},{2,7},{3,0},{4,1},{5,6},{6,3},{7,4},{8,13},{9,10},{10,... | collective-permute-start | bytes 589832 | tf_op jit(solution)/shard_map/ppermute | solution.py:351
  19.2 5.1 %collective-permute-start.7 = (bf16[192,512]{1,0:T(8,128)(2,1)S(1)}, bf16[192,512]{1,0:T(8,128)(2,1)S(1)}, u32[]{:S(2)}, u32[]{:S(2)}) collective-permute-start(bf16[192,512]{1,0:T(8,128)(2,1)S(1)} %collective-permute-done.6.refs_1_), channel_id=1, source_target_pairs={{0,5},{1,2},{2,7},{3,0},{4,1},{5,6},{6,3},{7,4},{8,13},{9,10},{10,... | collective-permute-start | bytes 589832 | tf_op jit(solution)/shard_map/ppermute | solution.py:351
  20.7 1.7 %collective-permute-start.11 = (bf16[2,64,512]{2,1,0:T(8,128)(2,1)S(1)}, bf16[2,64,512]{2,1,0:T(8,128)(2,1)S(1)}, u32[]{:S(2)}, u32[]{:S(2)}) collective-permute-start(bf16[2,64,512]{2,1,0:T(8,128)(2,1)S(1)} %pad_maximum_fusion.refs_0_), channel_id=1, source_target_pairs={{0,1},{1,0},{2,3},{3,2},{4,5},{5,4},{6,7},{7,6},{8,9},{9,8},{10,11... | collective-permute-start | bytes 393224 | tf_op jit(solution)/shard_map/ppermute | solution.py:347
  20.9 4.8 %collective-permute-start.1 = (bf16[2,64,512]{2,1,0:T(8,128)(2,1)S(1)}, bf16[2,64,512]{2,1,0:T(8,128)(2,1)S(1)}, u32[]{:S(2)}, u32[]{:S(2)}) collective-permute-start(bf16[2,64,512]{2,1,0:T(8,128)(2,1)S(1)} %pad_maximum_fusion.refs_0_), channel_id=1, source_target_pairs={{0,5},{1,2},{2,7},{3,0},{4,1},{5,6},{6,3},{7,4},{8,13},{9,10},{10,... | collective-permute-start | bytes 393224 | tf_op jit(solution)/shard_map/ppermute | solution.py:351
  22.4 3.5 %collective-permute-start.13 = (bf16[192,512]{1,0:T(8,128)(2,1)S(1)}, bf16[192,512]{1,0:T(8,128)(2,1)S(1)}, u32[]{:S(2)}, u32[]{:S(2)}) collective-permute-start(bf16[192,512]{1,0:T(8,128)(2,1)S(1)} %constant_dynamic-update-slice_fusion.refs_1_), channel_id=1, source_target_pairs={{0,1},{1,0},{2,3},{3,2},{4,5},{5,4},{6,7},{7,6},{8,9},{9,8},{10,11... | collective-permute-start | bytes 589832 | tf_op jit(solution)/shard_map/ppermute | solution.py:347
  22.4 4.8 %collective-permute-start.12 = (bf16[192,512]{1,0:T(8,128)(2,1)S(1)}, bf16[192,512]{1,0:T(8,128)(2,1)S(1)}, u32[]{:S(2)}, u32[]{:S(2)}) collective-permute-start(bf16[192,512]{1,0:T(8,128)(2,1)S(1)} %collective-permute-done.6.refs_1_), channel_id=1, source_target_pairs={{0,1},{1,0},{2,3},{3,2},{4,5},{5,4},{6,7},{7,6},{8,9},{9,8},{10,11... | collective-permute-start | bytes 589832 | tf_op jit(solution)/shard_map/ppermute | solution.py:347
  22.9 5.6 %collective-permute-start.10 = (bf16[192,512]{1,0:T(8,128)(2,1)S(1)}, bf16[192,512]{1,0:T(8,128)(2,1)S(1)}, u32[]{:S(2)}, u32[]{:S(2)}) collective-permute-start(bf16[192,512]{1,0:T(8,128)(2,1)S(1)} %collective-permute-done.9.refs_1_), channel_id=1, source_target_pairs={{0,1},{1,0},{2,3},{3,2},{4,5},{5,4},{6,7},{7,6},{8,9},{9,8},{10,11... | collective-permute-start | bytes 589832 | tf_op jit(solution)/shard_map/ppermute | solution.py:347
  24.3 6.3 %collective-permute-start.8 = (bf16[192,512]{1,0:T(8,128)(2,1)S(1)}, bf16[192,512]{1,0:T(8,128)(2,1)S(1)}, u32[]{:S(2)}, u32[]{:S(2)}) collective-permute-start(bf16[192,512]{1,0:T(8,128)(2,1)S(1)} %collective-permute-done.7.refs_1_), channel_id=1, source_target_pairs={{0,1},{1,0},{2,3},{3,2},{4,5},{5,4},{6,7},{7,6},{8,9},{9,8},{10,11... | collective-permute-start | bytes 589832 | tf_op jit(solution)/shard_map/ppermute | solution.py:347
  25.7 2.8 %collective-permute-start.2 = (bf16[2,64,512]{2,1,0:T(8,128)(2,1)S(1)}, bf16[2,64,512]{2,1,0:T(8,128)(2,1)S(1)}, u32[]{:S(2)}, u32[]{:S(2)}) collective-permute-start(bf16[2,64,512]{2,1,0:T(8,128)(2,1)S(1)} %collective-permute-done.1.refs_0_), channel_id=1, source_target_pairs={{0,1},{1,0},{2,3},{3,2},{4,5},{5,4},{6,7},{7,6},{8,9},{9,8},{10,11... | collective-permute-start | bytes 393224 | tf_op jit(solution)/shard_map/ppermute | solution.py:347
  27.2 3.4 %slice-start = ((s8[7340032]{0:T(1024)(128)(4,1)}), s8[4194304]{0:T(1024)(128)(4,1)S(1)}, s32[]{:S(2)}) async-start(s8[7340032]{0:T(1024)(128)(4,1)} %bitcast.11), calls=%async_computation | async-start | bytes 8388608
  28.5 2.1 %slice-start.1 = ((s8[7340032]{0:T(1024)(128)(4,1)}), s8[3145728]{0:T(1024)(128)(4,1)S(1)}, s32[]{:S(2)}) async-start(s8[7340032]{0:T(1024)(128)(4,1)} %bitcast.11), calls=%async_computation.1 | async-start | bytes 6291456
  31.8 3.5 %collective-permute-start.20 = (bf16[2,128,512]{2,1,0:T(8,128)(2,1)S(1)}, bf16[2,128,512]{2,1,0:T(8,128)(2,1)S(1)}, u32[]{:S(2)}, u32[]{:S(2)}) collective-permute-start(bf16[2,128,512]{2,1,0:T(8,128)(2,1)S(1)} %get-tuple-element.50), channel_id=1, source_target_pairs={{0,1},{1,0},{2,3},{3,2},{4,5},{5,4},{6,7},{7,6},{8,9},{9,8},{10,11... | collective-permute-start | bytes 786440 | tf_op jit(solution)/shard_map/ppermute | solution.py:347
  33.3 16.8 %copy-start.4 = (f32[96,2]{0,1:T(2,128)S(1)}, f32[96,2]{0,1:T(2,128)}, u32[]{:S(2)}) copy-start(f32[96,2]{0,1:T(2,128)} %param.8) | copy-start | bytes 2308
  33.3 3.6 %collective-permute-start.15 = (bf16[2,128,512]{2,1,0:T(8,128)(2,1)S(1)}, bf16[2,128,512]{2,1,0:T(8,128)(2,1)S(1)}, u32[]{:S(2)}, u32[]{:S(2)}) collective-permute-start(bf16[2,128,512]{2,1,0:T(8,128)(2,1)S(1)} %get-tuple-element.46), channel_id=1, source_target_pairs={{0,1},{1,0},{2,3},{3,2},{4,5},{5,4},{6,7},{7,6},{8,9},{9,8},{10,11... | collective-permute-start | bytes 786440 | tf_op jit(solution)/shard_map/ppermute | solution.py:347
  34.7 3.6 %collective-permute-start.19 = (bf16[2,128,512]{2,1,0:T(8,128)(2,1)S(1)}, bf16[2,128,512]{2,1,0:T(8,128)(2,1)S(1)}, u32[]{:S(2)}, u32[]{:S(2)}) collective-permute-start(bf16[2,128,512]{2,1,0:T(8,128)(2,1)S(1)} %get-tuple-element.48), channel_id=1, source_target_pairs={{0,1},{1,0},{2,3},{3,2},{4,5},{5,4},{6,7},{7,6},{8,9},{9,8},{10,11... | collective-permute-start | bytes 786440 | tf_op jit(solution)/shard_map/ppermute | solution.py:347
  35.2 3.2 %collective-permute-start.14 = (bf16[2,128,512]{2,1,0:T(8,128)(2,1)S(1)}, bf16[2,128,512]{2,1,0:T(8,128)(2,1)S(1)}, u32[]{:S(2)}, u32[]{:S(2)}) collective-permute-start(bf16[2,128,512]{2,1,0:T(8,128)(2,1)S(1)} %get-tuple-element.44), channel_id=1, source_target_pairs={{0,1},{1,0},{2,3},{3,2},{4,5},{5,4},{6,7},{7,6},{8,9},{9,8},{10,11... | collective-permute-start | bytes 786440 | tf_op jit(solution)/shard_map/ppermute | solution.py:347
  35.4 5.8 %collective-permute-start.21 = (bf16[2,128,512]{2,1,0:T(8,128)(2,1)S(1)}, bf16[2,128,512]{2,1,0:T(8,128)(2,1)S(1)}, u32[]{:S(2)}, u32[]{:S(2)}) collective-permute-start(bf16[2,128,512]{2,1,0:T(8,128)(2,1)S(1)} %add_convert_fusion), channel_id=1, source_target_pairs={{0,3},{1,4},{2,1},{3,6},{4,7},{5,0},{6,5},{7,2},{8,11},{9,12},{10,... | collective-permute-start | bytes 786440 | tf_op jit(solution)/shard_map/ppermute | solution.py:351
  37.0 7.0 %collective-permute-start.16 = (bf16[2,128,512]{2,1,0:T(8,128)(2,1)S(1)}, bf16[2,128,512]{2,1,0:T(8,128)(2,1)S(1)}, u32[]{:S(2)}, u32[]{:S(2)}) collective-permute-start(bf16[2,128,512]{2,1,0:T(8,128)(2,1)S(1)} %add_convert_fusion.1), channel_id=1, source_target_pairs={{0,3},{1,4},{2,1},{3,6},{4,7},{5,0},{6,5},{7,2},{8,11},{9,12},{10,... | collective-permute-start | bytes 786440 | tf_op jit(solution)/shard_map/ppermute | solution.py:351
  41.2 5.0 %collective-permute-start.22 = (bf16[1,128,512]{2,1,0:T(8,128)(2,1)S(1)}, bf16[1,128,512]{2,1,0:T(8,128)(2,1)S(1)}, u32[]{:S(2)}, u32[]{:S(2)}) collective-permute-start(bf16[1,128,512]{2,1,0:T(8,128)(2,1)S(1)} %fusion), channel_id=1, source_target_pairs={{0,2},{1,5},{2,0},{3,7},{4,6},{5,1},{6,4},{7,3},{8,10},{9,13},{10,... | collective-permute-start | bytes 393224 | tf_op jit(solution)/shard_map/ppermute | solution.py:351
  44.0 5.0 %collective-permute-start.17 = (bf16[1,128,512]{2,1,0:T(8,128)(2,1)S(1)}, bf16[1,128,512]{2,1,0:T(8,128)(2,1)S(1)}, u32[]{:S(2)}, u32[]{:S(2)}) collective-permute-start(bf16[1,128,512]{2,1,0:T(8,128)(2,1)S(1)} %fusion.3), channel_id=1, source_target_pairs={{0,2},{1,5},{2,0},{3,7},{4,6},{5,1},{6,4},{7,3},{8,10},{9,13},{10,... | collective-permute-start | bytes 393224 | tf_op jit(solution)/shard_map/ppermute | solution.py:351
  46.3 6.6 %collective-permute-start.23 = (bf16[64,512]{1,0:T(8,128)(2,1)S(1)}, bf16[64,512]{1,0:T(8,128)(2,1)S(1)}, u32[]{:S(2)}, u32[]{:S(2)}) collective-permute-start(bf16[64,512]{1,0:T(8,128)(2,1)S(1)} %get-tuple-element.52), channel_id=1, source_target_pairs={{0,16},{8,24},{16,0},{24,8},{1,17},{9,25},{17,1},{25,9},{2,18},{10... | collective-permute-start | bytes 196616 | tf_op jit(solution)/shard_map/ppermute | solution.py:344
  48.0 6.2 %collective-permute-start.24 = (bf16[64,512]{1,0:T(8,128)(2,1)S(1)}, bf16[64,512]{1,0:T(8,128)(2,1)S(1)}, u32[]{:S(2)}, u32[]{:S(2)}) collective-permute-start(bf16[64,512]{1,0:T(8,128)(2,1)S(1)} %get-tuple-element.51), channel_id=1, source_target_pairs={{0,24},{8,16},{16,8},{24,0},{1,25},{9,17},{17,9},{25,1},{2,26},{10... | collective-permute-start | bytes 196616 | tf_op jit(solution)/shard_map/ppermute | solution.py:344
  49.2 5.6 %collective-permute-start.18 = (bf16[64,512]{1,0:T(8,128)(2,1)S(1)}, bf16[64,512]{1,0:T(8,128)(2,1)S(1)}, u32[]{:S(2)}, u32[]{:S(2)}) collective-permute-start(bf16[64,512]{1,0:T(8,128)(2,1)S(1)} %get-tuple-element.53), channel_id=1, source_target_pairs={{0,8},{8,0},{16,24},{24,16},{1,9},{9,1},{17,25},{25,17},{2,10},{10... | collective-permute-start | bytes 196616 | tf_op jit(solution)/shard_map/ppermute | solution.py:344

commit v6 on v5

--- a/solution.py
+++ b/solution.py
@@ -170,6 +170,11 @@
     )(pick, ids, weight)
 
 
+def both(gate_ref, up_ref, pick, width):
+    at = pl.ds(pl.multiple_of(owner(pick) * width, 128), width)
+    return jnp.concatenate([gate_ref[0, :, at], up_ref[0, :, at]], axis=0)
+
+
 def owner(pick):
     across, even, odd = pick
     me = lax.axis_index("tensor")
@@ -188,17 +193,16 @@
     count = len(picks)
     xs, refs = refs[: 2 * count], refs[2 * count :]
     width = xs[0].shape[2]
-    gate, up = (None, None) if fresh else (refs[0][...], refs[1][...])
+    total = None if fresh else refs[0][...]
     for i, pick in enumerate(picks):
         x = jnp.concatenate([xs[2 * i][places[i]], xs[2 * i + 1][...]], axis=0)
-        g = contract_last(x, part(gate_ref, pick, width))
-        u = contract_last(x, part(up_ref, pick, width))
-        gate = g if gate is None else gate + g
-        up = u if up is None else up + u
+        share = contract_last(x, both(gate_ref, up_ref, pick, width))
+        total = share if total is None else total + share
     if not final:
-        refs[-2][...] = gate
-        refs[-1][...] = up
+        refs[-1][...] = total
         return
+    hid = total.shape[1] // 2
+    gate, up = total[:, :hid], total[:, hid:]
     hidden = (gate / (1.0 + jnp.exp(-gate)) * up).astype(jnp.bfloat16)
     refs[-2][...] = hidden
     split(hidden, give, down_ref, refs[-1:])
@@ -232,7 +236,7 @@
             jax.ShapeDtypeStruct((len(give), rows - cut, width), jnp.bfloat16),
         ]
     else:
-        outs = [jax.ShapeDtypeStruct((rows, hid), jnp.float32)] * 2
+        outs = [jax.ShapeDtypeStruct((rows, 2 * hid), jnp.float32)]
     extra = [w_down] if give else []
     xs = [x for item in items for x in (item[0], item[2])]
     places = [item[1] for item in items]

time: 55.7 us -> 55.5 us (level)
  transfers between devices with their start and end apart: 25 -> 25, of which waited for: 13 -> 13; matrix products, arithmetic and copies ran while one was open for 1% -> 1% of each run, Pallas kernels for 13% -> 12%
where the time goes in v6:
time: 55.5 us; the launch traced here: 55.4 us
  waiting for transfers between devices  23.9 us (43%)
  starting transfers between devices  20.7 us (37%)
  Pallas kernels  9.01 us (16%)
  local copies, waits for them, and re-layouts  1.07 us (2%)
    ppermute x9, waiting for transfers between devices, hop(): return lax.ppermute(value, 'tensor', pairs)  13.4 us
    ppermute x6, waiting for transfers between devices, across(): return lax.ppermute(value, 'expert', [(i, i ^ by) for i in range(experts)])  10.5 us
    ppermute x9, starting transfers between devices, hop(): return lax.ppermute(value, 'tensor', pairs)  9.41 us
    ppermute x6, starting transfers between devices, across(): return lax.ppermute(value, 'expert', [(i, i ^ by) for i in range(experts)])  8.9 us
    pallas_call x5, Pallas kernels, gate_up(): pl.pallas_call(functools.partial(gate_up_kernel, picks, places, give, fre...  5.31 us
    ppermute x10, starting transfers between devices, swap(): return lax.ppermute(value, 'tensor', [(i, i ^ 1) for i in range(tensor)])  2.38 us
    pallas_call x2, Pallas kernels, down(): pl.pallas_call(functools.partial(down_kernel, give, near, keep), out_shap...  2.25 us
  transfers between devices with their start and end apart: 25, of which 13 were waited for; matrix products, arithmetic and copies ran while one was open for 1% of the time, Pallas kernels for 12%

profile of v6, /device:TPU:0, one launch (start us, length us, event | category | flops | bytes accessed | tf_op | source)
XLA Modules:
  0.0 55.4 jit_solution(453190502162645379)
XLA Ops:
  0.0 0.7 %copy-done.3 = s32[96,2]{0,1:T(2,128)S(1)} copy-done((s32[96,2]{0,1:T(2,128)S(1)}, s32[96,2]{0,1:T(2,128)}, u32[]{:S(2)}) %copy-start.3) | copy-done | bytes 792
  1.1 3.1 %collective-permute-start.3 = (bf16[64,512]{1,0:T(8,128)(2,1)S(1)}, bf16[64,512]{1,0:T(8,128)(2,1)S(1)}, u32[]{:S(2)}, u32[]{:S(2)}) collective-permute-start(bf16[64,512]{1,0:T(8,128)(2,1)S(1)} %get-tuple-element.23), channel_id=1, source_target_pairs={{0,8},{8,0},{16,24},{24,16},{1,9},{9,1},{17,25},{25,17},{2,10},{10... | collective-permute-start | bytes 196616 | tf_op jit(solution)/shard_map/ppermute | solution.py:348
  4.2 2.6 %collective-permute-start.4 = (bf16[64,512]{1,0:T(8,128)(2,1)S(1)}, bf16[64,512]{1,0:T(8,128)(2,1)S(1)}, u32[]{:S(2)}, u32[]{:S(2)}) collective-permute-start(bf16[64,512]{1,0:T(8,128)(2,1)S(1)} %get-tuple-element.24), channel_id=1, source_target_pairs={{0,16},{8,24},{16,0},{24,8},{1,17},{9,25},{17,1},{25,9},{2,18},{10... | collective-permute-start | bytes 196616 | tf_op jit(solution)/shard_map/ppermute | solution.py:348
  6.8 4.7 %collective-permute-done.4 = bf16[64,512]{1,0:T(8,128)(2,1)S(1)} collective-permute-done((bf16[64,512]{1,0:T(8,128)(2,1)S(1)}, bf16[64,512]{1,0:T(8,128)(2,1)S(1)}, u32[]{:S(2)}, u32[]{:S(2)}) %collective-permute-start.4) | collective-permute-done | bytes 65568 | tf_op jit(solution)/shard_map/ppermute | solution.py:348
  11.5 1.4 %collective-permute-done.5 = bf16[64,512]{1,0:T(8,128)(2,1)S(1)} collective-permute-done((bf16[64,512]{1,0:T(8,128)(2,1)S(1)}, bf16[64,512]{1,0:T(8,128)(2,1)S(1)}, u32[]{:S(2)}, u32[]{:S(2)}) %collective-permute-start.5) | collective-permute-done | bytes 65568 | tf_op jit(solution)/shard_map/ppermute | solution.py:348
  12.9 1.5 %collective-permute-start.6 = (bf16[192,512]{1,0:T(8,128)(2,1)S(1)}, bf16[192,512]{1,0:T(8,128)(2,1)S(1)}, u32[]{:S(2)}, u32[]{:S(2)}) collective-permute-start(bf16[192,512]{1,0:T(8,128)(2,1)S(1)} %constant_dynamic-update-slice_fusion.refs_1_), channel_id=1, source_target_pairs={{0,2},{1,5},{2,0},{3,7},{4,6},{5,1},{6,4},{7,3},{8,10},{9,13},{10,... | collective-permute-start | bytes 589832 | tf_op jit(solution)/shard_map/ppermute | solution.py:355
  14.4 0.5 collective-permute-start
  14.9 4.3 %collective-permute-done.6.refs_1_ = bf16[192,512]{1,0:T(8,128)(2,1)S(1)} collective-permute-done((bf16[192,512]{1,0:T(8,128)(2,1)S(1)}, bf16[192,512]{1,0:T(8,128)(2,1)S(1)}, u32[]{:S(2)}, u32[]{:S(2)}) %collective-permute-start.6) | collective-permute-done | bytes 196640 | tf_op jit(solution)/shard_map/ppermute | solution.py:355
  19.2 1.4 %collective-permute-done = bf16[1,64,512]{2,1,0:T(8,128)(2,1)S(1)} collective-permute-done((bf16[1,64,512]{2,1,0:T(8,128)(2,1)S(1)}, bf16[1,64,512]{2,1,0:T(8,128)(2,1)S(1)}, u32[]{:S(2)}, u32[]{:S(2)}) %collective-permute-start) | collective-permute-done | bytes 65568 | tf_op jit(solution)/shard_map/ppermute | solution.py:355
  20.9 1.4 %collective-permute-start.1 = (bf16[2,64,512]{2,1,0:T(8,128)(2,1)S(1)}, bf16[2,64,512]{2,1,0:T(8,128)(2,1)S(1)}, u32[]{:S(2)}, u32[]{:S(2)}) collective-permute-start(bf16[2,64,512]{2,1,0:T(8,128)(2,1)S(1)} %pad_maximum_fusion.refs_0_), channel_id=1, source_target_pairs={{0,5},{1,2},{2,7},{3,0},{4,1},{5,6},{6,3},{7,4},{8,13},{9,10},{10,... | collective-permute-start | bytes 393224 | tf_op jit(solution)/shard_map/ppermute | solution.py:355
  22.9 1.4 %collective-permute-done.7.refs_1_ = bf16[192,512]{1,0:T(8,128)(2,1)S(1)} collective-permute-done((bf16[192,512]{1,0:T(8,128)(2,1)S(1)}, bf16[192,512]{1,0:T(8,128)(2,1)S(1)}, u32[]{:S(2)}, u32[]{:S(2)}) %collective-permute-start.7) | collective-permute-done | bytes 196640 | tf_op jit(solution)/shard_map/ppermute | solution.py:355
  24.5 1.2 %collective-permute-done.1.refs_0_ = bf16[2,64,512]{2,1,0:T(8,128)(2,1)S(1)} collective-permute-done((bf16[2,64,512]{2,1,0:T(8,128)(2,1)S(1)}, bf16[2,64,512]{2,1,0:T(8,128)(2,1)S(1)}, u32[]{:S(2)}, u32[]{:S(2)}) %collective-permute-start.1) | collective-permute-done | bytes 131104 | tf_op jit(solution)/shard_map/ppermute | solution.py:355
  25.9 1.2 %gate_up.5.refs_4_ = f32[256,1792]{1,0:T(8,128)S(1)} custom-call(bf16[1,896,4096]{2,1,0:T(8,128)(2,1)S(1)} %copy-done, bf16[1,896,4096]{2,1,0:T(8,128)(2,1)S(1)} %copy-done.1, bf16[2,64,512]{2,1,0:T(8,128)(2,1)S(1)} %pad_maximum_fusion.refs_0_, bf16[192,512]{1,0:T(8,128)(2,1)S(1)} %constant_dynamic-update-slice_fusion.refs_1_, ...), custom_call_target="tpu_custom_call" | custom-call | flops 14680064 | tf_op jit(solution)/shard_map/gate_up/pallas_call | solution.py:243
  27.1 1.2 %gate_up.6.refs_4_ = f32[256,1792]{1,0:T(8,128)S(1)} custom-call(bf16[1,896,4096]{2,1,0:T(8,128)(2,1)S(1)} %copy-done, bf16[1,896,4096]{2,1,0:T(8,128)(2,1)S(1)} %copy-done.1, bf16[2,64,512]{2,1,0:T(8,128)(2,1)S(1)} %pad_maximum_fusion.refs_0_, bf16[192,512]{1,0:T(8,128)(2,1)S(1)} %collective-permute-done.6.refs_1_, ...), custom_call_target="tpu_custom_call" | custom-call | flops 14680064 | tf_op jit(solution)/shard_map/gate_up/pallas_call | solution.py:243
  28.3 1.2 %gate_up.7.refs_2_ = f32[256,1792]{1,0:T(8,128)S(1)} custom-call(bf16[1,896,4096]{2,1,0:T(8,128)(2,1)S(1)} %copy-done, bf16[1,896,4096]{2,1,0:T(8,128)(2,1)S(1)} %copy-done.1, bf16[2,64,512]{2,1,0:T(8,128)(2,1)S(1)} %collective-permute-done.1.refs_0_, bf16[192,512]{1,0:T(8,128)(2,1)S(1)} %collective-permute-done.9.refs_1_, ...), custom_call_target="tpu_custom_call" | custom-call | flops 14680064 | tf_op jit(solution)/shard_map/gate_up/pallas_call | solution.py:243
  29.4 0.7 %gate_up.8.refs_3_ = f32[256,1792]{1,0:T(8,128)S(1)} custom-call(bf16[1,896,4096]{2,1,0:T(8,128)(2,1)S(1)} %copy-done, bf16[1,896,4096]{2,1,0:T(8,128)(2,1)S(1)} %copy-done.1, bf16[2,64,512]{2,1,0:T(8,128)(2,1)S(1)} %collective-permute-done.1.refs_0_, bf16[192,512]{1,0:T(8,128)(2,1)S(1)} %collective-permute-done.7.refs_1_, f32[256,1792]{1,0:T(8,128)S(1)} %gate_up.7.refs_2_), custom_call_target="tpu_custom_call" | custom-call | flops 7340032 | tf_op jit(solution)/shard_map/gate_up/pallas_call | solution.py:243
  30.4 1.1 %gate_up.9 = (bf16[256,896]{1,0:T(8,128)(2,1)S(1)}, bf16[2,128,512]{2,1,0:T(8,128)(2,1)S(1)}) custom-call(bf16[1,896,4096]{2,1,0:T(8,128)(2,1)S(1)} %copy-done, bf16[1,896,4096]{2,1,0:T(8,128)(2,1)S(1)} %copy-done.1, bf16[1,896,4096]{2,1,0:T(8,128)(2,1)S(1)} %bitcast.12, bf16[2,64,512]{2,1,0:T(8,128)(2,1)S(1)} %collective-permute-done.2.refs_2_.refs_1_, ...), custom_call_target="tpu_custom_call" | custom-call | flops 7340032 | tf_op jit(solution)/shard_map/gate_up/pallas_call | solution.py:243
  32.1 1.0 %down.3 = (bf16[2,128,512]{2,1,0:T(8,128)(2,1)S(1)}, f32[2,128,512]{2,1,0:T(8,128)S(1)}, f32[2,128,512]{2,1,0:T(8,128)S(1)}) custom-call(bf16[1,896,4096]{2,1,0:T(8,128)(2,1)S(1)} %bitcast.12, bf16[256,896]{1,0:T(8,128)(2,1)S(1)} %get-tuple-element.26.hidden_ref), custom_call_target="tpu_custom_call" | custom-call | flops 939524096 | bytes 3670016 | tf_op jit(solution)/shard_map/down/pallas_call | solution.py:281
  33.2 1.3 %down.2 = (bf16[2,128,512]{2,1,0:T(8,128)(2,1)S(1)}, bf16[2,128,512]{2,1,0:T(8,128)(2,1)S(1)}, f32[2,128,512]{2,1,0:T(8,128)S(1)}, f32[2,128,512]{2,1,0:T(8,128)S(1)}) custom-call(bf16[1,896,4096]{2,1,0:T(8,128)(2,1)S(1)} %bitcast.12, bf16[256,896]{1,0:T(8,128)(2,1)S(1)} %get-tuple-element.26.hidden_ref), custom_call_target="tpu_custom_call" | custom-call | flops 939524096 | bytes 3670016 | tf_op jit(solution)/shard_map/down/pallas_call | solution.py:281
  35.1 1.6 %collective-permute-start.21 = (bf16[2,128,512]{2,1,0:T(8,128)(2,1)S(1)}, bf16[2,128,512]{2,1,0:T(8,128)(2,1)S(1)}, u32[]{:S(2)}, u32[]{:S(2)}) collective-permute-start(bf16[2,128,512]{2,1,0:T(8,128)(2,1)S(1)} %add_convert_fusion), channel_id=1, source_target_pairs={{0,3},{1,4},{2,1},{3,6},{4,7},{5,0},{6,5},{7,2},{8,11},{9,12},{10,... | collective-permute-start | bytes 786440 | tf_op jit(solution)/shard_map/ppermute | solution.py:355
  36.8 1.3 %collective-permute-start.16 = (bf16[2,128,512]{2,1,0:T(8,128)(2,1)S(1)}, bf16[2,128,512]{2,1,0:T(8,128)(2,1)S(1)}, u32[]{:S(2)}, u32[]{:S(2)}) collective-permute-start(bf16[2,128,512]{2,1,0:T(8,128)(2,1)S(1)} %add_convert_fusion.1), channel_id=1, source_target_pairs={{0,3},{1,4},{2,1},{3,6},{4,7},{5,0},{6,5},{7,2},{8,11},{9,12},{10,... | collective-permute-start | bytes 786440 | tf_op jit(solution)/shard_map/ppermute | solution.py:355
  38.3 2.7 %collective-permute-done.21 = bf16[2,128,512]{2,1,0:T(8,128)(2,1)S(1)} collective-permute-done((bf16[2,128,512]{2,1,0:T(8,128)(2,1)S(1)}, bf16[2,128,512]{2,1,0:T(8,128)(2,1)S(1)}, u32[]{:S(2)}, u32[]{:S(2)}) %collective-permute-start.21) | collective-permute-done | bytes 262176 | tf_op jit(solution)/shard_map/ppermute | solution.py:355
  41.0 1.6 %collective-permute-start.22 = (bf16[1,128,512]{2,1,0:T(8,128)(2,1)S(1)}, bf16[1,128,512]{2,1,0:T(8,128)(2,1)S(1)}, u32[]{:S(2)}, u32[]{:S(2)}) collective-permute-start(bf16[1,128,512]{2,1,0:T(8,128)(2,1)S(1)} %fusion), channel_id=1, source_target_pairs={{0,2},{1,5},{2,0},{3,7},{4,6},{5,1},{6,4},{7,3},{8,10},{9,13},{10,... | collective-permute-start | bytes 393224 | tf_op jit(solution)/shard_map/ppermute | solution.py:355
  42.6 1.2 %collective-permute-done.16 = bf16[2,128,512]{2,1,0:T(8,128)(2,1)S(1)} collective-permute-done((bf16[2,128,512]{2,1,0:T(8,128)(2,1)S(1)}, bf16[2,128,512]{2,1,0:T(8,128)(2,1)S(1)}, u32[]{:S(2)}, u32[]{:S(2)}) %collective-permute-start.16) | collective-permute-done | bytes 262176 | tf_op jit(solution)/shard_map/ppermute | solution.py:355
  43.8 1.6 %collective-permute-start.17 = (bf16[1,128,512]{2,1,0:T(8,128)(2,1)S(1)}, bf16[1,128,512]{2,1,0:T(8,128)(2,1)S(1)}, u32[]{:S(2)}, u32[]{:S(2)}) collective-permute-start(bf16[1,128,512]{2,1,0:T(8,128)(2,1)S(1)} %fusion.3), channel_id=1, source_target_pairs={{0,2},{1,5},{2,0},{3,7},{4,6},{5,1},{6,4},{7,3},{8,10},{9,13},{10,... | collective-permute-start | bytes 393224 | tf_op jit(solution)/shard_map/ppermute | solution.py:355
  45.4 0.7 %collective-permute-done.22 = bf16[1,128,512]{2,1,0:T(8,128)(2,1)S(1)} collective-permute-done((bf16[1,128,512]{2,1,0:T(8,128)(2,1)S(1)}, bf16[1,128,512]{2,1,0:T(8,128)(2,1)S(1)}, u32[]{:S(2)}, u32[]{:S(2)}) %collective-permute-start.22) | collective-permute-done | bytes 131104 | tf_op jit(solution)/shard_map/ppermute | solution.py:355
  46.1 1.6 %collective-permute-start.23 = (bf16[64,512]{1,0:T(8,128)(2,1)S(1)}, bf16[64,512]{1,0:T(8,128)(2,1)S(1)}, u32[]{:S(2)}, u32[]{:S(2)}) collective-permute-start(bf16[64,512]{1,0:T(8,128)(2,1)S(1)} %get-tuple-element.36), channel_id=1, source_target_pairs={{0,16},{8,24},{16,0},{24,8},{1,17},{9,25},{17,1},{25,9},{2,18},{10... | collective-permute-start | bytes 196616 | tf_op jit(solution)/shard_map/ppermute | solution.py:348
  47.8 0.7 %collective-permute-start.24 = (bf16[64,512]{1,0:T(8,128)(2,1)S(1)}, bf16[64,512]{1,0:T(8,128)(2,1)S(1)}, u32[]{:S(2)}, u32[]{:S(2)}) collective-permute-start(bf16[64,512]{1,0:T(8,128)(2,1)S(1)} %get-tuple-element.35), channel_id=1, source_target_pairs={{0,24},{8,16},{16,8},{24,0},{1,25},{9,17},{17,9},{25,1},{2,26},{10... | collective-permute-start | bytes 196616 | tf_op jit(solution)/shard_map/ppermute | solution.py:348
  48.9 0.9 %collective-permute-start.18 = (bf16[64,512]{1,0:T(8,128)(2,1)S(1)}, bf16[64,512]{1,0:T(8,128)(2,1)S(1)}, u32[]{:S(2)}, u32[]{:S(2)}) collective-permute-start(bf16[64,512]{1,0:T(8,128)(2,1)S(1)} %get-tuple-element.37), channel_id=1, source_target_pairs={{0,8},{8,0},{16,24},{24,16},{1,9},{9,1},{17,25},{25,17},{2,10},{10... | collective-permute-start | bytes 196616 | tf_op jit(solution)/shard_map/ppermute | solution.py:348
  50.0 2.8 %collective-permute-done.23.refs_2_ = bf16[64,512]{1,0:T(8,128)(2,1)S(1)} collective-permute-done((bf16[64,512]{1,0:T(8,128)(2,1)S(1)}, bf16[64,512]{1,0:T(8,128)(2,1)S(1)}, u32[]{:S(2)}, u32[]{:S(2)}) %collective-permute-start.23) | collective-permute-done | bytes 65568 | tf_op jit(solution)/shard_map/ppermute | solution.py:348
  52.8 1.2 %collective-permute-done.24.refs_3_ = bf16[64,512]{1,0:T(8,128)(2,1)S(1)} collective-permute-done((bf16[64,512]{1,0:T(8,128)(2,1)S(1)}, bf16[64,512]{1,0:T(8,128)(2,1)S(1)}, u32[]{:S(2)}, u32[]{:S(2)}) %collective-permute-start.24) | collective-permute-done | bytes 65568 | tf_op jit(solution)/shard_map/ppermute | solution.py:348
  54.5 0.9 %combine.1 = bf16[96,512]{1,0:T(8,128)(2,1)} custom-call(bf16[96,256]{1,0:T(8,128)(2,1)S(1)} %get-tuple-element.20.high_ref, bf16[96,256]{1,0:T(8,128)(2,1)S(1)} %get-tuple-element.21.low_ref, bf16[64,512]{1,0:T(8,128)(2,1)S(1)} %get-tuple-element.38.refs_0_, bf16[64,512]{1,0:T(8,128)(2,1)S(1)} %collective-permute-done.18.refs_1_, ...), custom_call_target="tpu_custom_call" | custom-call | tf_op jit(solution)/shard_map/combine/pallas_call | solution.py:305
  (59 shorter events, 4.8 us)
Async XLA Ops:
  0.0 0.7 %copy-start.3 = (s32[96,2]{0,1:T(2,128)S(1)}, s32[96,2]{0,1:T(2,128)}, u32[]{:S(2)}) copy-start(s32[96,2]{0,1:T(2,128)} %param.7) | copy-start | bytes 2308
  0.0 0.9 %copy-start.2 = (bf16[96,512]{1,0:T(8,128)(2,1)S(1)}, bf16[96,512]{1,0:T(8,128)(2,1)}, u32[]{:S(2)}) copy-start(bf16[96,512]{1,0:T(8,128)(2,1)} %x_ref.1) | copy-start | bytes 294916
  0.0 25.9 %copy-start = (bf16[1,896,4096]{2,1,0:T(8,128)(2,1)S(1)}, bf16[1,896,4096]{2,1,0:T(8,128)(2,1)}, u32[]{:S(2)}) copy-start(bf16[1,896,4096]{2,1,0:T(8,128)(2,1)} %gate_ref.9) | copy-start | bytes 22020100
  0.0 25.9 %copy-start.1 = (bf16[1,896,4096]{2,1,0:T(8,128)(2,1)S(1)}, bf16[1,896,4096]{2,1,0:T(8,128)(2,1)}, u32[]{:S(2)}) copy-start(bf16[1,896,4096]{2,1,0:T(8,128)(2,1)} %up_ref.9) | copy-start | bytes 22020100
  1.1 5.7 %collective-permute-start.3 = (bf16[64,512]{1,0:T(8,128)(2,1)S(1)}, bf16[64,512]{1,0:T(8,128)(2,1)S(1)}, u32[]{:S(2)}, u32[]{:S(2)}) collective-permute-start(bf16[64,512]{1,0:T(8,128)(2,1)S(1)} %get-tuple-element.23), channel_id=1, source_target_pairs={{0,8},{8,0},{16,24},{24,16},{1,9},{9,1},{17,25},{25,17},{2,10},{10... | collective-permute-start | bytes 196616 | tf_op jit(solution)/shard_map/ppermute | solution.py:348
  4.2 7.3 %collective-permute-start.4 = (bf16[64,512]{1,0:T(8,128)(2,1)S(1)}, bf16[64,512]{1,0:T(8,128)(2,1)S(1)}, u32[]{:S(2)}, u32[]{:S(2)}) collective-permute-start(bf16[64,512]{1,0:T(8,128)(2,1)S(1)} %get-tuple-element.24), channel_id=1, source_target_pairs={{0,16},{8,24},{16,0},{24,8},{1,17},{9,25},{17,1},{25,9},{2,18},{10... | collective-permute-start | bytes 196616 | tf_op jit(solution)/shard_map/ppermute | solution.py:348
  6.8 6.1 %collective-permute-start.5 = (bf16[64,512]{1,0:T(8,128)(2,1)S(1)}, bf16[64,512]{1,0:T(8,128)(2,1)S(1)}, u32[]{:S(2)}, u32[]{:S(2)}) collective-permute-start(bf16[64,512]{1,0:T(8,128)(2,1)S(1)} %get-tuple-element.25), channel_id=1, source_target_pairs={{0,24},{8,16},{16,8},{24,0},{1,25},{9,17},{17,9},{25,1},{2,26},{10... | collective-permute-start | bytes 196616 | tf_op jit(solution)/shard_map/ppermute | solution.py:348
  12.9 6.3 %collective-permute-start.6 = (bf16[192,512]{1,0:T(8,128)(2,1)S(1)}, bf16[192,512]{1,0:T(8,128)(2,1)S(1)}, u32[]{:S(2)}, u32[]{:S(2)}) collective-permute-start(bf16[192,512]{1,0:T(8,128)(2,1)S(1)} %constant_dynamic-update-slice_fusion.refs_1_), channel_id=1, source_target_pairs={{0,2},{1,5},{2,0},{3,7},{4,6},{5,1},{6,4},{7,3},{8,10},{9,13},{10,... | collective-permute-start | bytes 589832 | tf_op jit(solution)/shard_map/ppermute | solution.py:355
  14.4 6.2 %collective-permute-start = (bf16[1,64,512]{2,1,0:T(8,128)(2,1)S(1)}, bf16[1,64,512]{2,1,0:T(8,128)(2,1)S(1)}, u32[]{:S(2)}, u32[]{:S(2)}) collective-permute-start(bf16[1,64,512]{2,1,0:T(8,128)(2,1)S(1)} %bitcast.13), channel_id=1, source_target_pairs={{0,2},{1,5},{2,0},{3,7},{4,6},{5,1},{6,4},{7,3},{8,10},{9,13},{10,... | collective-permute-start | bytes 196616 | tf_op jit(solution)/shard_map/ppermute | solution.py:355
  14.9 7.9 %collective-permute-start.9 = (bf16[192,512]{1,0:T(8,128)(2,1)S(1)}, bf16[192,512]{1,0:T(8,128)(2,1)S(1)}, u32[]{:S(2)}, u32[]{:S(2)}) collective-permute-start(bf16[192,512]{1,0:T(8,128)(2,1)S(1)} %constant_dynamic-update-slice_fusion.refs_1_), channel_id=1, source_target_pairs={{0,5},{1,2},{2,7},{3,0},{4,1},{5,6},{6,3},{7,4},{8,13},{9,10},{10,... | collective-permute-start | bytes 589832 | tf_op jit(solution)/shard_map/ppermute | solution.py:355
  19.2 5.1 %collective-permute-start.7 = (bf16[192,512]{1,0:T(8,128)(2,1)S(1)}, bf16[192,512]{1,0:T(8,128)(2,1)S(1)}, u32[]{:S(2)}, u32[]{:S(2)}) collective-permute-start(bf16[192,512]{1,0:T(8,128)(2,1)S(1)} %collective-permute-done.6.refs_1_), channel_id=1, source_target_pairs={{0,5},{1,2},{2,7},{3,0},{4,1},{5,6},{6,3},{7,4},{8,13},{9,10},{10,... | collective-permute-start | bytes 589832 | tf_op jit(solution)/shard_map/ppermute | solution.py:355
  20.7 1.7 %collective-permute-start.11 = (bf16[2,64,512]{2,1,0:T(8,128)(2,1)S(1)}, bf16[2,64,512]{2,1,0:T(8,128)(2,1)S(1)}, u32[]{:S(2)}, u32[]{:S(2)}) collective-permute-start(bf16[2,64,512]{2,1,0:T(8,128)(2,1)S(1)} %pad_maximum_fusion.refs_0_), channel_id=1, source_target_pairs={{0,1},{1,0},{2,3},{3,2},{4,5},{5,4},{6,7},{7,6},{8,9},{9,8},{10,11... | collective-permute-start | bytes 393224 | tf_op jit(solution)/shard_map/ppermute | solution.py:351
  20.9 4.8 %collective-permute-start.1 = (bf16[2,64,512]{2,1,0:T(8,128)(2,1)S(1)}, bf16[2,64,512]{2,1,0:T(8,128)(2,1)S(1)}, u32[]{:S(2)}, u32[]{:S(2)}) collective-permute-start(bf16[2,64,512]{2,1,0:T(8,128)(2,1)S(1)} %pad_maximum_fusion.refs_0_), channel_id=1, source_target_pairs={{0,5},{1,2},{2,7},{3,0},{4,1},{5,6},{6,3},{7,4},{8,13},{9,10},{10,... | collective-permute-start | bytes 393224 | tf_op jit(solution)/shard_map/ppermute | solution.py:355
  22.4 3.5 %collective-permute-start.13 = (bf16[192,512]{1,0:T(8,128)(2,1)S(1)}, bf16[192,512]{1,0:T(8,128)(2,1)S(1)}, u32[]{:S(2)}, u32[]{:S(2)}) collective-permute-start(bf16[192,512]{1,0:T(8,128)(2,1)S(1)} %constant_dynamic-update-slice_fusion.refs_1_), channel_id=1, source_target_pairs={{0,1},{1,0},{2,3},{3,2},{4,5},{5,4},{6,7},{7,6},{8,9},{9,8},{10,11... | collective-permute-start | bytes 589832 | tf_op jit(solution)/shard_map/ppermute | solution.py:351
  22.4 4.6 %collective-permute-start.12 = (bf16[192,512]{1,0:T(8,128)(2,1)S(1)}, bf16[192,512]{1,0:T(8,128)(2,1)S(1)}, u32[]{:S(2)}, u32[]{:S(2)}) collective-permute-start(bf16[192,512]{1,0:T(8,128)(2,1)S(1)} %collective-permute-done.6.refs_1_), channel_id=1, source_target_pairs={{0,1},{1,0},{2,3},{3,2},{4,5},{5,4},{6,7},{7,6},{8,9},{9,8},{10,11... | collective-permute-start | bytes 589832 | tf_op jit(solution)/shard_map/ppermute | solution.py:351
  22.9 5.4 %collective-permute-start.10 = (bf16[192,512]{1,0:T(8,128)(2,1)S(1)}, bf16[192,512]{1,0:T(8,128)(2,1)S(1)}, u32[]{:S(2)}, u32[]{:S(2)}) collective-permute-start(bf16[192,512]{1,0:T(8,128)(2,1)S(1)} %collective-permute-done.9.refs_1_), channel_id=1, source_target_pairs={{0,1},{1,0},{2,3},{3,2},{4,5},{5,4},{6,7},{7,6},{8,9},{9,8},{10,11... | collective-permute-start | bytes 589832 | tf_op jit(solution)/shard_map/ppermute | solution.py:351
  24.3 5.8 %collective-permute-start.8 = (bf16[192,512]{1,0:T(8,128)(2,1)S(1)}, bf16[192,512]{1,0:T(8,128)(2,1)S(1)}, u32[]{:S(2)}, u32[]{:S(2)}) collective-permute-start(bf16[192,512]{1,0:T(8,128)(2,1)S(1)} %collective-permute-done.7.refs_1_), channel_id=1, source_target_pairs={{0,1},{1,0},{2,3},{3,2},{4,5},{5,4},{6,7},{7,6},{8,9},{9,8},{10,11... | collective-permute-start | bytes 589832 | tf_op jit(solution)/shard_map/ppermute | solution.py:351
  25.7 2.5 %collective-permute-start.2 = (bf16[2,64,512]{2,1,0:T(8,128)(2,1)S(1)}, bf16[2,64,512]{2,1,0:T(8,128)(2,1)S(1)}, u32[]{:S(2)}, u32[]{:S(2)}) collective-permute-start(bf16[2,64,512]{2,1,0:T(8,128)(2,1)S(1)} %collective-permute-done.1.refs_0_), channel_id=1, source_target_pairs={{0,1},{1,0},{2,3},{3,2},{4,5},{5,4},{6,7},{7,6},{8,9},{9,8},{10,11... | collective-permute-start | bytes 393224 | tf_op jit(solution)/shard_map/ppermute | solution.py:351
  27.0 3.1 %slice-start = ((s8[7340032]{0:T(1024)(128)(4,1)}), s8[4194304]{0:T(1024)(128)(4,1)S(1)}, s32[]{:S(2)}) async-start(s8[7340032]{0:T(1024)(128)(4,1)} %bitcast.11), calls=%async_computation | async-start | bytes 8388608
  28.2 2.2 %slice-start.1 = ((s8[7340032]{0:T(1024)(128)(4,1)}), s8[3145728]{0:T(1024)(128)(4,1)S(1)}, s32[]{:S(2)}) async-start(s8[7340032]{0:T(1024)(128)(4,1)} %bitcast.11), calls=%async_computation.1 | async-start | bytes 6291456
  31.6 3.5 %collective-permute-start.20 = (bf16[2,128,512]{2,1,0:T(8,128)(2,1)S(1)}, bf16[2,128,512]{2,1,0:T(8,128)(2,1)S(1)}, u32[]{:S(2)}, u32[]{:S(2)}) collective-permute-start(bf16[2,128,512]{2,1,0:T(8,128)(2,1)S(1)} %get-tuple-element.34), channel_id=1, source_target_pairs={{0,1},{1,0},{2,3},{3,2},{4,5},{5,4},{6,7},{7,6},{8,9},{9,8},{10,11... | collective-permute-start | bytes 786440 | tf_op jit(solution)/shard_map/ppermute | solution.py:351
  33.1 3.6 %collective-permute-start.15 = (bf16[2,128,512]{2,1,0:T(8,128)(2,1)S(1)}, bf16[2,128,512]{2,1,0:T(8,128)(2,1)S(1)}, u32[]{:S(2)}, u32[]{:S(2)}) collective-permute-start(bf16[2,128,512]{2,1,0:T(8,128)(2,1)S(1)} %get-tuple-element.30), channel_id=1, source_target_pairs={{0,1},{1,0},{2,3},{3,2},{4,5},{5,4},{6,7},{7,6},{8,9},{9,8},{10,11... | collective-permute-start | bytes 786440 | tf_op jit(solution)/shard_map/ppermute | solution.py:351
  34.5 3.6 %collective-permute-start.19 = (bf16[2,128,512]{2,1,0:T(8,128)(2,1)S(1)}, bf16[2,128,512]{2,1,0:T(8,128)(2,1)S(1)}, u32[]{:S(2)}, u32[]{:S(2)}) collective-permute-start(bf16[2,128,512]{2,1,0:T(8,128)(2,1)S(1)} %get-tuple-element.32), channel_id=1, source_target_pairs={{0,1},{1,0},{2,3},{3,2},{4,5},{5,4},{6,7},{7,6},{8,9},{9,8},{10,11... | collective-permute-start | bytes 786440 | tf_op jit(solution)/shard_map/ppermute | solution.py:351
  35.0 3.2 %collective-permute-start.14 = (bf16[2,128,512]{2,1,0:T(8,128)(2,1)S(1)}, bf16[2,128,512]{2,1,0:T(8,128)(2,1)S(1)}, u32[]{:S(2)}, u32[]{:S(2)}) collective-permute-start(bf16[2,128,512]{2,1,0:T(8,128)(2,1)S(1)} %get-tuple-element.28), channel_id=1, source_target_pairs={{0,1},{1,0},{2,3},{3,2},{4,5},{5,4},{6,7},{7,6},{8,9},{9,8},{10,11... | collective-permute-start | bytes 786440 | tf_op jit(solution)/shard_map/ppermute | solution.py:351
  35.1 5.8 %collective-permute-start.21 = (bf16[2,128,512]{2,1,0:T(8,128)(2,1)S(1)}, bf16[2,128,512]{2,1,0:T(8,128)(2,1)S(1)}, u32[]{:S(2)}, u32[]{:S(2)}) collective-permute-start(bf16[2,128,512]{2,1,0:T(8,128)(2,1)S(1)} %add_convert_fusion), channel_id=1, source_target_pairs={{0,3},{1,4},{2,1},{3,6},{4,7},{5,0},{6,5},{7,2},{8,11},{9,12},{10,... | collective-permute-start | bytes 786440 | tf_op jit(solution)/shard_map/ppermute | solution.py:355
  36.8 7.0 %collective-permute-start.16 = (bf16[2,128,512]{2,1,0:T(8,128)(2,1)S(1)}, bf16[2,128,512]{2,1,0:T(8,128)(2,1)S(1)}, u32[]{:S(2)}, u32[]{:S(2)}) collective-permute-start(bf16[2,128,512]{2,1,0:T(8,128)(2,1)S(1)} %add_convert_fusion.1), channel_id=1, source_target_pairs={{0,3},{1,4},{2,1},{3,6},{4,7},{5,0},{6,5},{7,2},{8,11},{9,12},{10,... | collective-permute-start | bytes 786440 | tf_op jit(solution)/shard_map/ppermute | solution.py:355
  38.2 11.7 %copy-start.4 = (f32[96,2]{0,1:T(2,128)S(1)}, f32[96,2]{0,1:T(2,128)}, u32[]{:S(2)}) copy-start(f32[96,2]{0,1:T(2,128)} %param.8) | copy-start | bytes 2308
  41.0 5.0 %collective-permute-start.22 = (bf16[1,128,512]{2,1,0:T(8,128)(2,1)S(1)}, bf16[1,128,512]{2,1,0:T(8,128)(2,1)S(1)}, u32[]{:S(2)}, u32[]{:S(2)}) collective-permute-start(bf16[1,128,512]{2,1,0:T(8,128)(2,1)S(1)} %fusion), channel_id=1, source_target_pairs={{0,2},{1,5},{2,0},{3,7},{4,6},{5,1},{6,4},{7,3},{8,10},{9,13},{10,... | collective-permute-start | bytes 393224 | tf_op jit(solution)/shard_map/ppermute | solution.py:355
  43.8 5.0 %collective-permute-start.17 = (bf16[1,128,512]{2,1,0:T(8,128)(2,1)S(1)}, bf16[1,128,512]{2,1,0:T(8,128)(2,1)S(1)}, u32[]{:S(2)}, u32[]{:S(2)}) collective-permute-start(bf16[1,128,512]{2,1,0:T(8,128)(2,1)S(1)} %fusion.3), channel_id=1, source_target_pairs={{0,2},{1,5},{2,0},{3,7},{4,6},{5,1},{6,4},{7,3},{8,10},{9,13},{10,... | collective-permute-start | bytes 393224 | tf_op jit(solution)/shard_map/ppermute | solution.py:355
  46.1 6.6 %collective-permute-start.23 = (bf16[64,512]{1,0:T(8,128)(2,1)S(1)}, bf16[64,512]{1,0:T(8,128)(2,1)S(1)}, u32[]{:S(2)}, u32[]{:S(2)}) collective-permute-start(bf16[64,512]{1,0:T(8,128)(2,1)S(1)} %get-tuple-element.36), channel_id=1, source_target_pairs={{0,16},{8,24},{16,0},{24,8},{1,17},{9,25},{17,1},{25,9},{2,18},{10... | collective-permute-start | bytes 196616 | tf_op jit(solution)/shard_map/ppermute | solution.py:348
  47.8 6.2 %collective-permute-start.24 = (bf16[64,512]{1,0:T(8,128)(2,1)S(1)}, bf16[64,512]{1,0:T(8,128)(2,1)S(1)}, u32[]{:S(2)}, u32[]{:S(2)}) collective-permute-start(bf16[64,512]{1,0:T(8,128)(2,1)S(1)} %get-tuple-element.35), channel_id=1, source_target_pairs={{0,24},{8,16},{16,8},{24,0},{1,25},{9,17},{17,9},{25,1},{2,26},{10... | collective-permute-start | bytes 196616 | tf_op jit(solution)/shard_map/ppermute | solution.py:348
  48.9 5.6 %collective-permute-start.18 = (bf16[64,512]{1,0:T(8,128)(2,1)S(1)}, bf16[64,512]{1,0:T(8,128)(2,1)S(1)}, u32[]{:S(2)}, u32[]{:S(2)}) collective-permute-start(bf16[64,512]{1,0:T(8,128)(2,1)S(1)} %get-tuple-element.37), channel_id=1, source_target_pairs={{0,8},{8,0},{16,24},{24,16},{1,9},{9,1},{17,25},{25,17},{2,10},{10... | collective-permute-start | bytes 196616 | tf_op jit(solution)/shard_map/ppermute | solution.py:348
